TPU v7x, 256 devices: a whole 4x4x8 slice. The times are simulated.
256 devices in a mesh: dp: 8 (over z), space: 2 (over core), mp: 16 (over y, x).
Axes of the slice: x: 4, y: 4, z: 8, core: 2. Of those that a mesh axis runs over, the one named last changes fastest.
Arguments:
- features: bfloat16 [128, 64, 1024], P(('dp', 'space'), None, 'mp'), parts along dimension 0, may hold values from -6 to 6
- deconv_weight: bfloat16 [4, 512, 1024], P(None, 'mp'), may hold values from -0.1875 to 0.1875
- deconv_bias: float32 [512], P('mp'), may hold values from -3 to 3
- lateral_eight: bfloat16 [256, 512], P('mp'), may hold values from -0.25 to 0.25
- lateral_coarse: bfloat16 [2, 256, 1024], P(None, 'mp'), may hold values from -0.1875 to 0.1875
- output_conv: bfloat16 [3, 256, 9, 256], P(None, 'mp'), may hold values from -0.125 to 0.125
- norm_gain: float32 [6, 256], replicated, may hold values from 0.1 to 1.9
- norm_shift: float32 [6, 256], replicated, may hold values from -3 to 3
Outputs:
- level_eight: bfloat16 [256, 32768], P('mp', ('dp', 'space')), parts along dimension 1
- level_sixteen: bfloat16 [256, 8192], P('mp', ('dp', 'space')), parts along dimension 1
- level_thirty: bfloat16 [256, 2048], P('mp', ('dp', 'space')), parts along dimension 1
- level_sixty: bfloat16 [256, 512], P('mp', ('dp', 'space')), parts along dimension 1
There are 8 independent parts, one for each index of `dp`. A program takes and returns all parts, laid end to end along the dimension named above; an argument that names none is the same for every part. Nothing has to cross between parts.
All inputs are finite; a program needn't handle non-finite values.
Results may differ from a plain program's by a relative error of at most 0.015.
Values may be sent and summed in bfloat16 or wider, within the bound.
No kernel may reach another device: no remote copies, remote signals or barrier semaphores. Data moves between devices by JAX's collectives and lax.ppermute only.
A program may use at most 64 MiB of HBM per device.

v0:
```python
import functools

import jax
import jax.numpy as jnp
from jax import lax
from jax.sharding import Mesh
from jax.sharding import PartitionSpec as P

MP = ("mp_0", "mp_1")


EPSILON = 1e-06


def sent_to_all(x, axis):
    count = lax.axis_size(axis)
    return lax.all_to_all(jnp.broadcast_to(x[None], (count, *x.shape)), axis, 0, 0, tiled=True)


def in_order(blocks, dim):
    blocks = jnp.moveaxis(blocks, 0, dim)
    dims = blocks.shape
    return blocks.reshape(*dims[:dim], dims[dim] * dims[dim + 1], *dims[dim + 2 :])


def gathered_copies(x, axis, dim):
    blocks = sent_to_all(x, axis)
    return in_order(blocks, dim)


def extended(block, sides, width):
    for axis, dim in sides:
        count = lax.axis_size(axis)
        forward = [(i, i + 1) for i in range(count - 1)]
        backward = [(target, source) for source, target in forward]
        low = lax.ppermute(
            lax.slice_in_dim(block, block.shape[dim] - width, None, axis=dim), axis, forward
        )
        high = lax.ppermute(lax.slice_in_dim(block, 0, width, axis=dim), axis, backward)
        block = jnp.concatenate([low, block, high], axis=dim)
    return block


def by_axis(x, axes):
    return functools.reduce(lax.psum, axes, x)


def pool_pairs(values):
    height, width, depth = values.shape
    return jnp.max(values.reshape(height // 2, 2, width // 2, 2, depth), axis=(1, 3))


def contract_last(weight_rows, data):
    return lax.dot_general(
        weight_rows, data, (((1,), (1,)), ((), ())), preferred_element_type=jnp.float32
    )


def apply_norm(values, sums, squares, neck_width, gain_row, shift_row):
    floats = values.astype(jnp.float32)
    center = (sums / neck_width)[None, :]
    spread = (squares / neck_width)[None, :] - center * center
    scaled = (floats - center) * lax.rsqrt(spread + EPSILON)
    return (scaled * gain_row[:, None] + shift_row[:, None]).astype(jnp.bfloat16)


def cell_moments(values):
    floats = values.astype(jnp.float32)
    return (jnp.sum(floats, axis=0), jnp.sum(floats * floats, axis=0))


def conv_taps(totals, padded, weight, height, width):
    depth = padded.shape[0]
    for tap_index in range(9):
        row_off = tap_index // 3
        col_off = tap_index % 3
        window = padded[:, row_off : row_off + height, col_off : col_off + width].reshape(
            depth, height * width
        )
        rows_used = weight[:, tap_index, :]
        totals = totals + jnp.dot(rows_used, window, preferred_element_type=jnp.float32)
    return totals


def pyramid_level(lateral, height, width, level_index, output_conv, norm_gain, norm_shift):
    local_ch = lateral.shape[0]
    neck_width = local_ch * lax.axis_size(MP)
    own_first = lax.axis_index(MP) * local_ch
    weight = output_conv[level_index]
    initial = jnp.zeros((local_ch, height * width), jnp.float32)
    gathered = gathered_copies(lateral, MP, 0)
    sums, squares = cell_moments(gathered)
    normed = apply_norm(
        gathered, sums, squares, neck_width, norm_gain[2 * level_index], norm_shift[2 * level_index]
    )
    rimmed = extended(normed.reshape(neck_width, height, width), (("space", 1),), 1)
    padded = jnp.pad(rimmed, ((0, 0), (0, 0), (1, 1)))
    conv_out = conv_taps(initial, padded, weight, height, width)
    convolved = conv_out.astype(jnp.bfloat16)
    sums, squares = jax.tree.map(lambda part: by_axis(part, MP), cell_moments(convolved))
    gain_row = lax.dynamic_slice_in_dim(norm_gain[2 * level_index + 1], own_first, local_ch, 0)
    shift_row = lax.dynamic_slice_in_dim(norm_shift[2 * level_index + 1], own_first, local_ch, 0)
    return apply_norm(convolved, sums, squares, neck_width, gain_row, shift_row)


def channel_pyramid(
    features,
    deconv_weight,
    deconv_bias,
    lateral_eight,
    lateral_coarse,
    output_conv,
    norm_gain,
    norm_shift,
):
    row_count, col_count, _ = features.shape
    half_local = deconv_weight.shape[1]
    neck_local = lateral_coarse.shape[1]
    pixels = row_count * col_count
    coarse_pixels = row_count // 2 * (col_count // 2)
    deconv_flat = deconv_weight.reshape(4 * half_local, deconv_weight.shape[2])
    piece = gathered_copies(features, MP, 2)
    depth = piece.shape[2]
    flattened = piece.reshape(pixels, depth)
    raised = contract_last(deconv_flat, flattened)
    middle = contract_last(lateral_coarse[0], flattened)
    pooled_flat = pool_pairs(piece).reshape(coarse_pixels, depth)
    coarse = contract_last(lateral_coarse[1], pooled_flat)
    raised, middle, coarse = (raised, middle, coarse)
    raised = (
        raised.reshape(2, 2, half_local, row_count, col_count)
        + deconv_bias[None, None, :, None, None]
    )
    upsampled = raised.transpose(2, 3, 0, 4, 1).reshape(half_local, 4 * pixels).astype(jnp.bfloat16)
    piece = gathered_copies(upsampled, MP, 0)
    lateral_sum = jnp.dot(lateral_eight, piece, preferred_element_type=jnp.float32)
    lat_eight = lateral_sum.astype(jnp.bfloat16)
    lat_sixteen = middle.astype(jnp.bfloat16)
    lat_thirty = coarse.astype(jnp.bfloat16)
    level_eight = pyramid_level(
        lat_eight, 2 * row_count, 2 * col_count, 0, output_conv, norm_gain, norm_shift
    )
    level_sixteen = pyramid_level(
        lat_sixteen, row_count, col_count, 1, output_conv, norm_gain, norm_shift
    )
    level_thirty = pyramid_level(
        lat_thirty, row_count // 2, col_count // 2, 2, output_conv, norm_gain, norm_shift
    )
    level_sixty = level_thirty.reshape(neck_local, row_count // 2, col_count // 2)[
        :, ::2, ::2
    ].reshape(neck_local, -1)
    return (level_eight, level_sixteen, level_thirty, level_sixty)


def per_device(
    features,
    deconv_weight,
    deconv_bias,
    lateral_eight,
    lateral_coarse,
    output_conv,
    norm_gain,
    norm_shift,
):
    return channel_pyramid(
        features,
        deconv_weight,
        deconv_bias,
        lateral_eight,
        lateral_coarse,
        output_conv,
        norm_gain,
        norm_shift,
    )


def solution(mesh):
    finer = Mesh(
        mesh.devices.reshape(mesh.shape["dp"], mesh.shape["space"], 4, 4),
        ("dp", "space", "mp_0", "mp_1"),
    )
    in_specs = (
        P(("dp", "space"), None, MP),
        P(None, MP, None),
        P(MP),
        P(MP, None),
        P(None, MP, None),
        P(None, MP, None, None),
        P(),
        P(),
    )
    out_specs = (
        P(MP, ("dp", "space")),
        P(MP, ("dp", "space")),
        P(MP, ("dp", "space")),
        P(MP, ("dp", "space")),
    )
    return jax.shard_map(
        per_device, mesh=finer, in_specs=in_specs, out_specs=out_specs, check_vma=False
    )
```

profile of v0, /device:TPU:64, one launch (start us, length us, event | category | flops | bytes accessed | tf_op | source)
XLA Modules:
  0.0 185.4 jit_solution(8290357772764863054)
XLA Ops:
  0.6 1.5 broadcast_in_dim.10
  2.1 2.2 %reshape.437 = bf16[16,2,16384]{2,1,0:T(2,128)(2,1)} reshape(bf16[16,8,64,64]{3,2,1,0:T(8,128)(2,1)S(1)} %broadcast_in_dim.10) | data formatting | bytes 2097152
  4.4 7.0 %all-to-all-start = ((bf16[16,2,16384]{2,1,0:T(2,128)(2,1)}), bf16[16,2,16384]{2,1,0:T(2,128)(2,1)S(1)}, u32[]{:S(2)}, u32[]{:S(2)}) async-start(bf16[16,2,16384]{2,1,0:T(2,128)(2,1)} %reshape.437), calls=%async_computation | async-start | bytes 2097152 | tf_op jit(solution)/shard_map/all_to_all | solution.py:17
  20.2 8.9 %all-to-all-done = bf16[16,2,16384]{2,1,0:T(2,128)(2,1)S(1)} async-done(((bf16[16,2,16384]{2,1,0:T(2,128)(2,1)}), bf16[16,2,16384]{2,1,0:T(2,128)(2,1)S(1)}, u32[]{:S(2)}, u32[]{:S(2)}) %all-to-all-start) | async-done | bytes 1048608 | tf_op jit(solution)/shard_map/all_to_all | solution.py:17
  29.1 2.3 %reshape.438 = bf16[16,8,64,64]{3,2,1,0:T(8,128)(2,1)} reshape(bf16[16,2,16384]{2,1,0:T(2,128)(2,1)S(1)} %all-to-all-done) | data formatting | bytes 2097152
  31.4 3.0 %copy.106 = bf16[8,64,16,64]{3,2,1,0:T(8,128)(2,1)S(1)} copy(bf16[8,64,16,64]{3,1,0,2:T(8,128)(2,1)} %bitcast.237) | data formatting | bytes 2097152 | tf_op jit(solution)/shard_map/transpose | solution.py:21
  34.4 2.1 %reshape_reshape.7 = bf16[4,2,32,2,1024]{4,3,2,1,0:T(2,128)(2,1)} reshape(bf16[8,64,16,64]{3,2,1,0:T(8,128)(2,1)S(1)} %copy.106) | data formatting | bytes 2097152 | tf_op jit(solution)/shard_map/reshape;reshape | solution.py:50
  36.4 1.5 reshape_reshape.6
  37.9 2.3 %reshape.403 = bf16[8,64,1024,1,1]{2,1,0,3,4:T(8,128)(2,1)} reshape(bf16[8,64,16,64]{3,2,1,0:T(8,128)(2,1)S(1)} %copy.106) | data formatting | bytes 2097152 | tf_op jit(solution)/shard_map/dot_general | solution.py:54
  40.2 2.9 %reduce_max.9 = bf16[4,32,1024]{2,1,0:T(8,128)(2,1)S(1)} reduce(bf16[4,2,32,2,1024]{4,3,2,1,0:T(2,128)(2,1)} %reshape_reshape.7, bf16[]{:T(256)} %constant.46.clone.1), dimensions={1,3}, to_apply=%region_16.17 | reduce | flops 393216 | bytes 1310722 | tf_op jit(solution)/shard_map/reduce_max | solution.py:50
  43.1 0.9 fusion.22
  44.7 3.5 %all-to-all-start.4 = ((bf16[16,16,128]{2,1,0:T(8,128)(2,1)}), bf16[16,16,128]{2,1,0:T(8,128)(2,1)S(1)}, u32[]{:S(2)}, u32[]{:S(2)}) async-start(bf16[16,16,128]{2,1,0:T(8,128)(2,1)} %broadcast_in_dim.14), calls=%async_computation.4 | async-start | bytes 131072 | tf_op jit(solution)/shard_map/all_to_all | solution.py:17
  48.2 1.9 %fusion.13 = bf16[32,8,2,64,2]{3,0,1,4,2:T(8,128)(2,1)S(1)} fusion(bf16[2,2,32,1024,1]{3,2,4,1,0:T(8,128)(2,1)S(1)} %bitcast.234, bf16[8,64,1024,1,1]{2,1,0,3,4:T(8,128)(2,1)} %reshape.403, f32[32]{0:T(128)} %param.10), kind=kOutput, calls=%fused_computation.23 | convolution fusion | flops 134348800 | bytes 1441920 | tf_op jit(solution)/shard_map/dot_general | solution.py:54
  51.1 4.7 %all-to-all-done.4 = bf16[16,16,128]{2,1,0:T(8,128)(2,1)S(1)} async-done(((bf16[16,16,128]{2,1,0:T(8,128)(2,1)}), bf16[16,16,128]{2,1,0:T(8,128)(2,1)S(1)}, u32[]{:S(2)}, u32[]{:S(2)}) %all-to-all-start.4) | async-done | bytes 65568 | tf_op jit(solution)/shard_map/all_to_all | solution.py:17
  55.8 0.7 broadcast_in_dim.13
  56.5 3.5 %all-to-all-start.3 = ((bf16[16,16,512]{2,1,0:T(8,128)(2,1)}), bf16[16,16,512]{2,1,0:T(8,128)(2,1)S(1)}, u32[]{:S(2)}, u32[]{:S(2)}) async-start(bf16[16,16,512]{2,1,0:T(8,128)(2,1)} %broadcast_in_dim.13), calls=%async_computation.3 | async-start | bytes 524288 | tf_op jit(solution)/shard_map/all_to_all | solution.py:17
  60.9 1.3 collective-permute-start.4
  62.2 1.3 collective-permute-start.5
  63.7 1.6 collective-permute-done.5
  66.5 1.3 fusion.70
  67.9 0.8 all-to-all-done.3
  68.7 1.6 broadcast_in_dim.11
  70.3 6.5 %all-to-all-start.1 = ((bf16[16,32,2048]{2,1,0:T(8,128)(2,1)}), bf16[16,32,2048]{2,1,0:T(8,128)(2,1)S(1)}, u32[]{:S(2)}, u32[]{:S(2)}) async-start(bf16[16,32,2048]{2,1,0:T(8,128)(2,1)} %broadcast_in_dim.11), calls=%async_computation.1 | async-start | bytes 4194304 | tf_op jit(solution)/shard_map/all_to_all | solution.py:17
  77.1 1.2 reshape.400
  78.9 0.8 copy-done.4
  79.7 0.8 fusion.72
  80.5 1.8 collective-permute-start.2
  82.3 1.5 collective-permute-start.3
  84.0 1.3 copy.112
  85.8 0.7 pad_maximum_fusion.3
  87.2 0.8 convolution_add_fusion.8
  88.0 21.9 %all-to-all-done.1 = bf16[16,32,2048]{2,1,0:T(8,128)(2,1)S(1)} async-done(((bf16[16,32,2048]{2,1,0:T(8,128)(2,1)}), bf16[16,32,2048]{2,1,0:T(8,128)(2,1)S(1)}, u32[]{:S(2)}, u32[]{:S(2)}) %all-to-all-start.1) | async-done | bytes 2097184 | tf_op jit(solution)/shard_map/all_to_all | solution.py:17
  109.9 1.1 fusion.7
  111.0 1.1 broadcast_in_dim.12
  112.1 3.7 %all-to-all-start.2 = ((bf16[16,16,2048]{2,1,0:T(8,128)(2,1)}), bf16[16,16,2048]{2,1,0:T(8,128)(2,1)S(1)}, u32[]{:S(2)}, u32[]{:S(2)}) async-start(bf16[16,16,2048]{2,1,0:T(8,128)(2,1)} %broadcast_in_dim.12), calls=%async_computation.2 | async-start | bytes 2097152 | tf_op jit(solution)/shard_map/all_to_all | solution.py:17
  116.4 1.4 fusion.69
  117.8 14.9 %all-to-all-done.2 = bf16[16,16,2048]{2,1,0:T(8,128)(2,1)S(1)} async-done(((bf16[16,16,2048]{2,1,0:T(8,128)(2,1)}), bf16[16,16,2048]{2,1,0:T(8,128)(2,1)S(1)}, u32[]{:S(2)}, u32[]{:S(2)}) %all-to-all-start.2) | async-done | bytes 1048608 | tf_op jit(solution)/shard_map/all_to_all | solution.py:17
  133.5 1.2 fusion.11
  134.9 1.3 collective-permute-start
  136.2 1.3 collective-permute-start.1
  137.5 1.4 add_convert_fusion
  140.3 2.2 %pad_maximum_fusion = bf16[256,18,128]{2,1,0:T(8,128)(2,1)} fusion(bf16[256,1,128]{2,1,0:T(2,128)(2,1)S(1)} %collective-permute-done.1, bf16[256,16,128]{2,1,0:T(8,128)(2,1)S(1)} %fusion.11, bf16[256,1,128]{2,1,0:T(2,128)(2,1)S(1)} %collective-permute-done), kind=kLoop, calls=%fused_computation.19 | loop fusion | flops 3538944 | bytes 2359296 | tf_op jit(solution)/shard_map/concatenate | solution.py:40
  142.4 2.0 %copy.109 = bf16[256,18,128]{0,2,1:T(8,128)(2,1)S(1)} copy(bf16[256,18,128]{2,1,0:T(8,128)(2,1)} %pad_maximum_fusion) | data formatting | bytes 2359296 | tf_op jit(solution)/shard_map/concatenate | solution.py:40
  144.4 4.1 %pad_slice_fusion.5 = (bf16[256,16,128]{0,2,1:T(8,128)(2,1)S(1)}, bf16[256,16,128]{0,2,1:T(8,128)(2,1)S(1)}, bf16[256,16,128]{0,2,1:T(8,128)(2,1)S(1)}, bf16[256...) fusion(bf16[256,18,128]{0,2,1:T(8,128)(2,1)S(1)} %copy.109), kind=kLoop, calls=%fused_computation.63 | loop fusion | bytes 7471104 | tf_op jit(solution)/shard_map/slice | solution.py:77
  150.9 1.0 pad_maximum_fusion.1
  152.9 14.7 %all-reduce.4 = (f32[2048]{0:T(1024)S(1)}, f32[2048]{0:T(1024)S(1)}, f32[512]{0:T(512)S(1)}, f32[512]{0:T(512)S(1)}, f32[128]{0:T(128)S(1)}, /*index=5*/f32[128]{0:T(128)S(1)}) all-reduce(f32[2048]{0:T(1024)S(1)} %get-tuple-element.9, f32[2048]{0:T(1024)S(1)} %get-tuple-element.8, ...), channel_id=1, replica_groups=mesh['dp'=8,'space'=2,'mp_0'=4,'mp_1'=4] {'mp_0'}, use_global_device_ids=true, to_apply=%region_6.7 | all-reduce | flops 5376 | bytes 43008 | tf_op jit(solution)/shard_map/psum | solution.py:45
  167.6 15.4 %all-reduce.3 = (f32[2048]{0:T(1024)S(1)}, f32[2048]{0:T(1024)S(1)}, f32[512]{0:T(512)S(1)}, f32[512]{0:T(512)S(1)}, f32[128]{0:T(128)S(1)}, /*index=5*/f32[128]{0:T(128)S(1)}) all-reduce(f32[2048]{0:T(1024)S(1)} %get-tuple-element.28, f32[2048]{0:T(1024)S(1)} %get-tuple-element.29, ...), channel_id=1, replica_groups=mesh['dp'=8,'space'=2,'mp_0'=4,'mp_1'=4] {'mp_1'}, use_global_device_ids=true, to_apply=%region_7.8 | all-reduce | flops 5376 | bytes 43008 | tf_op jit(solution)/shard_map/psum | solution.py:45
  184.7 0.7 fusion.40
  (165 shorter events, 22.5 us)
Async XLA Ops:
  0.6 47.6 %copy-start = (bf16[4,32,1024]{2,1,0:T(8,128)(2,1)S(1)}, bf16[4,32,1024]{2,1,0:T(8,128)(2,1)}, u32[]{:S(2)}) copy-start(bf16[4,32,1024]{2,1,0:T(8,128)(2,1)} %param.9) | copy-start | bytes 786436
  2.1 9.3 %copy-start.25 = (f32[6,256]{1,0:T(8,128)S(1)}, f32[6,256]{1,0:T(8,128)}, u32[]{:S(2)}) copy-start(f32[6,256]{1,0:T(8,128)} %param.15) | copy-start | bytes 18436
  2.1 9.3 %copy-start.26 = (f32[6,256]{1,0:T(8,128)S(1)}, f32[6,256]{1,0:T(8,128)}, u32[]{:S(2)}) copy-start(f32[6,256]{1,0:T(8,128)} %param.14) | copy-start | bytes 18436
  2.1 17.4 %copy-start.11 = (bf16[3,16,9,256]{3,1,2,0:T(8,128)(2,1)S(1)}, bf16[3,16,9,256]{3,1,2,0:T(8,128)(2,1)}, u32[]{:S(2)}) copy-start(bf16[3,16,9,256]{3,1,2,0:T(8,128)(2,1)} %param.13) | copy-start | bytes 663556
  4.4 24.7 %all-to-all-start = ((bf16[16,2,16384]{2,1,0:T(2,128)(2,1)}), bf16[16,2,16384]{2,1,0:T(2,128)(2,1)S(1)}, u32[]{:S(2)}, u32[]{:S(2)}) async-start(bf16[16,2,16384]{2,1,0:T(2,128)(2,1)} %reshape.437), calls=%async_computation | async-start | bytes 2097152 | tf_op jit(solution)/shard_map/all_to_all | solution.py:17
  40.2 9.9 %copy-start.14 = (bf16[2,16,1024]{2,1,0:T(8,128)(2,1)S(1)}, bf16[2,16,1024]{2,1,0:T(8,128)(2,1)}, u32[]{:S(2)}) copy-start(bf16[2,16,1024]{2,1,0:T(8,128)(2,1)} %param.12) | copy-start | bytes 196612
  44.7 11.1 %all-to-all-start.4 = ((bf16[16,16,128]{2,1,0:T(8,128)(2,1)}), bf16[16,16,128]{2,1,0:T(8,128)(2,1)S(1)}, u32[]{:S(2)}, u32[]{:S(2)}) async-start(bf16[16,16,128]{2,1,0:T(8,128)(2,1)} %broadcast_in_dim.14), calls=%async_computation.4 | async-start | bytes 131072 | tf_op jit(solution)/shard_map/all_to_all | solution.py:17
  50.1 10.6 %copy-start.31 = (f32[1,256]{1,0:T(1,128)S(1)}, f32[1,256]{1,0:T(1,128)}, u32[]{:S(2)}) copy-start(f32[1,256]{1,0:T(1,128)} %get-tuple-element.74) | copy-start | bytes 3076
  50.1 10.6 %copy-start.32 = (f32[1,256]{1,0:T(1,128)S(1)}, f32[1,256]{1,0:T(1,128)}, u32[]{:S(2)}) copy-start(f32[1,256]{1,0:T(1,128)} %get-tuple-element.100) | copy-start | bytes 3076
  50.5 13.0 %copy-start.20 = (f32[16,16]{1,0:T(8,128)S(1)}, f32[16,16]{1,0:T(8,128)}, u32[]{:S(2)}) copy-start(f32[16,16]{1,0:T(8,128)} %add.329) | copy-start | bytes 3076
  50.5 13.0 %copy-start.21 = (f32[16,16]{1,0:T(8,128)S(1)}, f32[16,16]{1,0:T(8,128)}, u32[]{:S(2)}) copy-start(f32[16,16]{1,0:T(8,128)} %mul.284) | copy-start | bytes 3076
  56.5 12.2 %all-to-all-start.3 = ((bf16[16,16,512]{2,1,0:T(8,128)(2,1)}), bf16[16,16,512]{2,1,0:T(8,128)(2,1)S(1)}, u32[]{:S(2)}, u32[]{:S(2)}) async-start(bf16[16,16,512]{2,1,0:T(8,128)(2,1)} %broadcast_in_dim.13), calls=%async_computation.3 | async-start | bytes 524288 | tf_op jit(solution)/shard_map/all_to_all | solution.py:17
  60.9 2.8 %collective-permute-start.4 = (bf16[256,1,32]{0,2,1:T(8,128)(2,1)S(1)}, bf16[256,1,32]{0,2,1:T(8,128)(2,1)S(1)}, u32[]{:S(2)}, u32[]{:S(2)}) collective-permute-start(bf16[256,1,32]{0,2,1:T(8,128)(2,1)S(1)} %get-tuple-element.65), channel_id=1, source_target_pairs={{0,16},{1,17},{2,18},{3,19},{4,20},{5,21},{6,22},{7,23},{8,24},{9,... | collective-permute-start | bytes 49160 | tf_op jit(solution)/shard_map/ppermute | solution.py:36
  62.2 3.1 %collective-permute-start.5 = (bf16[256,1,32]{0,2,1:T(8,128)(2,1)S(1)}, bf16[256,1,32]{0,2,1:T(8,128)(2,1)S(1)}, u32[]{:S(2)}, u32[]{:S(2)}) collective-permute-start(bf16[256,1,32]{0,2,1:T(8,128)(2,1)S(1)} %get-tuple-element.66), channel_id=1, source_target_pairs={{16,0},{17,1},{18,2},{19,3},{20,4},{21,5},{22,6},{23,7},{24,8},{25... | collective-permute-start | bytes 49160 | tf_op jit(solution)/shard_map/ppermute | solution.py:39
  68.7 8.1 %copy-start.1 = (bf16[16,16,512]{2,1,0:T(8,128)(2,1)}, bf16[16,16,512]{2,1,0:T(8,128)(2,1)S(1)}, u32[]{:S(2)}) copy-start(bf16[16,16,512]{2,1,0:T(8,128)(2,1)S(1)} %all-to-all-done.3) | copy-start | bytes 786436
  70.3 8.0 %copy-start.29 = (f32[1,256]{1,0:T(1,128)S(1)}, f32[1,256]{1,0:T(1,128)}, u32[]{:S(2)}) copy-start(f32[1,256]{1,0:T(1,128)} %get-tuple-element.76) | copy-start | bytes 3076
  70.3 8.0 %copy-start.30 = (f32[1,256]{1,0:T(1,128)S(1)}, f32[1,256]{1,0:T(1,128)}, u32[]{:S(2)}) copy-start(f32[1,256]{1,0:T(1,128)} %get-tuple-element.99) | copy-start | bytes 3076
  70.3 39.6 %all-to-all-start.1 = ((bf16[16,32,2048]{2,1,0:T(8,128)(2,1)}), bf16[16,32,2048]{2,1,0:T(8,128)(2,1)S(1)}, u32[]{:S(2)}, u32[]{:S(2)}) async-start(bf16[16,32,2048]{2,1,0:T(8,128)(2,1)} %broadcast_in_dim.11), calls=%async_computation.1 | async-start | bytes 4194304 | tf_op jit(solution)/shard_map/all_to_all | solution.py:17
  76.8 7.0 %copy-start.17 = (f32[16,16]{1,0:T(8,128)S(1)}, f32[16,16]{1,0:T(8,128)}, u32[]{:S(2)}) copy-start(f32[16,16]{1,0:T(8,128)} %add.308) | copy-start | bytes 3076
  76.8 7.0 %copy-start.18 = (f32[16,16]{1,0:T(8,128)S(1)}, f32[16,16]{1,0:T(8,128)}, u32[]{:S(2)}) copy-start(f32[16,16]{1,0:T(8,128)} %mul.264) | copy-start | bytes 3076
  78.3 5.5 %copy-start.2 = (bf16[16,16,512]{2,1,0:T(8,128)(2,1)S(1)}, bf16[16,16,512]{2,1,0:T(8,128)(2,1)}, u32[]{:S(2)}) copy-start(bf16[16,16,512]{2,1,0:T(8,128)(2,1)} %copy-done.1) | copy-start | bytes 786436
  80.5 4.8 %collective-permute-start.2 = (bf16[256,1,64]{2,1,0:T(2,128)(2,1)}, bf16[256,1,64]{2,1,0:T(2,128)(2,1)S(1)}, u32[]{:S(2)}, u32[]{:S(2)}) collective-permute-start(bf16[256,1,64]{2,1,0:T(2,128)(2,1)} %get-tuple-element.44), channel_id=1, source_target_pairs={{0,16},{1,17},{2,18},{3,19},{4,20},{5,21},{6,22},{7,23},{8,24},{9,... | collective-permute-start | bytes 98312 | tf_op jit(solution)/shard_map/ppermute | solution.py:36
  82.3 3.2 %collective-permute-start.3 = (bf16[256,1,64]{2,1,0:T(2,128)(2,1)S(1)}, bf16[256,1,64]{2,1,0:T(2,128)(2,1)S(1)}, u32[]{:S(2)}, u32[]{:S(2)}) collective-permute-start(bf16[256,1,64]{2,1,0:T(2,128)(2,1)S(1)} %get-tuple-element.45), channel_id=1, source_target_pairs={{16,0},{17,1},{18,2},{19,3},{20,4},{21,5},{22,6},{23,7},{24,8},{25... | collective-permute-start | bytes 98312 | tf_op jit(solution)/shard_map/ppermute | solution.py:39
  111.0 4.9 %copy-start.12 = (f32[512,16]{0,1:T(8,128)S(1)}, f32[512,16]{0,1:T(8,128)}, u32[]{:S(2)}) copy-start(f32[512,16]{0,1:T(8,128)} %convolution_add_fusion.8) | copy-start | bytes 98308
  111.0 5.3 %copy-start.5 = (bf16[256,8,64]{0,2,1:T(8,128)(2,1)S(1)}, bf16[256,8,64]{0,2,1:T(8,128)(2,1)}, u32[]{:S(2)}) copy-start(bf16[256,8,64]{0,2,1:T(8,128)(2,1)} %get-tuple-element.52) | copy-start | bytes 786436
  112.1 20.7 %all-to-all-start.2 = ((bf16[16,16,2048]{2,1,0:T(8,128)(2,1)}), bf16[16,16,2048]{2,1,0:T(8,128)(2,1)S(1)}, u32[]{:S(2)}, u32[]{:S(2)}) async-start(bf16[16,16,2048]{2,1,0:T(8,128)(2,1)} %broadcast_in_dim.12), calls=%async_computation.2 | async-start | bytes 2097152 | tf_op jit(solution)/shard_map/all_to_all | solution.py:17
  117.8 15.6 %copy-start.27 = (f32[1,256]{1,0:T(1,128)S(1)}, f32[1,256]{1,0:T(1,128)}, u32[]{:S(2)}) copy-start(f32[1,256]{1,0:T(1,128)} %get-tuple-element.83) | copy-start | bytes 3076
  117.8 15.6 %copy-start.28 = (f32[1,256]{1,0:T(1,128)S(1)}, f32[1,256]{1,0:T(1,128)}, u32[]{:S(2)}) copy-start(f32[1,256]{1,0:T(1,128)} %get-tuple-element.97) | copy-start | bytes 3076
  133.4 4.1 %copy-start.15 = (f32[16,16]{1,0:T(8,128)S(1)}, f32[16,16]{1,0:T(8,128)}, u32[]{:S(2)}) copy-start(f32[16,16]{1,0:T(8,128)} %add.285) | copy-start | bytes 3076
  133.4 4.1 %copy-start.16 = (f32[16,16]{1,0:T(8,128)S(1)}, f32[16,16]{1,0:T(8,128)}, u32[]{:S(2)}) copy-start(f32[16,16]{1,0:T(8,128)} %mul.242) | copy-start | bytes 3076
  134.9 4.0 %collective-permute-start = (bf16[256,1,128]{2,1,0:T(2,128)(2,1)S(1)}, bf16[256,1,128]{2,1,0:T(2,128)(2,1)S(1)}, u32[]{:S(2)}, u32[]{:S(2)}) collective-permute-start(bf16[256,1,128]{2,1,0:T(2,128)(2,1)S(1)} %get-tuple-element.42), channel_id=1, source_target_pairs={{0,16},{1,17},{2,18},{3,19},{4,20},{5,21},{6,22},{7,23},{8,24},{9,... | collective-permute-start | bytes 196616 | tf_op jit(solution)/shard_map/ppermute | solution.py:36
  136.2 3.2 %collective-permute-start.1 = (bf16[256,1,128]{2,1,0:T(2,128)(2,1)S(1)}, bf16[256,1,128]{2,1,0:T(2,128)(2,1)S(1)}, u32[]{:S(2)}, u32[]{:S(2)}) collective-permute-start(bf16[256,1,128]{2,1,0:T(2,128)(2,1)S(1)} %get-tuple-element.43), channel_id=1, source_target_pairs={{16,0},{17,1},{18,2},{19,3},{20,4},{21,5},{22,6},{23,7},{24,8},{25... | collective-permute-start | bytes 196616 | tf_op jit(solution)/shard_map/ppermute | solution.py:39
  144.4 4.1 %copy-start.10 = (bf16[16,9,256]{2,0,1:T(8,128)(2,1)S(1)}, bf16[16,9,256]{2,0,1:T(8,128)(2,1)}, u32[]{:S(2)}) copy-start(bf16[16,9,256]{2,0,1:T(8,128)(2,1)} %get-tuple-element.55) | copy-start | bytes 221188
  149.3 1.6 copy-start.7
  149.3 1.6 copy-start.9
  150.8 1.5 copy-start.3
  151.9 0.9 copy-start.23
  151.9 0.9 copy-start.24
  151.9 0.9 copy-start.33
  151.9 31.0 %copy-start.19 = (f32[128,16]{0,1:T(8,128)S(1)}, f32[128,16]{0,1:T(8,128)}, u32[]{:S(2)}) copy-start(f32[128,16]{0,1:T(8,128)} %get-tuple-element.96) | copy-start | bytes 24580
  152.0 31.0 %copy-start.39 = (f32[16]{0:T(128)S(1)}, f32[16]{0:T(128)}, u32[]{:S(2)}) copy-start(f32[16]{0:T(128)} %fusion.65) | copy-start | bytes 196
  152.0 31.0 %copy-start.40 = (f32[16]{0:T(128)S(1)}, f32[16]{0:T(128)}, u32[]{:S(2)}) copy-start(f32[16]{0:T(128)} %fusion.66) | copy-start | bytes 196
  152.0 32.0 %copy-start.13 = (f32[512,16]{0,1:T(8,128)S(1)}, f32[512,16]{0,1:T(8,128)}, u32[]{:S(2)}) copy-start(f32[512,16]{0,1:T(8,128)} %get-tuple-element.95) | copy-start | bytes 98308
  152.0 32.0 %copy-start.37 = (f32[16]{0:T(128)S(1)}, f32[16]{0:T(128)}, u32[]{:S(2)}) copy-start(f32[16]{0:T(128)} %fusion.63) | copy-start | bytes 196
  152.0 32.0 %copy-start.38 = (f32[16]{0:T(128)S(1)}, f32[16]{0:T(128)}, u32[]{:S(2)}) copy-start(f32[16]{0:T(128)} %fusion.64) | copy-start | bytes 196
  152.0 32.7 %copy-start.35 = (f32[16]{0:T(128)S(1)}, f32[16]{0:T(128)}, u32[]{:S(2)}) copy-start(f32[16]{0:T(128)} %fusion.61) | copy-start | bytes 196
  152.0 32.7 %copy-start.36 = (f32[16]{0:T(128)S(1)}, f32[16]{0:T(128)}, u32[]{:S(2)}) copy-start(f32[16]{0:T(128)} %fusion.62) | copy-start | bytes 196
  183.0 2.4 %copy-start.22 = (bf16[16,128]{1,0:T(8,128)(2,1)}, bf16[16,128]{1,0:T(8,128)(2,1)S(1)}, u32[]{:S(2)}) copy-start(bf16[16,128]{1,0:T(8,128)(2,1)S(1)} %fusion.60) | copy-start | bytes 12292
  (4 other events, 3.0 us)
where the time goes:
time: 186 us; the launch traced here: 185 us
  waiting for transfers between devices  53.5 us (29%)
  local copies, waits for them, and re-layouts  41.9 us (23%)
  starting transfers between devices  32.6 us (18%)
  blocking collectives  30.1 us (16%)
  matrix products  13.3 us (7%)
  other arithmetic  12.7 us (7%)
    all_to_all x5, waiting for transfers between devices, sent_to_all(): lax.all_to_all(jnp.broadcast_to(x[None], (count, *x.shape)), axis, 0, 0,...  51.2 us
    psum x2, blocking collectives, by_axis(): return functools.reduce(lax.psum, axes, x)  30.1 us
    all_to_all x5, starting transfers between devices, sent_to_all(): lax.all_to_all(jnp.broadcast_to(x[None], (count, *x.shape)), axis, 0, 0,...  24.2 us
    dot_general x27, matrix products, conv_taps(): jnp.dot(rows_used, window, preferred_element_type=jnp.float32)  9.03 us
    unnamed x85, local copies, waits for them, and re-layouts  6.61 us
    broadcast_in_dim x5, local copies, waits for them, and re-layouts, sent_to_all(): jnp.broadcast_to(x[None], (count, *x.shape))  5.54 us
    convert_element_type x9, other arithmetic, apply_norm(): (scaled * gain_row[:, None] + shift_row[:, None]).astype(jnp.bfloat16)  5.1 us
    ppermute x3, starting transfers between devices, extended(): lax.ppermute(lax.slice_in_dim(block, block.shape[dim] - width, None, axis...  4.37 us
  transfers between devices with their start and end apart: 11, of which 8 were waited for; matrix products, arithmetic and copies ran while one was open for 14% of the time, Pallas kernels for 0%

commit v1 on v0

v1 whole, which is shorter than its diff:
```python
import jax
import jax.numpy as jnp
from jax import lax
from jax.experimental import pallas as pl
from jax.experimental.pallas import tpu as pltpu
from jax.sharding import Mesh
from jax.sharding import PartitionSpec as P

MP = ("mp_0", "mp_1")
EPSILON = 1e-06
BF = jnp.bfloat16
F32 = jnp.float32
LANES = 128


def dot(a, b):
    return jnp.dot(a, b, preferred_element_type=F32)


def iota(shape, dim):
    return lax.broadcasted_iota(jnp.int32, shape, dim)


def one_hot(shape, source_of_column):
    rows = iota(shape, 0)
    columns = iota(shape, 1)
    return jnp.where(rows == source_of_column(columns), 1.0, 0.0).astype(BF)


def channel_norm(values, gain, shift):
    count = values.shape[0]
    center = jnp.sum(values, axis=0, keepdims=True) / count
    spread = jnp.sum(values * values, axis=0, keepdims=True) / count - center * center
    return (values - center) * lax.rsqrt(spread + EPSILON) * gain + shift


def spread_features(where, x, conv, lat, xb, wb):
    band = where[0]
    members = xb.shape[0]
    flat = x[...].astype(F32).T.astype(BF)
    for m in range(members):
        xb[m] = flat
    taps, rows, depth = conv.shape
    first = band == 0
    half = depth // 2
    own = conv[...].reshape(taps * rows, depth)
    own = jnp.where(first, own[:, :half], own[:, half:])
    lateral = lat[...]
    width = lateral.shape[1] // 2
    lateral = jnp.where(first, lateral[:, :width], lateral[:, width:])
    for m in range(members):
        wb[m, : taps * rows] = own
        for k in range(width // LANES):
            wb[m, taps * rows + k * rows : taps * rows + (k + 1) * rows] = lateral[
                :, k * LANES : (k + 1) * LANES
            ]


def raise_map(where, gathered, deconv, bias, coarse_w, rows_out, lat_out, edge_out):
    band = where[0]
    members, local, pixels = gathered.shape
    x = gathered[...].reshape(members * local, pixels)
    taps, half_local, depth = deconv.shape
    columns = pixels // (members // 2)
    raised = dot(deconv[...].reshape(taps * half_local, depth), x)
    diagonal = iota((half_local, half_local), 0) == iota((half_local, half_local), 1)
    bias_column = jnp.sum(jnp.where(diagonal, bias[...], 0.0), axis=1, keepdims=True)
    low = iota((half_local, LANES), 1) < columns
    for a in range(2):
        for p in range(pixels // LANES):
            tiles = [
                raised[
                    (2 * a + b) * half_local : (2 * a + b + 1) * half_local,
                    p * LANES : (p + 1) * LANES,
                ]
                + bias_column
                for b in range(2)
            ]
            swapped = [pltpu.roll(tile, columns, 1) for tile in tiles]
            rows_out[4 * p + a] = jnp.where(low, tiles[0], swapped[1]).astype(BF)
            rows_out[4 * p + 2 + a] = jnp.where(low, swapped[0], tiles[1]).astype(BF)
    middle = dot(coarse_w[0], x).astype(BF)
    floats = x.astype(F32)
    wide = jnp.maximum(floats, pltpu.roll(floats, pixels - 1, 1))
    pooled = jnp.maximum(wide, pltpu.roll(wide, pixels - columns, 1)).astype(BF)
    coarse = dot(coarse_w[1], pooled).astype(BF)
    small = columns // 2
    pick = one_hot(
        (pixels, LANES), lambda l: (l // small) * (2 * columns) + (l % small) * 2
    )
    coarse = dot(coarse, pick).astype(BF)
    lat_out[:, :pixels] = middle
    lat_out[:, pixels:] = coarse
    top = band == 0
    last = members - 1
    edge_out[:half_local] = jnp.where(top, rows_out[last], rows_out[0])
    tile = jnp.where(
        top,
        pltpu.roll(middle[:, pixels - LANES :].astype(F32), columns, 1),
        middle[:, :LANES].astype(F32),
    )
    floats = coarse.astype(F32)
    tail = jnp.where(top, pltpu.roll(floats, LANES - small, 1), pltpu.roll(floats, columns, 1))
    low = iota(tile.shape, 1) < columns
    edge_out[half_local:] = jnp.where(low, tile, tail).astype(BF)


def lay_out_rows(where, rows, lat, edge, out):
    band = where[0]
    members, half_local, _ = rows.shape
    neck_local = lat.shape[0]
    other = edge[:half_local]
    top = band == 0
    for m in range(members):
        above = rows[m - 1] if m > 0 else other
        below = rows[m + 1] if m < members - 1 else other
        out[m, :half_local] = above
        out[m, half_local : 2 * half_local] = rows[m]
        out[m, 2 * half_local : 3 * half_local] = below
        base = 3 * half_local
        for k in range(lat.shape[1] // LANES):
            out[m, base : base + neck_local] = lat[:, k * LANES : (k + 1) * LANES]
            base += neck_local
        out[m, base : base + neck_local] = edge[half_local:]


def small_conv(normed, halo, weight, width, band, halo_at):
    taps, out_local, depth = weight.shape
    stacked = weight.reshape(taps * out_local, depth)
    main = dot(stacked, normed)
    rim = dot(stacked, halo)
    cells = normed.shape[1]

    def across(values, r):
        size = values.shape[1]
        column = iota((out_local, size), 1) % width
        pieces = [
            values[(3 * r + q) * out_local : (3 * r + q + 1) * out_local] for q in range(3)
        ]
        left = jnp.where(column == 0, 0.0, pltpu.roll(pieces[0], 1, 1))
        right = jnp.where(column == width - 1, 0.0, pltpu.roll(pieces[2], size - 1, 1))
        return left + pieces[1] + right

    lane = iota((out_local, cells), 1)
    first = band == 0
    above = pltpu.roll(across(main, 0), width, 1)
    rim_above = pltpu.roll(across(rim, 0), (LANES - halo_at) % LANES, 1) if halo_at else across(rim, 0)
    rim_below = across(rim, 2)
    shift = (LANES - width - halo_at) % LANES
    if shift:
        rim_below = pltpu.roll(rim_below, shift, 1)
    if cells > LANES:
        blank = jnp.zeros((out_local, cells - LANES), F32)
        rim_above = jnp.concatenate([rim_above, blank], axis=1)
        rim_below = jnp.concatenate([blank, rim_below], axis=1)
    rim_above = jnp.where(first, 0.0, rim_above)
    rim_below = jnp.where(first, rim_below, 0.0)
    above = jnp.where(lane < width, rim_above, above)
    below = pltpu.roll(across(main, 2), cells - width, 1)
    below = jnp.where(lane >= cells - width, rim_below, below)
    return above + across(main, 1) + below


def levels(where, got, weights, weights_other, conv, gains, out, own_sixteen, own_thirty):
    band = where[0]
    row = where[1]
    members = got.shape[0]
    first_band = band == 0
    neck_local = conv.shape[2]
    neck = members * neck_local
    taps = conv.shape[1]
    half_local = (got.shape[1] - 6 * neck_local) // 3
    columns = LANES // 2

    def gain(index):
        return gains[:, index : index + 1], gains[:, 6 + index : 7 + index]

    mine = weights[...]
    other = weights_other[...]
    low = jnp.where(first_band, mine, other)
    high = jnp.where(first_band, other, mine)

    def weight_rows(source, index):
        return source[:, index * neck_local : (index + 1) * neck_local].reshape(neck, LANES)

    lateral = jnp.concatenate(
        [weight_rows(low, taps), weight_rows(low, taps + 1), weight_rows(high, taps), weight_rows(high, taps + 1)],
        axis=1,
    )
    raised = jnp.concatenate(
        [
            got[:, r * half_local : (r + 1) * half_local].reshape(members * half_local, LANES)
            for r in range(3)
        ],
        axis=1,
    )
    lat = dot(lateral, raised).astype(BF).astype(F32)
    normed = channel_norm(lat, *gain(0))
    lane = iota((neck, LANES), 1)
    odd = lane >= columns
    total = jnp.zeros((neck, LANES), F32)
    for r in range(3):
        center = normed[:, r * LANES : (r + 1) * LANES]
        if r == 0:
            center = jnp.where(first_band & (row == 0), 0.0, center)
        if r == 2:
            center = jnp.where(jnp.logical_not(first_band) & (row == members - 1), 0.0, center)
        swapped = pltpu.roll(center, columns, 1)
        left = jnp.where(odd, swapped, pltpu.roll(swapped, 1, 1))
        left = jnp.where(lane == 0, 0.0, left)
        right = jnp.where(odd, pltpu.roll(swapped, LANES - 1, 1), swapped)
        right = jnp.where(lane == LANES - 1, 0.0, right)
        for q, window in enumerate((left, center, right)):
            tap = jnp.concatenate([weight_rows(low, 3 * r + q), weight_rows(high, 3 * r + q)], axis=1)
            total = total + dot(tap, window.astype(BF))
    convolved = total.astype(BF).astype(F32)
    level = channel_norm(convolved, *gain(1)).astype(BF)
    mix = one_hot((LANES, LANES), lambda l: (l % 2) * columns + l // 2)
    out[:, :neck_local] = dot(level, mix).reshape(members, neck_local, LANES)

    def tile(k):
        base = 3 * half_local + k * neck_local
        return got[:, base : base + neck_local].reshape(neck, LANES).astype(F32)

    middle = jnp.concatenate([tile(k) for k in range(4)], axis=1)
    rim = tile(5)
    gain_two, shift_two = gain(2)
    sixteen = small_conv(
        channel_norm(middle, gain_two, shift_two).astype(BF),
        channel_norm(rim, gain_two, shift_two).astype(BF),
        conv[1], columns, band, 0,
    ).astype(BF)
    gain_four, shift_four = gain(4)
    thirty = small_conv(
        channel_norm(tile(4), gain_four, shift_four).astype(BF),
        channel_norm(rim, gain_four, shift_four).astype(BF),
        conv[2], columns // 2, band, columns,
    ).astype(BF)
    own_sixteen[...] = sixteen
    own_thirty[...] = thirty
    floats = jnp.concatenate([sixteen, thirty], axis=1).astype(F32)
    sums = jnp.sum(floats, axis=0, keepdims=True)
    squares = jnp.sum(floats * floats, axis=0, keepdims=True)
    pieces = floats.shape[1] // LANES
    stats = jnp.concatenate(
        [part[:, k * LANES : (k + 1) * LANES] for part in (sums, squares) for k in range(pieces)]
        + [jnp.zeros((neck_local - 2 * pieces, LANES), F32)],
        axis=0,
    )
    for m in range(members):
        out[m, neck_local:] = stats


def finish(where, got, own_sixteen, own_thirty, gains, eight, sixteen, thirty, sixty):
    row = where[1]
    members = got.shape[0]
    neck_local = own_sixteen.shape[0]
    neck = members * neck_local
    for m in range(members):
        eight[:, m * LANES : (m + 1) * LANES] = got[m, :neck_local].astype(BF)
    stats = jnp.sum(got[:, neck_local:], axis=0) / neck
    start = pl.multiple_of(row * neck_local, neck_local)
    own = gains[pl.ds(start, neck_local), :]
    pieces = own_sixteen.shape[1] // LANES + 1

    def apply(values, k, index):
        center = stats[k : k + 1]
        spread = stats[pieces + k : pieces + k + 1] - center * center
        return (
            (values.astype(F32) - center) * lax.rsqrt(spread + EPSILON) * own[:, index : index + 1]
            + own[:, 6 + index : 7 + index]
        ).astype(BF)

    for k in range(pieces - 1):
        at = slice(k * LANES, (k + 1) * LANES)
        sixteen[:, at] = apply(own_sixteen[:, at], k, 3)
    last = apply(own_thirty[...], pieces - 1, 5)
    thirty[...] = last
    small = LANES // 4
    cells = sixty.shape[1]
    pick = one_hot(
        (LANES, cells), lambda l: (l // (small // 2)) * (2 * small) + (l % (small // 2)) * 2
    )
    sixty[...] = dot(last, pick).astype(BF)


def call(kernel, outs, where, *operands):
    specs = [pl.BlockSpec(memory_space=pltpu.SMEM)] + [
        pl.BlockSpec(memory_space=pltpu.VMEM) for _ in operands
    ]
    return pl.pallas_call(
        kernel,
        in_specs=specs,
        out_specs=jax.tree.map(lambda _: pl.BlockSpec(memory_space=pltpu.VMEM), outs),
        out_shape=outs,
        name=kernel.__name__,
    )(where, *operands)


def per_device(
    features,
    deconv_weight,
    deconv_bias,
    lateral_eight,
    lateral_coarse,
    output_conv,
    norm_gain,
    norm_shift,
):
    row_count, col_count, local = features.shape
    members = lax.axis_size(MP)
    pixels = row_count * col_count
    half_local = deconv_weight.shape[1]
    neck_local = lateral_eight.shape[0]
    neck = members * neck_local
    shape = jax.ShapeDtypeStruct
    where = jnp.stack([lax.axis_index("space"), lax.axis_index(MP)]).astype(jnp.int32)
    gains = jnp.concatenate([norm_gain, norm_shift], axis=0).T
    conv = output_conv.transpose(0, 2, 1, 3)
    weight_rows = 11 * neck_local
    swap = [(0, 1), (1, 0)]

    xb, wb = call(
        spread_features,
        (shape((members, local, pixels), BF), shape((members, weight_rows, LANES), BF)),
        where, features.reshape(pixels, local), conv[0], lateral_eight,
    )
    gathered = lax.all_to_all(xb, MP, 0, 0, tiled=True)
    weights = lax.all_to_all(wb, MP, 0, 0, tiled=True)
    weights_other = lax.ppermute(weights, "space", swap)
    rows, lat, edge = call(
        raise_map,
        (
            shape((members, half_local, LANES), BF),
            shape((neck_local, pixels + LANES), BF),
            shape((half_local + neck_local, LANES), BF),
        ),
        where, gathered, deconv_weight, deconv_bias.reshape(1, half_local), lateral_coarse,
    )
    edge = lax.ppermute(edge, "space", swap)
    blocks = call(
        lay_out_rows,
        shape((members, 3 * half_local + 6 * neck_local, LANES), BF),
        where, rows, lat, edge,
    )
    got = lax.all_to_all(blocks, MP, 0, 0, tiled=True)
    blocks, own_sixteen, own_thirty = call(
        levels,
        (
            shape((members, 2 * neck_local, LANES), F32),
            shape((neck_local, pixels), BF),
            shape((neck_local, pixels // 4), BF),
        ),
        where, got, weights, weights_other, conv, gains,
    )
    got = lax.all_to_all(blocks, MP, 0, 0, tiled=True)
    return call(
        finish,
        (
            shape((neck_local, 4 * pixels), BF),
            shape((neck_local, pixels), BF),
            shape((neck_local, pixels // 4), BF),
            shape((neck_local, pixels // 16), BF),
        ),
        where, got, own_sixteen, own_thirty, gains,
    )


def solution(mesh):
    finer = Mesh(
        mesh.devices.reshape(mesh.shape["dp"], mesh.shape["space"], 4, 4),
        ("dp", "space", "mp_0", "mp_1"),
    )
    in_specs = (
        P(("dp", "space"), None, MP),
        P(None, MP, None),
        P(MP),
        P(MP, None),
        P(None, MP, None),
        P(None, MP, None, None),
        P(),
        P(),
    )
    return jax.shard_map(
        per_device,
        mesh=finer,
        in_specs=in_specs,
        out_specs=(P(MP, ("dp", "space")),) * 4,
        check_vma=False,
    )
```

time: 186 us -> 82.4 us (0.44)
  local copies, waits for them, and re-layouts: 41.9 us -> 3.81 us
  waiting for transfers between devices: 53.5 us -> 18.8 us
  starting transfers between devices: 32.6 us -> 7.31 us
  matrix products: 13.3 us -> 0 us
  Pallas kernels: 0 us -> 13.3 us
  other arithmetic: 12.7 us -> 0.67 us
  blocking collectives: 30.1 us -> 37.2 us
    all_to_all x0 -> x2, blocking collectives: none -> 37.2 us  [the longest x1 24.3 us: per_device(): gathered = lax.all_to_all(xb, MP, 0, 0, tiled=True)]
    all_to_all x5 -> x2, waiting for transfers between devices: 51.2 us -> 16 us  [the longest x1 10.8 us: per_device(): got = lax.all_to_all(blocks, MP, 0, 0, tiled=True)]
    psum x2 -> x0, blocking collectives: 30.1 us -> none  [by_axis(): return functools.reduce(lax.psum, axes, x)]
    all_to_all x5 -> x2, starting transfers between devices: 24.2 us -> 7.22 us  [the longest x1 3.61 us: per_device(): got = lax.all_to_all(blocks, MP, 0, 0, tiled=True)]
    dot_general x31 -> x0, matrix products: 13.3 us -> none  [the longest x27 9.03 us: conv_taps(): jnp.dot(rows_used, window, preferred_element_type=jnp.float32)]
    pallas_call x0 -> x5, Pallas kernels: none -> 13.3 us  [call(): pl.pallas_call(kernel, in_specs=specs, out_specs=jax.tree.map(lambda _: p...]
    ppermute x6 -> x2, starting transfers between devices: 8.43 us -> 0.1 us  [the longest x1 0.09 us: per_device(): weights_other = lax.ppermute(weights, 'space', swap)]
    slice x8 -> x0, local copies, waits for them, and re-layouts: 6.09 us -> none  [the longest x3 4.28 us: conv_taps(): padded[:, row_off:row_off + height, col_off:col_off + width]]
  transfers between devices with their start and end apart: 11 -> 4, of which waited for: 8 -> 4; matrix products, arithmetic and copies ran while one was open for 14% -> 1% of each run, Pallas kernels for 0% -> 6%
where the time goes in v1:
time: 82.4 us; the launch traced here: 81.7 us
  blocking collectives  37.2 us (45%)
  waiting for transfers between devices  18.8 us (23%)
  Pallas kernels  13.3 us (16%)
  starting transfers between devices  7.31 us (9%)
  local copies, waits for them, and re-layouts  3.81 us (5%)
    all_to_all x1, blocking collectives, per_device(): gathered = lax.all_to_all(xb, MP, 0, 0, tiled=True)  24.3 us
    pallas_call x5, Pallas kernels, call(): pl.pallas_call(kernel, in_specs=specs, out_specs=jax.tree.map(lambda _: p...  13.3 us
    all_to_all x1, blocking collectives, per_device(): got = lax.all_to_all(blocks, MP, 0, 0, tiled=True)  12.9 us
    all_to_all x1, waiting for transfers between devices, per_device(): got = lax.all_to_all(blocks, MP, 0, 0, tiled=True)  10.8 us
    all_to_all x1, waiting for transfers between devices, per_device(): weights = lax.all_to_all(wb, MP, 0, 0, tiled=True)  5.27 us
    all_to_all x1, starting transfers between devices, per_device(): got = lax.all_to_all(blocks, MP, 0, 0, tiled=True)  3.61 us
    all_to_all x1, starting transfers between devices, per_device(): weights = lax.all_to_all(wb, MP, 0, 0, tiled=True)  3.6 us
  transfers between devices with their start and end apart: 4, of which 4 were waited for; matrix products, arithmetic and copies ran while one was open for 1% of the time, Pallas kernels for 6%

profile of v1, /device:TPU:64, one launch (start us, length us, event | category | flops | bytes accessed | tf_op | source)
XLA Modules:
  0.0 81.7 jit_solution(15395147456620961246)
XLA Ops:
  0.6 1.5 %slice_bitcast_fusion.conv = bf16[9,16,256]{2,1,0:T(8,128)(2,1)} fusion(bf16[3,9,16,256]{3,2,1,0:T(8,128)(2,1)} %bitcast.10), kind=kLoop, calls=%fused_computation | loop fusion | bytes 147456 | tf_op jit(solution)/shard_map/squeeze | solution.py:326
  2.1 0.7 pad_add_fusion.where
  2.8 2.3 %spread_features.1 = (bf16[16,64,512]{2,1,0:T(8,128)(2,1)}, bf16[16,176,128]{2,1,0:T(8,128)(2,1)}) custom-call(s32[2]{0:T(128)} %pad_add_fusion.where, bf16[512,64]{1,0:T(8,128)(2,1)} %bitcast.12, bf16[9,16,256]{2,1,0:T(8,128)(2,1)} %slice_bitcast_fusion.conv, bf16[16,512]{1,0:T(8,128)(2,1)} %lat.1), custom_call_target="tpu_custom_call" | custom-call | tf_op jit(solution)/shard_map/spread_features/pallas_call | solution.py:291
  5.1 24.3 %all_to_all.20.gathered = bf16[16,64,512]{2,1,0:T(8,128)(2,1)} all-to-all(bf16[16,64,512]{2,1,0:T(8,128)(2,1)} %get-tuple-element.12), channel_id=1, replica_groups=mesh['dp'=8,'space'=2,'mp_0'=4,'mp_1'=4] {'mp_0','mp_1'}, dimensions={0} | all-to-all | bytes 2097152 | tf_op jit(solution)/shard_map/all_to_all | solution.py:328
  29.4 3.6 %all-to-all-start.2 = ((bf16[16,176,128]{2,1,0:T(8,128)(2,1)}), bf16[16,176,128]{2,1,0:T(8,128)(2,1)S(1)}, u32[]{:S(2)}, u32[]{:S(2)}) async-start(bf16[16,176,128]{2,1,0:T(8,128)(2,1)} %get-tuple-element.16), calls=%async_computation.2 | async-start | bytes 1441792 | tf_op jit(solution)/shard_map/all_to_all | solution.py:329
  33.0 3.3 %raise_map.1 = (bf16[16,32,128]{2,1,0:T(8,128)(2,1)}, bf16[16,640]{1,0:T(8,128)(2,1)}, bf16[48,128]{1,0:T(8,128)(2,1)}) custom-call(s32[2]{0:T(128)} %pad_add_fusion.where, bf16[16,64,512]{2,1,0:T(8,128)(2,1)} %all_to_all.20.gathered, bf16[4,32,1024]{2,1,0:T(8,128)(2,1)} %deconv.1, f32[1,32]{1,0:T(1,128)} %bitcast.13, bf16[2,16,1024]{2,1,0:T(8,128)(2,1)} %coarse_w.1), custom_call_target="tpu_custom_call" | custom-call | tf_op jit(solution)/shard_map/raise_map/pallas_call | solution.py:291
  36.3 0.0 collective-permute-start
  36.3 1.4 %collective-permute-done.edge = bf16[48,128]{1,0:T(8,128)(2,1)S(1)} collective-permute-done((bf16[48,128]{1,0:T(8,128)(2,1)}, bf16[48,128]{1,0:T(8,128)(2,1)S(1)}, u32[]{:S(2)}, u32[]{:S(2)}) %collective-permute-start) | collective-permute-done | bytes 12320 | tf_op jit(solution)/shard_map/ppermute | solution.py:340
  37.6 0.0 copy-start.3
  37.6 0.6 copy-done.3
  38.2 1.9 %lay_out_rows.1 = bf16[16,192,128]{2,1,0:T(8,128)(2,1)} custom-call(s32[2]{0:T(128)} %pad_add_fusion.where, bf16[16,32,128]{2,1,0:T(8,128)(2,1)} %get-tuple-element.13.rows, bf16[16,640]{1,0:T(8,128)(2,1)} %get-tuple-element.14.lat, bf16[48,128]{1,0:T(8,128)(2,1)} %copy-done.3), custom_call_target="tpu_custom_call" | custom-call | tf_op jit(solution)/shard_map/lay_out_rows/pallas_call | solution.py:291
  40.2 0.0 copy-start.4
  40.2 0.0 copy-start.5
  40.2 5.3 %all-to-all-done.2.weights = bf16[16,176,128]{2,1,0:T(8,128)(2,1)S(1)} async-done(((bf16[16,176,128]{2,1,0:T(8,128)(2,1)}), bf16[16,176,128]{2,1,0:T(8,128)(2,1)S(1)}, u32[]{:S(2)}, u32[]{:S(2)}) %all-to-all-start.2) | async-done | bytes 720928 | tf_op jit(solution)/shard_map/all_to_all | solution.py:329
  45.5 0.0 copy-start.1
  45.5 3.6 %all-to-all-start.1 = ((bf16[16,192,128]{2,1,0:T(8,128)(2,1)}), bf16[16,192,128]{2,1,0:T(8,128)(2,1)S(1)}, u32[]{:S(2)}, u32[]{:S(2)}) async-start(bf16[16,192,128]{2,1,0:T(8,128)(2,1)} %lay_out_rows.1), calls=%async_computation.1 | async-start | bytes 1572864 | tf_op jit(solution)/shard_map/all_to_all | solution.py:346
  49.1 0.0 copy-done.1
  49.1 0.1 collective-permute-start.1
  49.2 0.0 copy-done.4
  49.2 0.0 copy-done.5
  49.2 0.8 copy.14
  50.0 1.4 %collective-permute-done.1.weights_other = bf16[16,176,128]{2,1,0:T(8,128)(2,1)S(1)} collective-permute-done((bf16[16,176,128]{2,1,0:T(8,128)(2,1)S(1)}, bf16[16,176,128]{2,1,0:T(8,128)(2,1)S(1)}, u32[]{:S(2)}, u32[]{:S(2)}) %collective-permute-start.1) | collective-permute-done | bytes 720928 | tf_op jit(solution)/shard_map/ppermute | solution.py:330
  51.4 0.0 copy-start.2
  51.4 10.8 %all-to-all-done.1.got = bf16[16,192,128]{2,1,0:T(8,128)(2,1)S(1)} async-done(((bf16[16,192,128]{2,1,0:T(8,128)(2,1)}), bf16[16,192,128]{2,1,0:T(8,128)(2,1)S(1)}, u32[]{:S(2)}, u32[]{:S(2)}) %all-to-all-start.1) | async-done | bytes 786464 | tf_op jit(solution)/shard_map/all_to_all | solution.py:346
  62.1 0.0 copy-start
  62.1 0.0 copy-done.2
  62.1 0.9 %copy-done = bf16[16,192,128]{2,1,0:T(8,128)(2,1)} copy-done((bf16[16,192,128]{2,1,0:T(8,128)(2,1)}, bf16[16,192,128]{2,1,0:T(8,128)(2,1)S(1)}, u32[]{:S(2)}) %copy-start) | copy-done | bytes 786456
  63.1 4.0 %levels.1 = (f32[16,32,128]{2,1,0:T(8,128)}, bf16[16,512]{1,0:T(8,128)(2,1)}, bf16[16,128]{1,0:T(8,128)(2,1)}) custom-call(s32[2]{0:T(128)} %pad_add_fusion.where, bf16[16,192,128]{2,1,0:T(8,128)(2,1)} %copy-done, bf16[16,176,128]{2,1,0:T(8,128)(2,1)} %copy-done.1, bf16[16,176,128]{2,1,0:T(8,128)(2,1)} %copy-done.2, bf16[3,9,16,256]{3,2,1,0:T(8,128)(2,1)} %bitcast.11, ...), custom_call_target="tpu_custom_call" | custom-call | tf_op jit(solution)/shard_map/levels/pallas_call | solution.py:291
  67.1 12.9 %all_to_all.21.got = f32[16,32,128]{2,1,0:T(8,128)} all-to-all(f32[16,32,128]{2,1,0:T(8,128)} %get-tuple-element.17), channel_id=1, replica_groups=mesh['dp'=8,'space'=2,'mp_0'=4,'mp_1'=4] {'mp_0','mp_1'}, dimensions={0} | all-to-all | bytes 524288 | tf_op jit(solution)/shard_map/all_to_all | solution.py:356
  79.9 1.8 %finish.1 = (bf16[16,2048]{1,0:T(8,128)(2,1)}, bf16[16,512]{1,0:T(8,128)(2,1)}, bf16[16,128]{1,0:T(8,128)(2,1)}, bf16[16,32]{1,0:T(8,128)(2,1)}) custom-call(s32[2]{0:T(128)} %pad_add_fusion.where, f32[16,32,128]{2,1,0:T(8,128)} %all_to_all.21.got, bf16[16,512]{1,0:T(8,128)(2,1)} %get-tuple-element.18.own_sixteen, ...), custom_call_target="tpu_custom_call" | custom-call | tf_op jit(solution)/shard_map/finish/pallas_call | solution.py:291
  (1 shorter events, 0.0 us)
Async XLA Ops:
  29.4 16.1 %all-to-all-start.2 = ((bf16[16,176,128]{2,1,0:T(8,128)(2,1)}), bf16[16,176,128]{2,1,0:T(8,128)(2,1)S(1)}, u32[]{:S(2)}, u32[]{:S(2)}) async-start(bf16[16,176,128]{2,1,0:T(8,128)(2,1)} %get-tuple-element.16), calls=%async_computation.2 | async-start | bytes 1441792 | tf_op jit(solution)/shard_map/all_to_all | solution.py:329
  36.3 1.4 %collective-permute-start = (bf16[48,128]{1,0:T(8,128)(2,1)}, bf16[48,128]{1,0:T(8,128)(2,1)S(1)}, u32[]{:S(2)}, u32[]{:S(2)}) collective-permute-start(bf16[48,128]{1,0:T(8,128)(2,1)} %get-tuple-element.15), channel_id=1, source_target_pairs={{0,16},{16,0},{1,17},{17,1},{2,18},{18,2},{3,19},{19,3},{4,20},{20... | collective-permute-start | bytes 36872 | tf_op jit(solution)/shard_map/ppermute | solution.py:340
  37.6 0.6 copy-start.3
  40.2 9.0 %copy-start.4 = (f32[6,256]{1,0:T(8,128)S(1)}, f32[6,256]{1,0:T(8,128)}, u32[]{:S(2)}) copy-start(f32[6,256]{1,0:T(8,128)} %param.15) | copy-start | bytes 18436
  40.2 9.0 %copy-start.5 = (f32[6,256]{1,0:T(8,128)S(1)}, f32[6,256]{1,0:T(8,128)}, u32[]{:S(2)}) copy-start(f32[6,256]{1,0:T(8,128)} %param.14) | copy-start | bytes 18436
  45.5 3.6 %copy-start.1 = (bf16[16,176,128]{2,1,0:T(8,128)(2,1)}, bf16[16,176,128]{2,1,0:T(8,128)(2,1)S(1)}, u32[]{:S(2)}) copy-start(bf16[16,176,128]{2,1,0:T(8,128)(2,1)S(1)} %all-to-all-done.2.weights) | copy-start | bytes 2162692
  45.5 16.7 %all-to-all-start.1 = ((bf16[16,192,128]{2,1,0:T(8,128)(2,1)}), bf16[16,192,128]{2,1,0:T(8,128)(2,1)S(1)}, u32[]{:S(2)}, u32[]{:S(2)}) async-start(bf16[16,192,128]{2,1,0:T(8,128)(2,1)} %lay_out_rows.1), calls=%async_computation.1 | async-start | bytes 1572864 | tf_op jit(solution)/shard_map/all_to_all | solution.py:346
  49.1 2.3 %collective-permute-start.1 = (bf16[16,176,128]{2,1,0:T(8,128)(2,1)S(1)}, bf16[16,176,128]{2,1,0:T(8,128)(2,1)S(1)}, u32[]{:S(2)}, u32[]{:S(2)}) collective-permute-start(bf16[16,176,128]{2,1,0:T(8,128)(2,1)S(1)} %all-to-all-done.2.weights), channel_id=1, source_target_pairs={{0,16},{16,0},{1,17},{17,1},{2,18},{18,2},{3,19},{19,3},{4,20},{20... | collective-permute-start | bytes 2162696 | tf_op jit(solution)/shard_map/ppermute | solution.py:330
  51.4 10.8 %copy-start.2 = (bf16[16,176,128]{2,1,0:T(8,128)(2,1)}, bf16[16,176,128]{2,1,0:T(8,128)(2,1)S(1)}, u32[]{:S(2)}) copy-start(bf16[16,176,128]{2,1,0:T(8,128)(2,1)S(1)} %collective-permute-done.1.weights_other) | copy-start | bytes 2162692
  62.1 0.9 %copy-start = (bf16[16,192,128]{2,1,0:T(8,128)(2,1)}, bf16[16,192,128]{2,1,0:T(8,128)(2,1)S(1)}, u32[]{:S(2)}) copy-start(bf16[16,192,128]{2,1,0:T(8,128)(2,1)S(1)} %all-to-all-done.1.got) | copy-start | bytes 2359300

commit v2 on v1

v2 whole, which is shorter than its diff:
```python
import jax
import jax.numpy as jnp
from jax import lax
from jax.experimental import pallas as pl
from jax.experimental.pallas import tpu as pltpu
from jax.sharding import Mesh
from jax.sharding import PartitionSpec as P

MP = ("mp_0", "mp_1")
EPSILON = 1e-06
BF = jnp.bfloat16
F32 = jnp.float32
LANES = 128
GRANT = 12 * 1024 * 1024
NECK_ROWS = 16


def dot(a, b):
    return jnp.dot(a, b, preferred_element_type=F32)


def iota(shape, dim):
    return lax.broadcasted_iota(jnp.int32, shape, dim)


def one_hot(shape, source_of_column):
    rows = iota(shape, 0)
    columns = iota(shape, 1)
    return jnp.where(rows == source_of_column(columns), 1.0, 0.0).astype(BF)


def channel_norm(values, gain, shift):
    count = values.shape[0]
    center = jnp.sum(values, axis=0, keepdims=True) / count
    spread = jnp.sum(values * values, axis=0, keepdims=True) / count - center * center
    return (values - center) * lax.rsqrt(spread + EPSILON) * gain + shift


def weight_piece(block, base, index):
    members = block.shape[0]
    rows = NECK_ROWS
    start = base + rows * (index // 4)
    lane = LANES * (index % 4)
    return block[:, start : start + rows, lane : lane + LANES].reshape(members * rows, LANES)


def spread_features(band_at, row_at, x, conv, lat, out):
    members = out.shape[0]
    local = x.shape[1]
    first = band_at[0] == 0
    flat = x[...].astype(F32).T.astype(BF)
    taps = conv.shape[1]
    half = conv.shape[3] // 2
    pieces = [jnp.where(first, conv[0, t, :, :half], conv[0, t, :, half:]) for t in range(taps)]
    half = lat.shape[1] // 2
    lateral = jnp.where(first, lat[:, :half], lat[:, half:])
    pieces += [lateral[:, :LANES], lateral[:, LANES:], jnp.zeros_like(pieces[0])]
    weights = jnp.concatenate(
        [jnp.concatenate(pieces[k : k + 4], axis=1) for k in range(0, len(pieces), 4)], axis=0
    )
    for m in range(members):
        out[m, :local] = flat
        out[m, local:] = weights


def raise_map(band_at, row_at, gathered, deconv, bias, coarse_w, out, rows):
    members = gathered.shape[0]
    pixels = gathered.shape[2]
    taps, half_local, depth = deconv.shape
    local = depth // members
    x = gathered[:, :local].reshape(depth, pixels)
    columns = 2 * pixels // members
    small = columns // 2
    raised = dot(deconv[...].reshape(taps * half_local, depth), x)
    diagonal = iota((half_local, half_local), 0) == iota((half_local, half_local), 1)
    bias_column = jnp.sum(jnp.where(diagonal, bias[...], 0.0), axis=1, keepdims=True)
    low = iota((half_local, LANES), 1) < columns
    for a in range(2):
        for p in range(pixels // LANES):
            tiles = [
                raised[
                    (2 * a + b) * half_local : (2 * a + b + 1) * half_local,
                    p * LANES : (p + 1) * LANES,
                ]
                + bias_column
                for b in range(2)
            ]
            swapped = [pltpu.roll(tile, columns, 1) for tile in tiles]
            rows[4 * p + a] = jnp.where(low, tiles[0], swapped[1]).astype(BF)
            rows[4 * p + 2 + a] = jnp.where(low, swapped[0], tiles[1]).astype(BF)
    middle = dot(coarse_w[0], x).astype(BF)
    low = iota((depth, LANES), 1) < columns
    pairs = []
    for p in range(pixels // LANES):
        tile = x[:, p * LANES : (p + 1) * LANES].astype(F32)
        pairs.append(jnp.maximum(tile, pltpu.roll(tile, columns, 1)))
    packed = []
    for p in range(0, len(pairs), 2):
        both = jnp.where(low, pairs[p], pairs[p + 1])
        packed.append(jnp.maximum(both, pltpu.roll(both, LANES - 1, 1)).astype(BF))
    coarse = dot(coarse_w[1], jnp.concatenate(packed, axis=1)).astype(BF)
    coarse = dot(coarse, one_hot((pixels // 2, LANES), lambda l: 2 * l)).astype(BF)
    tail = [middle[:, p * LANES : (p + 1) * LANES] for p in range(pixels // LANES)] + [coarse]
    tail = jnp.concatenate(tail, axis=0)
    first = band_at[0] == 0
    for m in range(members):
        row = jnp.where(first, m, members - 1 - m)
        for k in range(3):
            out[m, k * half_local : (k + 1) * half_local] = rows[
                jnp.clip(row + k - 1, 0, members - 1)
            ]
        out[m, 3 * half_local :] = tail


def columns_of(gain, shift):
    blank = jnp.zeros((2, gain.shape[1]), F32)
    return jnp.concatenate([gain[...], blank, shift[...], blank], axis=0).T


def scaled(table, index):
    return table[:, index : index + 1], table[:, 8 + index : 9 + index]


def lateral_weight(low, high, base):
    return jnp.concatenate(
        [weight_piece(block, base, 9 + k) for block in (low, high) for k in range(2)], axis=1
    )


def windows(center):
    lane = iota(center.shape, 1)
    columns = LANES // 2
    odd = lane >= columns
    swapped = pltpu.roll(center, columns, 1)
    left = jnp.where(odd, swapped, pltpu.roll(swapped, 1, 1))
    left = jnp.where(lane == 0, 0.0, left)
    right = jnp.where(odd, pltpu.roll(swapped, LANES - 1, 1), swapped)
    right = jnp.where(lane == LANES - 1, 0.0, right)
    return [window.astype(BF) for window in (left, center, right)]


def level_eight(band_at, row_at, got, gathered, other, gain, shift, total_out):
    members = got.shape[0]
    first = band_at[0] == 0
    row = jnp.where(first, row_at[0], members - 1 - row_at[0])
    local = gathered.shape[1] - 3 * NECK_ROWS
    half_local = (got.shape[1] - 5 * NECK_ROWS) // 3
    table = columns_of(gain, shift)
    mine = gathered[:, local:]
    theirs = other[:, local:]
    low = jnp.where(first, mine, theirs)
    high = jnp.where(first, theirs, mine)
    raised = jnp.concatenate(
        [
            got[:, r * half_local : (r + 1) * half_local].reshape(members * half_local, LANES)
            for r in range(3)
        ],
        axis=1,
    )
    lat = dot(lateral_weight(low, high, 0), raised).astype(BF).astype(F32)
    normed = channel_norm(lat, *scaled(table, 0))
    total = None
    for r in range(3):
        center = normed[:, r * LANES : (r + 1) * LANES]
        if r == 0:
            center = jnp.where(row == 0, 0.0, center)
        if r == 2:
            center = jnp.where(row == members - 1, 0.0, center)
        for q, window in enumerate(windows(center)):
            tap = jnp.concatenate(
                [weight_piece(block, 0, 3 * r + q) for block in (low, high)], axis=1
            )
            part = dot(tap, window)
            total = part if total is None else total + part
    total_out[...] = total


def small_conv(normed, halo, weight, width, first):
    taps, out_local, depth = weight.shape
    stacked = weight.reshape(taps * out_local, depth)
    main = dot(stacked, normed)
    rim = dot(stacked, halo)
    cells = normed.shape[1]

    def across(values, r):
        size = values.shape[1]
        column = iota((out_local, size), 1) % width
        pieces = [
            values[(3 * r + q) * out_local : (3 * r + q + 1) * out_local] for q in range(3)
        ]
        left = jnp.where(column == 0, 0.0, pltpu.roll(pieces[0], 1, 1))
        right = jnp.where(column == width - 1, 0.0, pltpu.roll(pieces[2], size - 1, 1))
        return left + pieces[1] + right

    lane = iota((out_local, cells), 1)
    rim_above = jnp.where(first, 0.0, across(rim, 0))
    rim_below = jnp.where(first, pltpu.roll(across(rim, 2), LANES - width, 1), 0.0)
    if cells > LANES:
        blank = jnp.zeros((out_local, cells - LANES), F32)
        rim_above = jnp.concatenate([rim_above, blank], axis=1)
        rim_below = jnp.concatenate([blank, rim_below], axis=1)
    above = jnp.where(lane < width, rim_above, pltpu.roll(across(main, 0), width, 1))
    below = jnp.where(
        lane >= cells - width, rim_below, pltpu.roll(across(main, 2), cells - width, 1)
    )
    return above + across(main, 1) + below


def levels(
    band_at, row_at, got, got_other, total, gathered, other, conv, gain, shift,
    out, own_sixteen, own_thirty, own_table, table_at,
):
    members = got.shape[0]
    first = band_at[0] == 0
    neck = members * NECK_ROWS
    local = gathered.shape[1] - 3 * NECK_ROWS
    half_local = (got.shape[1] - 5 * NECK_ROWS) // 3
    columns = LANES // 2
    table = columns_of(gain, shift)
    table_at[...] = table
    start = pl.multiple_of(row_at[0] * NECK_ROWS, NECK_ROWS)
    own_table[...] = table_at[pl.ds(start, NECK_ROWS), :]

    mine = gathered[:, local:]
    theirs = other[:, local:]
    low = jnp.where(first, mine, theirs)
    high = jnp.where(first, theirs, mine)
    raised = got_other[:, half_local : 2 * half_local].reshape(members * half_local, LANES)
    lat = dot(lateral_weight(low, high, 0), raised).astype(BF).astype(F32)
    center = channel_norm(lat, *scaled(table, 0))
    center = jnp.where(row_at[0] == members - 1, center, 0.0)
    convolved = total[...]
    for q, window in enumerate(windows(center)):
        tap = jnp.concatenate(
            [
                jnp.where(first, weight_piece(block, 0, 6 + q), weight_piece(block, 0, q))
                for block in (low, high)
            ],
            axis=1,
        )
        convolved = convolved + dot(tap, window)
    convolved = convolved.astype(BF).astype(F32)
    level = channel_norm(convolved, *scaled(table, 1)).astype(BF)
    mix = one_hot((LANES, LANES), lambda l: (l % 2) * columns + l // 2)
    out[:, :NECK_ROWS] = dot(level, mix).astype(BF).reshape(members, NECK_ROWS, LANES)

    def tile(source, k):
        base = 3 * half_local + k * NECK_ROWS
        return source[:, base : base + NECK_ROWS].reshape(neck, LANES).astype(F32)

    middle = jnp.concatenate([tile(got, k) for k in range(4)], axis=1)
    rim = jnp.where(first, tile(got_other, 0), pltpu.roll(tile(got_other, 3), columns, 1))
    sixteen = small_conv(
        channel_norm(middle, *scaled(table, 2)).astype(BF),
        channel_norm(rim, *scaled(table, 2)).astype(BF),
        conv[1], columns, first,
    ).astype(BF)
    rim = tile(got_other, 4)
    rim = jnp.where(first, rim, pltpu.roll(rim, columns // 2, 1))
    thirty = small_conv(
        channel_norm(tile(got, 4), *scaled(table, 4)).astype(BF),
        channel_norm(rim, *scaled(table, 4)).astype(BF),
        conv[2], columns // 2, first,
    ).astype(BF)
    own_sixteen[...] = sixteen
    own_thirty[...] = thirty
    floats = jnp.concatenate([sixteen, thirty], axis=1).astype(F32)
    sums = jnp.sum(floats, axis=0, keepdims=True)
    squares = jnp.sum(floats * floats, axis=0, keepdims=True)
    pieces = floats.shape[1] // LANES
    stats = jnp.concatenate(
        [part[:, k * LANES : (k + 1) * LANES] for part in (sums, squares) for k in range(pieces)]
        + [jnp.zeros((NECK_ROWS - 2 * pieces, LANES), F32)],
        axis=0,
    )
    parts = []
    for _ in range(3):
        parts.append(stats.astype(BF))
        stats = stats - parts[-1].astype(F32)
    parts = jnp.concatenate(parts, axis=0)
    for m in range(members):
        out[m, NECK_ROWS:] = parts


def finish(band_at, row_at, got, own_sixteen, own_thirty, table, eight, sixteen, thirty, sixty):
    members = got.shape[0]
    first = band_at[0] == 0
    neck = members * NECK_ROWS
    for r in range(members):
        source = jnp.where(first, r, members - 1 - r)
        eight[:, r * LANES : (r + 1) * LANES] = got[source, :NECK_ROWS]
    stats = jnp.sum(got[:, NECK_ROWS:].astype(F32), axis=0)
    stats = stats[:NECK_ROWS] + stats[NECK_ROWS : 2 * NECK_ROWS] + stats[2 * NECK_ROWS :]
    stats = stats / neck
    pieces = own_sixteen.shape[1] // LANES + 1

    def apply(values, k, index):
        gain, shift = scaled(table, index)
        center = stats[k : k + 1]
        spread = stats[pieces + k : pieces + k + 1] - center * center
        return ((values.astype(F32) - center) * lax.rsqrt(spread + EPSILON) * gain + shift).astype(BF)

    for k in range(pieces - 1):
        at = slice(k * LANES, (k + 1) * LANES)
        sixteen[:, at] = apply(own_sixteen[:, at], k, 3)
    last = apply(own_thirty[...], pieces - 1, 5)
    thirty[...] = last
    small = LANES // 4
    pick = one_hot(
        (LANES, sixty.shape[1]),
        lambda l: (l // (small // 2)) * (2 * small) + (l % (small // 2)) * 2,
    )
    sixty[...] = dot(last, pick).astype(BF)


def call(kernel, outs, where, *operands, scratch=()):
    specs = [pl.BlockSpec(memory_space=pltpu.SMEM) for _ in where] + [
        pl.BlockSpec(memory_space=pltpu.VMEM) for _ in operands
    ]
    return pl.pallas_call(
        kernel,
        in_specs=specs,
        out_specs=jax.tree.map(lambda _: pl.BlockSpec(memory_space=pltpu.VMEM), outs),
        out_shape=outs,
        scratch_shapes=scratch,
        name=kernel.__name__,
        compiler_params=pltpu.CompilerParams(vmem_limit_bytes=GRANT),
    )(*where, *operands)


def per_device(
    features,
    deconv_weight,
    deconv_bias,
    lateral_eight,
    lateral_coarse,
    output_conv,
    norm_gain,
    norm_shift,
):
    row_count, col_count, local = features.shape
    members = lax.axis_size(MP)
    pixels = row_count * col_count
    half_local = deconv_weight.shape[1]
    neck = norm_gain.shape[1]
    assert members == 2 * row_count and 2 * col_count == LANES
    assert lateral_eight.shape[0] == NECK_ROWS and members * NECK_ROWS == neck
    shape = jax.ShapeDtypeStruct
    where = [lax.axis_index(axis).astype(jnp.int32).reshape(1) for axis in ("space", MP)]
    conv = output_conv.transpose(0, 2, 1, 3)
    swap = [(0, 1), (1, 0)]

    blocks = call(
        spread_features,
        shape((members, local + 3 * NECK_ROWS, pixels), BF),
        where, features.reshape(pixels, local), conv, lateral_eight,
    )
    gathered = lax.all_to_all(blocks, MP, 0, 0, tiled=True)
    other = lax.ppermute(gathered, "space", swap)
    blocks = call(
        raise_map,
        shape((members, 3 * half_local + 5 * NECK_ROWS, LANES), BF),
        where, gathered, deconv_weight, deconv_bias.reshape(1, half_local), lateral_coarse,
        scratch=[pltpu.VMEM((members, half_local, LANES), BF)],
    )
    got = lax.all_to_all(blocks, MP, 0, 0, tiled=True)
    got_other = lax.ppermute(got, "space", swap)
    total = call(
        level_eight, shape((neck, LANES), F32),
        where, got, gathered, other, norm_gain, norm_shift,
    )
    blocks, own_sixteen, own_thirty, table = call(
        levels,
        (
            shape((members, 4 * NECK_ROWS, LANES), BF),
            shape((NECK_ROWS, pixels), BF),
            shape((NECK_ROWS, pixels // 4), BF),
            shape((NECK_ROWS, 16), F32),
        ),
        where, got, got_other, total, gathered, other, conv, norm_gain, norm_shift,
        scratch=[pltpu.VMEM((neck, 16), F32)],
    )
    got = lax.all_to_all(blocks, MP, 0, 0, tiled=True)
    return call(
        finish,
        (
            shape((NECK_ROWS, 4 * pixels), BF),
            shape((NECK_ROWS, pixels), BF),
            shape((NECK_ROWS, pixels // 4), BF),
            shape((NECK_ROWS, pixels // 16), BF),
        ),
        where, got, own_sixteen, own_thirty, table,
    )


def solution(mesh):
    finer = Mesh(
        mesh.devices.reshape(mesh.shape["dp"], mesh.shape["space"], 4, 4),
        ("dp", "space", "mp_0", "mp_1"),
    )
    in_specs = (
        P(("dp", "space"), None, MP),
        P(None, MP, None),
        P(MP),
        P(MP, None),
        P(None, MP, None),
        P(None, MP, None, None),
        P(),
        P(),
    )
    return jax.shard_map(
        per_device,
        mesh=finer,
        in_specs=in_specs,
        out_specs=(P(MP, ("dp", "space")),) * 4,
        check_vma=False,
    )
```

time: 82.4 us -> 70.8 us (0.86)
  blocking collectives: 37.2 us -> 61.7 us
  waiting for transfers between devices: 18.8 us -> 1.13 us
  Pallas kernels: 13.3 us -> 4.37 us
  starting transfers between devices: 7.31 us -> 0.01 us
  local copies, waits for them, and re-layouts: 3.81 us -> 2.59 us
    all_to_all x1 -> x2, blocking collectives: 12.9 us -> 29.2 us  [per_device(): got = lax.all_to_all(blocks, MP, 0, 0, tiled=True)]
    all_to_all x2 -> x0, waiting for transfers between devices: 16 us -> none  [the longest x1 10.8 us: per_device(): got = lax.all_to_all(blocks, MP, 0, 0, tiled=True)]
    pallas_call x5, Pallas kernels: 13.3 us -> 4.37 us  [call(): pl.pallas_call(kernel, in_specs=specs, out_specs=jax.tree.map(lambda _: p...]
    all_to_all x1, blocking collectives: 24.3 us -> 32.5 us  [per_device(): gathered = lax.all_to_all(blocks, MP, 0, 0, tiled=True)]
    all_to_all x2 -> x0, starting transfers between devices: 7.22 us -> none  [the longest x1 3.61 us: per_device(): got = lax.all_to_all(blocks, MP, 0, 0, tiled=True)]
    ppermute x2, waiting for transfers between devices: 2.75 us -> 1.13 us  [the longest x1 1.13 us: per_device(): got_other = lax.ppermute(got, 'space', swap)]
    squeeze x1 -> x0, local copies, waits for them, and re-layouts: 1.51 us -> none  [per_device(): conv[0]]
    unnamed x12 -> x18, local copies, waits for them, and re-layouts: 1.52 us -> 2.59 us
  transfers between devices with their start and end apart: 4 -> 2, of which waited for: 4 -> 1; matrix products, arithmetic and copies ran while one was open for 1% -> 0% of each run, Pallas kernels for 6% -> 3%
where the time goes in v2:
time: 70.8 us; the launch traced here: 70.5 us
  blocking collectives  61.7 us (87%)
  Pallas kernels  4.37 us (6%)
  local copies, waits for them, and re-layouts  2.59 us (4%)
  waiting for transfers between devices  1.13 us (2%)
  between operations  0.74 us (1%)
    all_to_all x1, blocking collectives, per_device(): gathered = lax.all_to_all(blocks, MP, 0, 0, tiled=True)  32.5 us
    all_to_all x2, blocking collectives, per_device(): got = lax.all_to_all(blocks, MP, 0, 0, tiled=True)  29.2 us
    pallas_call x5, Pallas kernels, call(): pl.pallas_call(kernel, in_specs=specs, out_specs=jax.tree.map(lambda _: p...  4.37 us
    unnamed x18, local copies, waits for them, and re-layouts  2.59 us
  transfers between devices with their start and end apart: 2, of which 1 were waited for; matrix products, arithmetic and copies ran while one was open for 0% of the time, Pallas kernels for 3%

profile of v2, /device:TPU:64, one launch (start us, length us, event | category | flops | bytes accessed | tf_op | source)
XLA Modules:
  0.0 70.5 jit_solution(11279890713232657003)
XLA Ops:
  0.6 0.0 copy-start
  0.7 0.9 %copy-done = bf16[3,16,9,256]{3,1,2,0:T(8,128)(2,1)S(1)} copy-done((bf16[3,16,9,256]{3,1,2,0:T(8,128)(2,1)S(1)}, bf16[3,16,9,256]{3,1,2,0:T(8,128)(2,1)}, u32[]{:S(2)}) %copy-start) | copy-done | bytes 221208
  1.6 0.0 copy-start.3
  1.6 0.9 %copy-done.3 = bf16[8,64,64]{2,1,0:T(8,128)(2,1)S(1)} copy-done((bf16[8,64,64]{2,1,0:T(8,128)(2,1)S(1)}, bf16[8,64,64]{2,1,0:T(8,128)(2,1)}, u32[]{:S(2)}) %copy-start.3) | copy-done | bytes 65560
  2.5 0.0 copy-start.7
  2.5 0.7 %copy-done.7 = bf16[16,512]{1,0:T(8,128)(2,1)S(1)} copy-done((bf16[16,512]{1,0:T(8,128)(2,1)S(1)}, bf16[16,512]{1,0:T(8,128)(2,1)}, u32[]{:S(2)}) %copy-start.7) | copy-done | bytes 16408
  3.2 0.2 spread_features.1
  3.4 0.0 copy-start.2
  3.4 0.0 copy-start.4
  3.4 0.0 copy-start.8
  3.4 32.5 %all_to_all.15.gathered = bf16[16,112,512]{2,1,0:T(8,128)(2,1)S(1)} all-to-all(bf16[16,112,512]{2,1,0:T(8,128)(2,1)S(1)} %spread_features.1), channel_id=1, replica_groups=mesh['dp'=8,'space'=2,'mp_0'=4,'mp_1'=4] {'mp_0','mp_1'}, dimensions={0} | all-to-all | bytes 3670016 | tf_op jit(solution)/shard_map/all_to_all | solution.py:358
  36.0 0.0 collective-permute-start.1
  36.0 0.0 copy-done.2
  36.0 0.0 copy-done.4
  36.0 0.0 copy-done.8
  36.0 0.0 copy-start.5
  36.0 0.0 copy-start.6
  36.0 1.1 %raise_map.1 = bf16[16,176,128]{2,1,0:T(8,128)(2,1)S(1)} custom-call(s32[1]{0:T(128)} %bitcast.band_at, s32[1]{0:T(128)} %bitcast.1.row_at, bf16[16,112,512]{2,1,0:T(8,128)(2,1)S(1)} %all_to_all.15.gathered, bf16[4,32,1024]{2,1,0:T(8,128)(2,1)S(1)} %copy-done.2, f32[1,32]{1,0:T(1,128)S(1)} %bitcast.8, bf16[2,16,1024]{2,1,0:T(8,128)(2,1)S(1)} %copy-done.4), custom_call_target="tpu_custom_call" | custom-call | tf_op jit(solution)/shard_map/raise_map/pallas_call | solution.py:320
  37.1 17.2 %all_to_all.16.got = bf16[16,176,128]{2,1,0:T(8,128)(2,1)S(1)} all-to-all(bf16[16,176,128]{2,1,0:T(8,128)(2,1)S(1)} %raise_map.1), channel_id=1, replica_groups=mesh['dp'=8,'space'=2,'mp_0'=4,'mp_1'=4] {'mp_0','mp_1'}, dimensions={0} | all-to-all | bytes 1441792 | tf_op jit(solution)/shard_map/all_to_all | solution.py:366
  54.3 0.0 copy-start.1
  54.3 0.0 collective-permute-start
  54.3 0.0 collective-permute-done.1.other
  54.3 0.0 copy-done.5
  54.3 0.0 copy-done.6
  54.3 1.0 %level_eight.1.total = f32[256,128]{1,0:T(8,128)S(1)} custom-call(s32[1]{0:T(128)} %bitcast.band_at, s32[1]{0:T(128)} %bitcast.1.row_at, bf16[16,176,128]{2,1,0:T(8,128)(2,1)S(1)} %all_to_all.16.got, bf16[16,112,512]{2,1,0:T(8,128)(2,1)S(1)} %all_to_all.15.gathered, bf16[16,112,512]{2,1,0:T(8,128)(2,1)S(1)} %collective-permute-done.1.other, ...), custom_call_target="tpu_custom_call" | custom-call | tf_op jit(solution)/shard_map/level_eight/pallas_call | solution.py:320
  55.3 1.1 %collective-permute-done.got_other = bf16[16,176,128]{2,1,0:T(8,128)(2,1)S(1)} collective-permute-done((bf16[16,176,128]{2,1,0:T(8,128)(2,1)S(1)}, bf16[16,176,128]{2,1,0:T(8,128)(2,1)S(1)}, u32[]{:S(2)}, u32[]{:S(2)}) %collective-permute-start) | collective-permute-done | bytes 720928 | tf_op jit(solution)/shard_map/ppermute | solution.py:367
  56.5 0.0 copy-done.1
  56.5 1.3 %levels.1 = (bf16[16,64,128]{2,1,0:T(8,128)(2,1)S(1)}, bf16[16,512]{1,0:T(8,128)(2,1)S(1)}, bf16[16,128]{1,0:T(8,128)(2,1)S(1)}, f32[16,16]{1,0:T(8,128)S(1)}) custom-call(s32[1]{0:T(128)} %bitcast.band_at, s32[1]{0:T(128)} %bitcast.1.row_at, bf16[16,176,128]{2,1,0:T(8,128)(2,1)S(1)} %all_to_all.16.got, ...), custom_call_target="tpu_custom_call" | custom-call | tf_op jit(solution)/shard_map/levels/pallas_call | solution.py:320
  57.8 12.0 %all_to_all.17.got = bf16[16,64,128]{2,1,0:T(8,128)(2,1)S(1)} all-to-all(bf16[16,64,128]{2,1,0:T(8,128)(2,1)S(1)} %get-tuple-element.8), channel_id=1, replica_groups=mesh['dp'=8,'space'=2,'mp_0'=4,'mp_1'=4] {'mp_0','mp_1'}, dimensions={0} | all-to-all | bytes 524288 | tf_op jit(solution)/shard_map/all_to_all | solution.py:383
  69.8 0.8 %finish.1 = (bf16[16,2048]{1,0:T(8,128)(2,1)}, bf16[16,512]{1,0:T(8,128)(2,1)}, bf16[16,128]{1,0:T(8,128)(2,1)}, bf16[16,32]{1,0:T(8,128)(2,1)}) custom-call(s32[1]{0:T(128)} %bitcast.band_at, s32[1]{0:T(128)} %bitcast.1.row_at, bf16[16,64,128]{2,1,0:T(8,128)(2,1)S(1)} %all_to_all.17.got, bf16[16,512]{1,0:T(8,128)(2,1)S(1)} %get-tuple-element.9.own_sixteen, ...), custom_call_target="tpu_custom_call" | custom-call | tf_op jit(solution)/shard_map/finish/pallas_call | solution.py:320
Async XLA Ops:
  0.6 0.9 %copy-start = (bf16[3,16,9,256]{3,1,2,0:T(8,128)(2,1)S(1)}, bf16[3,16,9,256]{3,1,2,0:T(8,128)(2,1)}, u32[]{:S(2)}) copy-start(bf16[3,16,9,256]{3,1,2,0:T(8,128)(2,1)} %param.13) | copy-start | bytes 663556
  1.6 0.9 %copy-start.3 = (bf16[8,64,64]{2,1,0:T(8,128)(2,1)S(1)}, bf16[8,64,64]{2,1,0:T(8,128)(2,1)}, u32[]{:S(2)}) copy-start(bf16[8,64,64]{2,1,0:T(8,128)(2,1)} %param.8) | copy-start | bytes 196612
  2.5 0.7 %copy-start.7 = (bf16[16,512]{1,0:T(8,128)(2,1)S(1)}, bf16[16,512]{1,0:T(8,128)(2,1)}, u32[]{:S(2)}) copy-start(bf16[16,512]{1,0:T(8,128)(2,1)} %lat.1) | copy-start | bytes 49156
  3.4 32.6 %copy-start.2 = (bf16[4,32,1024]{2,1,0:T(8,128)(2,1)S(1)}, bf16[4,32,1024]{2,1,0:T(8,128)(2,1)}, u32[]{:S(2)}) copy-start(bf16[4,32,1024]{2,1,0:T(8,128)(2,1)} %deconv.1) | copy-start | bytes 786436
  3.4 32.6 %copy-start.4 = (bf16[2,16,1024]{2,1,0:T(8,128)(2,1)S(1)}, bf16[2,16,1024]{2,1,0:T(8,128)(2,1)}, u32[]{:S(2)}) copy-start(bf16[2,16,1024]{2,1,0:T(8,128)(2,1)} %coarse_w.1) | copy-start | bytes 196612
  3.4 32.6 %copy-start.8 = (f32[32]{0:T(128)S(1)}, f32[32]{0:T(128)}, u32[]{:S(2)}) copy-start(f32[32]{0:T(128)} %param.10) | copy-start | bytes 388
  36.0 18.3 %collective-permute-start.1 = (bf16[16,112,512]{2,1,0:T(8,128)(2,1)S(1)}, bf16[16,112,512]{2,1,0:T(8,128)(2,1)S(1)}, u32[]{:S(2)}, u32[]{:S(2)}) collective-permute-start(bf16[16,112,512]{2,1,0:T(8,128)(2,1)S(1)} %all_to_all.15.gathered), channel_id=1, source_target_pairs={{0,16},{16,0},{1,17},{17,1},{2,18},{18,2},{3,19},{19,3},{4,20},{20... | collective-permute-start | bytes 5505032 | tf_op jit(solution)/shard_map/ppermute | solution.py:359
  36.0 18.3 %copy-start.5 = (f32[6,256]{1,0:T(8,128)S(1)}, f32[6,256]{1,0:T(8,128)}, u32[]{:S(2)}) copy-start(f32[6,256]{1,0:T(8,128)} %gain.3) | copy-start | bytes 18436
  36.0 18.3 %copy-start.6 = (f32[6,256]{1,0:T(8,128)S(1)}, f32[6,256]{1,0:T(8,128)}, u32[]{:S(2)}) copy-start(f32[6,256]{1,0:T(8,128)} %shift.3) | copy-start | bytes 18436
  54.3 2.2 %copy-start.1 = (bf16[3,16,9,256]{3,1,2,0:T(8,128)(2,1)S(1)}, bf16[3,16,9,256]{3,1,2,0:T(8,128)(2,1)}, u32[]{:S(2)}) copy-start(bf16[3,16,9,256]{3,1,2,0:T(8,128)(2,1)} %param.13) | copy-start | bytes 663556
  54.3 2.2 %collective-permute-start = (bf16[16,176,128]{2,1,0:T(8,128)(2,1)S(1)}, bf16[16,176,128]{2,1,0:T(8,128)(2,1)S(1)}, u32[]{:S(2)}, u32[]{:S(2)}) collective-permute-start(bf16[16,176,128]{2,1,0:T(8,128)(2,1)S(1)} %all_to_all.16.got), channel_id=1, source_target_pairs={{0,16},{16,0},{1,17},{17,1},{2,18},{18,2},{3,19},{19,3},{4,20},{20... | collective-permute-start | bytes 2162696 | tf_op jit(solution)/shard_map/ppermute | solution.py:367

commit v3 on v2

--- a/solution.py
+++ b/solution.py
@@ -6,6 +6,7 @@
 from jax.sharding import Mesh
 from jax.sharding import PartitionSpec as P
 
+
 MP = ("mp_0", "mp_1")
 EPSILON = 1e-06
 BF = jnp.bfloat16
@@ -13,6 +14,8 @@
 LANES = 128
 GRANT = 12 * 1024 * 1024
 NECK_ROWS = 16
+SHARES = 2
+PER_SHARE = 6
 
 
 def dot(a, b):
@@ -36,41 +39,63 @@
     return (values - center) * lax.rsqrt(spread + EPSILON) * gain + shift
 
 
-def weight_piece(block, base, index):
-    members = block.shape[0]
-    rows = NECK_ROWS
-    start = base + rows * (index // 4)
-    lane = LANES * (index % 4)
-    return block[:, start : start + rows, lane : lane + LANES].reshape(members * rows, LANES)
-
-
-def spread_features(band_at, row_at, x, conv, lat, out):
+def weight_piece(halves, index):
+    share, at = index // PER_SHARE, index % PER_SHARE
+    return jnp.concatenate(
+        [
+            half[share, :, at * NECK_ROWS : (at + 1) * NECK_ROWS].reshape(-1, LANES)
+            for half in halves
+        ],
+        axis=1,
+    )
+
+
+def spread_features(
+    band_at, parity_at, x_from, conv_from, lat_from, out, x, conv, lat, arrived
+):
+    copies = [
+        pltpu.make_async_copy(x_from, x, arrived.at[0]),
+        pltpu.make_async_copy(conv_from.at[0], conv, arrived.at[1]),
+        pltpu.make_async_copy(lat_from, lat, arrived.at[2]),
+    ]
+    for copy in copies:
+        copy.start()
+    for copy in copies:
+        copy.wait()
     members = out.shape[0]
-    local = x.shape[1]
     first = band_at[0] == 0
+    even = parity_at[0] == 0
     flat = x[...].astype(F32).T.astype(BF)
-    taps = conv.shape[1]
-    half = conv.shape[3] // 2
-    pieces = [jnp.where(first, conv[0, t, :, :half], conv[0, t, :, half:]) for t in range(taps)]
+    flat = jnp.concatenate(
+        [flat[:, k : k + LANES] for k in range(0, flat.shape[1], LANES)], axis=0
+    )
     half = lat.shape[1] // 2
     lateral = jnp.where(first, lat[:, :half], lat[:, half:])
-    pieces += [lateral[:, :LANES], lateral[:, LANES:], jnp.zeros_like(pieces[0])]
-    weights = jnp.concatenate(
-        [jnp.concatenate(pieces[k : k + 4], axis=1) for k in range(0, len(pieces), 4)], axis=0
-    )
+    pieces = [jnp.where(first, conv[t, :, :LANES], conv[t, :, LANES:]) for t in range(9)]
+    pieces += [lateral[:, :LANES], lateral[:, LANES:], lateral[:, LANES:]]
+    weights = [jnp.where(even, pieces[k], pieces[PER_SHARE + k]) for k in range(PER_SHARE)]
+    weights = jnp.concatenate(weights, axis=0)
+    start = flat.shape[0]
     for m in range(members):
-        out[m, :local] = flat
-        out[m, local:] = weights
-
-
-def raise_map(band_at, row_at, gathered, deconv, bias, coarse_w, out, rows):
+        out[m, :start] = flat
+        out[m, start:] = weights
+
+
+def raise_map(band_at, gathered, deconv, bias, coarse_w, out, share, share_low, share_high, rows):
     members = gathered.shape[0]
-    pixels = gathered.shape[2]
     taps, half_local, depth = deconv.shape
     local = depth // members
-    x = gathered[:, :local].reshape(depth, pixels)
+    weight_rows = share.shape[1]
+    split = gathered.shape[1] - weight_rows
+    pixels = split // local * LANES
+    half = members // 2
+    share[...] = gathered[:, split:]
+    share_low[...] = gathered[:half, split:]
+    share_high[...] = gathered[half:, split:]
+    x = jnp.concatenate(
+        [gathered[:, k : k + local].reshape(depth, LANES) for k in range(0, split, local)], axis=1
+    )
     columns = 2 * pixels // members
-    small = columns // 2
     raised = dot(deconv[...].reshape(taps * half_local, depth), x)
     diagonal = iota((half_local, half_local), 0) == iota((half_local, half_local), 1)
     bias_column = jnp.sum(jnp.where(diagonal, bias[...], 0.0), axis=1, keepdims=True)
@@ -121,10 +146,17 @@
     return table[:, index : index + 1], table[:, 8 + index : 9 + index]
 
 
-def lateral_weight(low, high, base):
-    return jnp.concatenate(
-        [weight_piece(block, base, 9 + k) for block in (low, high) for k in range(2)], axis=1
-    )
+def merge_shares(parity_at, own, low, high, out):
+    parity = parity_at[0]
+    middle = low.shape[0]
+    out[parity] = own[...]
+    out[1 - parity, :middle] = low[...]
+    out[1 - parity, middle:] = high[...]
+
+
+def lateral_weight(halves):
+    pair = [weight_piece([half], 9 + k) for half in halves for k in range(2)]
+    return jnp.concatenate(pair, axis=1)
 
 
 def windows(center):
@@ -139,17 +171,19 @@
     return [window.astype(BF) for window in (left, center, right)]
 
 
-def level_eight(band_at, row_at, got, gathered, other, gain, shift, total_out):
+def ordered_halves(first, mine, theirs):
+    low = jnp.where(first, mine[...], theirs[...])
+    high = jnp.where(first, theirs[...], mine[...])
+    return low, high
+
+
+def level_eight(band_at, row_at, got, mine, theirs, gain, shift, total_out):
     members = got.shape[0]
     first = band_at[0] == 0
     row = jnp.where(first, row_at[0], members - 1 - row_at[0])
-    local = gathered.shape[1] - 3 * NECK_ROWS
     half_local = (got.shape[1] - 5 * NECK_ROWS) // 3
     table = columns_of(gain, shift)
-    mine = gathered[:, local:]
-    theirs = other[:, local:]
-    low = jnp.where(first, mine, theirs)
-    high = jnp.where(first, theirs, mine)
+    halves = ordered_halves(first, mine, theirs)
     raised = jnp.concatenate(
         [
             got[:, r * half_local : (r + 1) * half_local].reshape(members * half_local, LANES)
@@ -157,7 +191,7 @@
         ],
         axis=1,
     )
-    lat = dot(lateral_weight(low, high, 0), raised).astype(BF).astype(F32)
+    lat = dot(lateral_weight(halves), raised).astype(BF).astype(F32)
     normed = channel_norm(lat, *scaled(table, 0))
     total = None
     for r in range(3):
@@ -167,10 +201,7 @@
         if r == 2:
             center = jnp.where(row == members - 1, 0.0, center)
         for q, window in enumerate(windows(center)):
-            tap = jnp.concatenate(
-                [weight_piece(block, 0, 3 * r + q) for block in (low, high)], axis=1
-            )
-            part = dot(tap, window)
+            part = dot(weight_piece(halves, 3 * r + q), window)
             total = part if total is None else total + part
     total_out[...] = total
 
@@ -207,13 +238,12 @@
 
 
 def levels(
-    band_at, row_at, got, got_other, total, gathered, other, conv, gain, shift,
+    band_at, row_at, got, got_other, total, mine, theirs, conv, gain, shift,
     out, own_sixteen, own_thirty, own_table, table_at,
 ):
     members = got.shape[0]
     first = band_at[0] == 0
     neck = members * NECK_ROWS
-    local = gathered.shape[1] - 3 * NECK_ROWS
     half_local = (got.shape[1] - 5 * NECK_ROWS) // 3
     columns = LANES // 2
     table = columns_of(gain, shift)
@@ -221,23 +251,14 @@
     start = pl.multiple_of(row_at[0] * NECK_ROWS, NECK_ROWS)
     own_table[...] = table_at[pl.ds(start, NECK_ROWS), :]
 
-    mine = gathered[:, local:]
-    theirs = other[:, local:]
-    low = jnp.where(first, mine, theirs)
-    high = jnp.where(first, theirs, mine)
+    halves = ordered_halves(first, mine, theirs)
     raised = got_other[:, half_local : 2 * half_local].reshape(members * half_local, LANES)
-    lat = dot(lateral_weight(low, high, 0), raised).astype(BF).astype(F32)
+    lat = dot(lateral_weight(halves), raised).astype(BF).astype(F32)
     center = channel_norm(lat, *scaled(table, 0))
     center = jnp.where(row_at[0] == members - 1, center, 0.0)
     convolved = total[...]
     for q, window in enumerate(windows(center)):
-        tap = jnp.concatenate(
-            [
-                jnp.where(first, weight_piece(block, 0, 6 + q), weight_piece(block, 0, q))
-                for block in (low, high)
-            ],
-            axis=1,
-        )
+        tap = jnp.where(first, weight_piece(halves, 6 + q), weight_piece(halves, q))
         convolved = convolved + dot(tap, window)
     convolved = convolved.astype(BF).astype(F32)
     level = channel_norm(convolved, *scaled(table, 1)).astype(BF)
@@ -282,7 +303,7 @@
         out[m, NECK_ROWS:] = parts
 
 
-def finish(band_at, row_at, got, own_sixteen, own_thirty, table, eight, sixteen, thirty, sixty):
+def finish(band_at, got, own_sixteen, own_thirty, table, eight, sixteen, thirty, sixty):
     members = got.shape[0]
     first = band_at[0] == 0
     neck = members * NECK_ROWS
@@ -313,9 +334,9 @@
     sixty[...] = dot(last, pick).astype(BF)
 
 
-def call(kernel, outs, where, *operands, scratch=()):
+def call(kernel, outs, where, *operands, scratch=(), space=pltpu.VMEM):
     specs = [pl.BlockSpec(memory_space=pltpu.SMEM) for _ in where] + [
-        pl.BlockSpec(memory_space=pltpu.VMEM) for _ in operands
+        pl.BlockSpec(memory_space=space) for _ in operands
     ]
     return pl.pallas_call(
         kernel,
@@ -323,9 +344,8 @@
         out_specs=jax.tree.map(lambda _: pl.BlockSpec(memory_space=pltpu.VMEM), outs),
         out_shape=outs,
         scratch_shapes=scratch,
-        name=kernel.__name__,
         compiler_params=pltpu.CompilerParams(vmem_limit_bytes=GRANT),
-    )(*where, *operands)
+    )(*where, *(pltpu.with_memory_space_constraint(x, space) for x in operands))
 
 
 def per_device(
@@ -346,28 +366,59 @@
     assert members == 2 * row_count and 2 * col_count == LANES
     assert lateral_eight.shape[0] == NECK_ROWS and members * NECK_ROWS == neck
     shape = jax.ShapeDtypeStruct
-    where = [lax.axis_index(axis).astype(jnp.int32).reshape(1) for axis in ("space", MP)]
+    band, row, plane = (
+        lax.axis_index(axis).astype(jnp.int32).reshape(1) for axis in ("space", MP, "dp")
+    )
+    planes = lax.axis_size("dp")
+    assert planes % SHARES == 0
+    parity = plane & 1
     conv = output_conv.transpose(0, 2, 1, 3)
-    swap = [(0, 1), (1, 0)]
+    share_rows = PER_SHARE * NECK_ROWS
+
+    def from_plane(value, step):
+        return lax.ppermute(value, "dp", [((i + step) % planes, i) for i in range(planes)])
+
+    def from_core(value):
+        return lax.ppermute(value, "space", [(0, 1), (1, 0)])
 
     blocks = call(
         spread_features,
-        shape((members, local + 3 * NECK_ROWS, pixels), BF),
-        where, features.reshape(pixels, local), conv, lateral_eight,
+        shape((members, local * pixels // LANES + share_rows, LANES), BF),
+        (band, parity), features.reshape(pixels, local), conv, lateral_eight,
+        space=pltpu.HBM,
+        scratch=[
+            pltpu.VMEM((pixels, local), BF),
+            pltpu.VMEM(conv.shape[1:], BF),
+            pltpu.VMEM(lateral_eight.shape, BF),
+            pltpu.SemaphoreType.DMA((3,)),
+        ],
     )
     gathered = lax.all_to_all(blocks, MP, 0, 0, tiled=True)
-    other = lax.ppermute(gathered, "space", swap)
-    blocks = call(
+    blocks, share, share_low, share_high = call(
         raise_map,
-        shape((members, 3 * half_local + 5 * NECK_ROWS, LANES), BF),
-        where, gathered, deconv_weight, deconv_bias.reshape(1, half_local), lateral_coarse,
+        (
+            shape((members, 3 * half_local + 5 * NECK_ROWS, LANES), BF),
+            shape((members, share_rows, LANES), BF),
+            shape((members // 2, share_rows, LANES), BF),
+            shape((members // 2, share_rows, LANES), BF),
+        ),
+        (band,), gathered, deconv_weight, deconv_bias.reshape(1, half_local), lateral_coarse,
         scratch=[pltpu.VMEM((members, half_local, LANES), BF)],
     )
     got = lax.all_to_all(blocks, MP, 0, 0, tiled=True)
-    got_other = lax.ppermute(got, "space", swap)
+    share_low = from_plane(share_low, -1)
+    share_high = from_plane(share_high, 1)
+    mine = call(
+        merge_shares,
+        shape((SHARES, members, share_rows, LANES), BF),
+        (parity,), share, share_low, share_high,
+    )
+    theirs = from_core(mine)
+    got_other = from_core(got)
     total = call(
-        level_eight, shape((neck, LANES), F32),
-        where, got, gathered, other, norm_gain, norm_shift,
+        level_eight,
+        shape((neck, LANES), F32),
+        (band, row), got, mine, theirs, norm_gain, norm_shift,
     )
     blocks, own_sixteen, own_thirty, table = call(
         levels,
@@ -377,7 +428,7 @@
             shape((NECK_ROWS, pixels // 4), BF),
             shape((NECK_ROWS, 16), F32),
         ),
-        where, got, got_other, total, gathered, other, conv, norm_gain, norm_shift,
+        (band, row), got, got_other, total, mine, theirs, conv, norm_gain, norm_shift,
         scratch=[pltpu.VMEM((neck, 16), F32)],
     )
     got = lax.all_to_all(blocks, MP, 0, 0, tiled=True)
@@ -389,7 +440,7 @@
             shape((NECK_ROWS, pixels // 4), BF),
             shape((NECK_ROWS, pixels // 16), BF),
         ),
-        where, got, own_sixteen, own_thirty, table,
+        (band,), got, own_sixteen, own_thirty, table,
     )
 
 

time: 70.8 us -> 67.8 us (0.958)
  the two profiles are of different devices: /device:TPU:64 before, /device:TPU:96 now
where the time goes in v3:
time: 67.8 us; the launch traced here: 67.5 us
  blocking collectives  42.8 us (63%)
  waiting for transfers between devices  10.6 us (16%)
  starting transfers between devices  7.04 us (10%)
  Pallas kernels  6.35 us (9%)
  between operations  0.73 us (1%)
    all_to_all x1, blocking collectives, per_device(): gathered = lax.all_to_all(blocks, MP, 0, 0, tiled=True)  28.3 us
    all_to_all x1, blocking collectives, per_device(): got = lax.all_to_all(blocks, MP, 0, 0, tiled=True)  14.4 us
    ppermute x2, waiting for transfers between devices, from_plane(): lax.ppermute(value, 'dp', [((i + step) % planes, i) for i in range(planes)])  6.88 us
    pallas_call x6, Pallas kernels, call(): pl.pallas_call(kernel, in_specs=specs, out_specs=jax.tree.map(lambda _: p...  6.35 us
    all_to_all x1, starting transfers between devices, per_device(): got = lax.all_to_all(blocks, MP, 0, 0, tiled=True)  3.73 us
    ppermute x2, starting transfers between devices, from_plane(): lax.ppermute(value, 'dp', [((i + step) % planes, i) for i in range(planes)])  3.21 us
    all_to_all x1, waiting for transfers between devices, per_device(): got = lax.all_to_all(blocks, MP, 0, 0, tiled=True)  2.53 us
  transfers between devices with their start and end apart: 5, of which 4 were waited for; matrix products, arithmetic and copies ran while one was open for 0% of the time, Pallas kernels for 2%

profile of v3, /device:TPU:96, one launch (start us, length us, event | category | flops | bytes accessed | tf_op | source)
XLA Modules:
  0.0 67.5 jit_solution(4097987353410559639)
XLA Ops:
  0.6 1.2 %shard_map.111 = bf16[16,352,128]{2,1,0:T(8,128)(2,1)S(1)} custom-call(s32[1]{0:T(128)} %bitcast.band_at, s32[1]{0:T(128)} %bitcast.2.parity_at, bf16[512,64]{1,0:T(8,128)(2,1)} %bitcast.9, bf16[3,9,16,256]{3,2,1,0:T(8,128)(2,1)} %bitcast.6, bf16[16,512]{1,0:T(8,128)(2,1)} %lat_from.1), custom_call_target="tpu_custom_call" | custom-call | tf_op jit(solution)/shard_map/pallas_call | solution.py:341
  1.8 0.0 copy-start.1
  1.8 0.0 copy-start.2
  1.8 0.0 copy-start.5
  1.8 28.3 %all_to_all.15.gathered = bf16[16,352,128]{2,1,0:T(8,128)(2,1)S(1)} all-to-all(bf16[16,352,128]{2,1,0:T(8,128)(2,1)S(1)} %shard_map.111), channel_id=1, replica_groups=mesh['dp'=8,'space'=2,'mp_0'=4,'mp_1'=4] {'mp_0','mp_1'}, dimensions={0} | all-to-all | bytes 2883584 | tf_op jit(solution)/shard_map/all_to_all | solution.py:396
  30.2 0.0 copy-done.1
  30.2 0.0 copy-done.2
  30.2 0.0 copy-done.5
  30.2 2.0 %shard_map.112 = (bf16[16,176,128]{2,1,0:T(8,128)(2,1)}, bf16[16,96,128]{2,1,0:T(8,128)(2,1)S(1)}, bf16[8,96,128]{2,1,0:T(8,128)(2,1)S(1)}, bf16[8,96,128]{2,1,0:T(8,128)(2,1)S(1)}) custom-call(s32[1]{0:T(128)} %bitcast.band_at, bf16[16,352,128]{2,1,0:T(8,128)(2,1)S(1)} %all_to_all.15.gathered, bf16[4,32,1024]{2,1,0:T(8,128)(2,1)S(1)} %copy-done.1, ...), custom_call_target="tpu_custom_call" | custom-call | tf_op jit(solution)/shard_map/pallas_call | solution.py:341
  32.2 0.0 copy-start.3
  32.2 0.0 copy-start.4
  32.2 3.7 %all-to-all-start.1 = ((bf16[16,176,128]{2,1,0:T(8,128)(2,1)}), bf16[16,176,128]{2,1,0:T(8,128)(2,1)S(1)}, u32[]{:S(2)}, u32[]{:S(2)}) async-start(bf16[16,176,128]{2,1,0:T(8,128)(2,1)} %get-tuple-element.12), calls=%async_computation.1 | async-start | bytes 1441792 | tf_op jit(solution)/shard_map/all_to_all | solution.py:408
  36.0 3.2 %collective-permute-start.1 = (bf16[8,96,128]{2,1,0:T(8,128)(2,1)S(1)}, bf16[8,96,128]{2,1,0:T(8,128)(2,1)S(1)}, u32[]{:S(2)}, u32[]{:S(2)}) collective-permute-start(bf16[8,96,128]{2,1,0:T(8,128)(2,1)S(1)} %get-tuple-element.14), channel_id=1, source_target_pairs={{224,0},{0,32},{32,64},{64,96},{96,128},{128,160},{160,192},{192,2... | collective-permute-start | bytes 589832 | tf_op jit(solution)/shard_map/ppermute | solution.py:379
  39.2 0.0 collective-permute-start.2
  39.2 3.2 %collective-permute-done.1.low = bf16[8,96,128]{2,1,0:T(8,128)(2,1)S(1)} collective-permute-done((bf16[8,96,128]{2,1,0:T(8,128)(2,1)S(1)}, bf16[8,96,128]{2,1,0:T(8,128)(2,1)S(1)}, u32[]{:S(2)}, u32[]{:S(2)}) %collective-permute-start.1) | collective-permute-done | bytes 196640 | tf_op jit(solution)/shard_map/ppermute | solution.py:379
  42.4 3.7 %collective-permute-done.2.high = bf16[8,96,128]{2,1,0:T(8,128)(2,1)S(1)} collective-permute-done((bf16[8,96,128]{2,1,0:T(8,128)(2,1)S(1)}, bf16[8,96,128]{2,1,0:T(8,128)(2,1)S(1)}, u32[]{:S(2)}, u32[]{:S(2)}) %collective-permute-start.2) | collective-permute-done | bytes 196640 | tf_op jit(solution)/shard_map/ppermute | solution.py:379
  46.1 0.1 shard_map.113.mine
  46.1 0.0 copy-start
  46.1 0.1 collective-permute-start.3
  46.2 2.5 %all-to-all-done.1.got = bf16[16,176,128]{2,1,0:T(8,128)(2,1)S(1)} async-done(((bf16[16,176,128]{2,1,0:T(8,128)(2,1)}), bf16[16,176,128]{2,1,0:T(8,128)(2,1)S(1)}, u32[]{:S(2)}, u32[]{:S(2)}) %all-to-all-start.1) | async-done | bytes 720928 | tf_op jit(solution)/shard_map/all_to_all | solution.py:408
  48.8 0.0 collective-permute-start
  48.8 0.0 collective-permute-done.3.theirs
  48.8 0.0 copy-done.3
  48.8 0.0 copy-done.4
  48.8 1.0 %shard_map.114.total = f32[256,128]{1,0:T(8,128)S(1)} custom-call(s32[1]{0:T(128)} %bitcast.band_at, s32[1]{0:T(128)} %bitcast.1.row_at, bf16[16,176,128]{2,1,0:T(8,128)(2,1)S(1)} %all-to-all-done.1.got, bf16[2,16,96,128]{3,2,1,0:T(8,128)(2,1)S(1)} %shard_map.113.mine, bf16[2,16,96,128]{3,2,1,0:T(8,128)(2,1)S(1)} %collective-permute-done.3.theirs, ...), custom_call_target="tpu_custom_call" | custom-call | tf_op jit(solution)/shard_map/pallas_call | solution.py:341
  49.8 1.2 %collective-permute-done.got_other = bf16[16,176,128]{2,1,0:T(8,128)(2,1)S(1)} collective-permute-done((bf16[16,176,128]{2,1,0:T(8,128)(2,1)S(1)}, bf16[16,176,128]{2,1,0:T(8,128)(2,1)S(1)}, u32[]{:S(2)}, u32[]{:S(2)}) %collective-permute-start) | collective-permute-done | bytes 720928 | tf_op jit(solution)/shard_map/ppermute | solution.py:382
  50.9 0.0 copy-done
  51.0 1.3 %shard_map.115 = (bf16[16,64,128]{2,1,0:T(8,128)(2,1)S(1)}, bf16[16,512]{1,0:T(8,128)(2,1)S(1)}, bf16[16,128]{1,0:T(8,128)(2,1)S(1)}, f32[16,16]{1,0:T(8,128)S(1)}) custom-call(s32[1]{0:T(128)} %bitcast.band_at, s32[1]{0:T(128)} %bitcast.1.row_at, bf16[16,176,128]{2,1,0:T(8,128)(2,1)S(1)} %all-to-all-done.1.got, ...), custom_call_target="tpu_custom_call" | custom-call | tf_op jit(solution)/shard_map/pallas_call | solution.py:341
  52.3 14.4 %all_to_all.16.got = bf16[16,64,128]{2,1,0:T(8,128)(2,1)S(1)} all-to-all(bf16[16,64,128]{2,1,0:T(8,128)(2,1)S(1)} %get-tuple-element.16), channel_id=1, replica_groups=mesh['dp'=8,'space'=2,'mp_0'=4,'mp_1'=4] {'mp_0','mp_1'}, dimensions={0} | all-to-all | bytes 524288 | tf_op jit(solution)/shard_map/all_to_all | solution.py:434
  66.7 0.8 %shard_map.116 = (bf16[16,2048]{1,0:T(8,128)(2,1)}, bf16[16,512]{1,0:T(8,128)(2,1)}, bf16[16,128]{1,0:T(8,128)(2,1)}, bf16[16,32]{1,0:T(8,128)(2,1)}) custom-call(s32[1]{0:T(128)} %bitcast.band_at, bf16[16,64,128]{2,1,0:T(8,128)(2,1)S(1)} %all_to_all.16.got, bf16[16,512]{1,0:T(8,128)(2,1)S(1)} %get-tuple-element.17.own_sixteen, ...), custom_call_target="tpu_custom_call" | custom-call | tf_op jit(solution)/shard_map/pallas_call | solution.py:341
Async XLA Ops:
  1.8 28.4 %copy-start.1 = (bf16[4,32,1024]{2,1,0:T(8,128)(2,1)S(1)}, bf16[4,32,1024]{2,1,0:T(8,128)(2,1)}, u32[]{:S(2)}) copy-start(bf16[4,32,1024]{2,1,0:T(8,128)(2,1)} %deconv.1) | copy-start | bytes 786436
  1.8 28.4 %copy-start.2 = (bf16[2,16,1024]{2,1,0:T(8,128)(2,1)S(1)}, bf16[2,16,1024]{2,1,0:T(8,128)(2,1)}, u32[]{:S(2)}) copy-start(bf16[2,16,1024]{2,1,0:T(8,128)(2,1)} %coarse_w.1) | copy-start | bytes 196612
  1.8 28.4 %copy-start.5 = (f32[32]{0:T(128)S(1)}, f32[32]{0:T(128)}, u32[]{:S(2)}) copy-start(f32[32]{0:T(128)} %param.10) | copy-start | bytes 388
  32.2 16.5 %copy-start.3 = (f32[6,256]{1,0:T(8,128)S(1)}, f32[6,256]{1,0:T(8,128)}, u32[]{:S(2)}) copy-start(f32[6,256]{1,0:T(8,128)} %gain.3) | copy-start | bytes 18436
  32.2 16.5 %copy-start.4 = (f32[6,256]{1,0:T(8,128)S(1)}, f32[6,256]{1,0:T(8,128)}, u32[]{:S(2)}) copy-start(f32[6,256]{1,0:T(8,128)} %shift.3) | copy-start | bytes 18436
  32.2 16.5 %all-to-all-start.1 = ((bf16[16,176,128]{2,1,0:T(8,128)(2,1)}), bf16[16,176,128]{2,1,0:T(8,128)(2,1)S(1)}, u32[]{:S(2)}, u32[]{:S(2)}) async-start(bf16[16,176,128]{2,1,0:T(8,128)(2,1)} %get-tuple-element.12), calls=%async_computation.1 | async-start | bytes 1441792 | tf_op jit(solution)/shard_map/all_to_all | solution.py:408
  36.0 6.4 %collective-permute-start.1 = (bf16[8,96,128]{2,1,0:T(8,128)(2,1)S(1)}, bf16[8,96,128]{2,1,0:T(8,128)(2,1)S(1)}, u32[]{:S(2)}, u32[]{:S(2)}) collective-permute-start(bf16[8,96,128]{2,1,0:T(8,128)(2,1)S(1)} %get-tuple-element.14), channel_id=1, source_target_pairs={{224,0},{0,32},{32,64},{64,96},{96,128},{128,160},{160,192},{192,2... | collective-permute-start | bytes 589832 | tf_op jit(solution)/shard_map/ppermute | solution.py:379
  39.2 6.9 %collective-permute-start.2 = (bf16[8,96,128]{2,1,0:T(8,128)(2,1)S(1)}, bf16[8,96,128]{2,1,0:T(8,128)(2,1)S(1)}, u32[]{:S(2)}, u32[]{:S(2)}) collective-permute-start(bf16[8,96,128]{2,1,0:T(8,128)(2,1)S(1)} %get-tuple-element.15), channel_id=1, source_target_pairs={{32,0},{64,32},{96,64},{128,96},{160,128},{192,160},{224,192},{0,2... | collective-permute-start | bytes 589832 | tf_op jit(solution)/shard_map/ppermute | solution.py:379
  46.1 4.8 %copy-start = (bf16[3,16,9,256]{3,1,2,0:T(8,128)(2,1)S(1)}, bf16[3,16,9,256]{3,1,2,0:T(8,128)(2,1)}, u32[]{:S(2)}) copy-start(bf16[3,16,9,256]{3,1,2,0:T(8,128)(2,1)} %param.13) | copy-start | bytes 663556
  46.1 2.6 %collective-permute-start.3 = (bf16[2,16,96,128]{3,2,1,0:T(8,128)(2,1)S(1)}, bf16[2,16,96,128]{3,2,1,0:T(8,128)(2,1)S(1)}, u32[]{:S(2)}, u32[]{:S(2)}) collective-permute-start(bf16[2,16,96,128]{3,2,1,0:T(8,128)(2,1)S(1)} %shard_map.113.mine), channel_id=1, source_target_pairs={{0,16},{16,0},{1,17},{17,1},{2,18},{18,2},{3,19},{19,3},{4,20},{20... | collective-permute-start | bytes 2359304 | tf_op jit(solution)/shard_map/ppermute | solution.py:382
  48.8 2.2 %collective-permute-start = (bf16[16,176,128]{2,1,0:T(8,128)(2,1)S(1)}, bf16[16,176,128]{2,1,0:T(8,128)(2,1)S(1)}, u32[]{:S(2)}, u32[]{:S(2)}) collective-permute-start(bf16[16,176,128]{2,1,0:T(8,128)(2,1)S(1)} %all-to-all-done.1.got), channel_id=1, source_target_pairs={{0,16},{16,0},{1,17},{17,1},{2,18},{18,2},{3,19},{19,3},{4,20},{20... | collective-permute-start | bytes 2162696 | tf_op jit(solution)/shard_map/ppermute | solution.py:382

commit v4 on v3

--- a/solution.py
+++ b/solution.py
@@ -16,6 +16,25 @@
 NECK_ROWS = 16
 SHARES = 2
 PER_SHARE = 6
+
+
+GATHER_ORDER, SPREAD_ORDER, RETURN_ORDER = -1, 1, -1
+
+
+def place(index, members, order):
+    return index if order > 0 else members - 1 - index
+
+
+def exchanged(blocks, order):
+    members = blocks.shape[0]
+    groups = [[place(m, members, order) for m in range(members)]]
+    return lax.all_to_all(blocks, MP, 0, 0, tiled=True, axis_index_groups=None if order > 0 else groups)
+
+
+def by_source(blocks, order):
+    if order < 0:
+        blocks = jnp.concatenate([blocks[m : m + 1] for m in reversed(range(blocks.shape[0]))], axis=0)
+    return blocks
 
 
 def dot(a, b):
@@ -89,11 +108,16 @@
     split = gathered.shape[1] - weight_rows
     pixels = split // local * LANES
     half = members // 2
-    share[...] = gathered[:, split:]
-    share_low[...] = gathered[:half, split:]
-    share_high[...] = gathered[half:, split:]
+    weights = by_source(gathered[:, split:], GATHER_ORDER)
+    share[...] = weights
+    share_low[...] = weights[:half]
+    share_high[...] = weights[half:]
     x = jnp.concatenate(
-        [gathered[:, k : k + local].reshape(depth, LANES) for k in range(0, split, local)], axis=1
+        [
+            by_source(gathered[:, k : k + local], GATHER_ORDER).reshape(depth, LANES)
+            for k in range(0, split, local)
+        ],
+        axis=1,
     )
     columns = 2 * pixels // members
     raised = dot(deconv[...].reshape(taps * half_local, depth), x)
@@ -130,11 +154,12 @@
     first = band_at[0] == 0
     for m in range(members):
         row = jnp.where(first, m, members - 1 - m)
+        at = place(m, members, SPREAD_ORDER)
         for k in range(3):
-            out[m, k * half_local : (k + 1) * half_local] = rows[
+            out[at, k * half_local : (k + 1) * half_local] = rows[
                 jnp.clip(row + k - 1, 0, members - 1)
             ]
-        out[m, 3 * half_local :] = tail
+        out[at, 3 * half_local :] = tail
 
 
 def columns_of(gain, shift):
@@ -186,7 +211,9 @@
     halves = ordered_halves(first, mine, theirs)
     raised = jnp.concatenate(
         [
-            got[:, r * half_local : (r + 1) * half_local].reshape(members * half_local, LANES)
+            by_source(got[:, r * half_local : (r + 1) * half_local], SPREAD_ORDER).reshape(
+                members * half_local, LANES
+            )
             for r in range(3)
         ],
         axis=1,
@@ -252,7 +279,8 @@
     own_table[...] = table_at[pl.ds(start, NECK_ROWS), :]
 
     halves = ordered_halves(first, mine, theirs)
-    raised = got_other[:, half_local : 2 * half_local].reshape(members * half_local, LANES)
+    raised = by_source(got_other[:, half_local : 2 * half_local], SPREAD_ORDER)
+    raised = raised.reshape(members * half_local, LANES)
     lat = dot(lateral_weight(halves), raised).astype(BF).astype(F32)
     center = channel_norm(lat, *scaled(table, 0))
     center = jnp.where(row_at[0] == members - 1, center, 0.0)
@@ -263,11 +291,13 @@
     convolved = convolved.astype(BF).astype(F32)
     level = channel_norm(convolved, *scaled(table, 1)).astype(BF)
     mix = one_hot((LANES, LANES), lambda l: (l % 2) * columns + l // 2)
-    out[:, :NECK_ROWS] = dot(level, mix).astype(BF).reshape(members, NECK_ROWS, LANES)
+    level = dot(level, mix).astype(BF).reshape(members, NECK_ROWS, LANES)
+    for m in range(members):
+        out[place(m, members, RETURN_ORDER), :NECK_ROWS] = level[m]
 
     def tile(source, k):
         base = 3 * half_local + k * NECK_ROWS
-        return source[:, base : base + NECK_ROWS].reshape(neck, LANES).astype(F32)
+        return by_source(source[:, base : base + NECK_ROWS], SPREAD_ORDER).reshape(neck, LANES).astype(F32)
 
     middle = jnp.concatenate([tile(got, k) for k in range(4)], axis=1)
     rim = jnp.where(first, tile(got_other, 0), pltpu.roll(tile(got_other, 3), columns, 1))
@@ -308,7 +338,7 @@
     first = band_at[0] == 0
     neck = members * NECK_ROWS
     for r in range(members):
-        source = jnp.where(first, r, members - 1 - r)
+        source = jnp.where(first == (RETURN_ORDER > 0), r, members - 1 - r)
         eight[:, r * LANES : (r + 1) * LANES] = got[source, :NECK_ROWS]
     stats = jnp.sum(got[:, NECK_ROWS:].astype(F32), axis=0)
     stats = stats[:NECK_ROWS] + stats[NECK_ROWS : 2 * NECK_ROWS] + stats[2 * NECK_ROWS :]
@@ -393,7 +423,7 @@
             pltpu.SemaphoreType.DMA((3,)),
         ],
     )
-    gathered = lax.all_to_all(blocks, MP, 0, 0, tiled=True)
+    gathered = exchanged(blocks, GATHER_ORDER)
     blocks, share, share_low, share_high = call(
         raise_map,
         (
@@ -405,7 +435,7 @@
         (band,), gathered, deconv_weight, deconv_bias.reshape(1, half_local), lateral_coarse,
         scratch=[pltpu.VMEM((members, half_local, LANES), BF)],
     )
-    got = lax.all_to_all(blocks, MP, 0, 0, tiled=True)
+    got = exchanged(blocks, SPREAD_ORDER)
     share_low = from_plane(share_low, -1)
     share_high = from_plane(share_high, 1)
     mine = call(
@@ -431,7 +461,7 @@
         (band, row), got, got_other, total, mine, theirs, conv, norm_gain, norm_shift,
         scratch=[pltpu.VMEM((neck, 16), F32)],
     )
-    got = lax.all_to_all(blocks, MP, 0, 0, tiled=True)
+    got = exchanged(blocks, RETURN_ORDER)
     return call(
         finish,
         (

time: 67.8 us -> 65 us (0.959)
  the two profiles are of different devices: /device:TPU:96 before, /device:TPU:64 now
where the time goes in v4:
time: 65 us; the launch traced here: 63.7 us
  blocking collectives  37.3 us (57%)
  waiting for transfers between devices  11.4 us (18%)
  starting transfers between devices  7.89 us (12%)
  Pallas kernels  6.34 us (10%)
  between operations  0.73 us (1%)
    all_to_all x2, blocking collectives, exchanged(): lax.all_to_all(blocks, MP, 0, 0, tiled=True, axis_index_groups=None if or...  37.3 us
    ppermute x2, waiting for transfers between devices, from_plane(): lax.ppermute(value, 'dp', [((i + step) % planes, i) for i in range(planes)])  6.67 us
    pallas_call x6, Pallas kernels, call(): pl.pallas_call(kernel, in_specs=specs, out_specs=jax.tree.map(lambda _: p...  6.34 us
    all_to_all x1, starting transfers between devices, exchanged(): lax.all_to_all(blocks, MP, 0, 0, tiled=True, axis_index_groups=None if or...  5.69 us
    all_to_all x1, waiting for transfers between devices, exchanged(): lax.all_to_all(blocks, MP, 0, 0, tiled=True, axis_index_groups=None if or...  3.6 us
    ppermute x2, starting transfers between devices, from_plane(): lax.ppermute(value, 'dp', [((i + step) % planes, i) for i in range(planes)])  2.1 us
  transfers between devices with their start and end apart: 5, of which 4 were waited for; matrix products, arithmetic and copies ran while one was open for 0% of the time, Pallas kernels for 2%

profile of v4, /device:TPU:64, one launch (start us, length us, event | category | flops | bytes accessed | tf_op | source)
XLA Modules:
  0.0 63.7 jit_solution(3179455473362164810)
XLA Ops:
  0.6 1.2 %shard_map.111 = bf16[16,352,128]{2,1,0:T(8,128)(2,1)S(1)} custom-call(s32[1]{0:T(128)} %bitcast.band_at, s32[1]{0:T(128)} %bitcast.2.parity_at, bf16[512,64]{1,0:T(8,128)(2,1)} %bitcast.9, bf16[3,9,16,256]{3,2,1,0:T(8,128)(2,1)} %bitcast.6, bf16[16,512]{1,0:T(8,128)(2,1)} %lat_from.1), custom_call_target="tpu_custom_call" | custom-call | tf_op jit(solution)/shard_map/pallas_call | solution.py:371
  1.8 0.0 copy-start.1
  1.8 0.0 copy-start.2
  1.8 0.0 copy-start.5
  1.8 25.8 %all_to_all.15.gathered = bf16[16,352,128]{2,1,0:T(8,128)(2,1)S(1)} all-to-all(bf16[16,352,128]{2,1,0:T(8,128)(2,1)S(1)} %shard_map.111), channel_id=1, replica_groups={{15,14,13,12,11,10,9,8,7,6,5,4,3,2,1,0},{31,30,29,28,27,26,25,24,23,22,..., dimensions={0} | all-to-all | bytes 2883584 | tf_op jit(solution)/shard_map/all_to_all | solution.py:31
  27.6 0.0 copy-done.1
  27.6 0.0 copy-done.2
  27.6 0.0 copy-done.5
  27.6 2.0 %shard_map.112 = (bf16[16,176,128]{2,1,0:T(8,128)(2,1)}, bf16[16,96,128]{2,1,0:T(8,128)(2,1)S(1)}, bf16[8,96,128]{2,1,0:T(8,128)(2,1)S(1)}, bf16[8,96,128]{2,1,0:T(8,128)(2,1)S(1)}) custom-call(s32[1]{0:T(128)} %bitcast.band_at, bf16[16,352,128]{2,1,0:T(8,128)(2,1)S(1)} %all_to_all.15.gathered, bf16[4,32,1024]{2,1,0:T(8,128)(2,1)S(1)} %copy-done.1, ...), custom_call_target="tpu_custom_call" | custom-call | tf_op jit(solution)/shard_map/pallas_call | solution.py:371
  29.7 0.0 copy-start.3
  29.7 0.0 copy-start.4
  29.7 5.7 %all-to-all-start.1 = ((bf16[16,176,128]{2,1,0:T(8,128)(2,1)}), bf16[16,176,128]{2,1,0:T(8,128)(2,1)S(1)}, u32[]{:S(2)}, u32[]{:S(2)}) async-start(bf16[16,176,128]{2,1,0:T(8,128)(2,1)} %get-tuple-element.12), calls=%async_computation.1 | async-start | bytes 1441792 | tf_op jit(solution)/shard_map/all_to_all | solution.py:31
  35.4 2.0 %collective-permute-start.1 = (bf16[8,96,128]{2,1,0:T(8,128)(2,1)S(1)}, bf16[8,96,128]{2,1,0:T(8,128)(2,1)S(1)}, u32[]{:S(2)}, u32[]{:S(2)}) collective-permute-start(bf16[8,96,128]{2,1,0:T(8,128)(2,1)S(1)} %get-tuple-element.14), channel_id=1, source_target_pairs={{224,0},{0,32},{32,64},{64,96},{96,128},{128,160},{160,192},{192,2... | collective-permute-start | bytes 589832 | tf_op jit(solution)/shard_map/ppermute | solution.py:409
  37.4 0.1 collective-permute-start.2
  37.5 3.6 %collective-permute-done.1.low = bf16[8,96,128]{2,1,0:T(8,128)(2,1)S(1)} collective-permute-done((bf16[8,96,128]{2,1,0:T(8,128)(2,1)S(1)}, bf16[8,96,128]{2,1,0:T(8,128)(2,1)S(1)}, u32[]{:S(2)}, u32[]{:S(2)}) %collective-permute-start.1) | collective-permute-done | bytes 196640 | tf_op jit(solution)/shard_map/ppermute | solution.py:409
  41.1 3.0 %collective-permute-done.2.high = bf16[8,96,128]{2,1,0:T(8,128)(2,1)S(1)} collective-permute-done((bf16[8,96,128]{2,1,0:T(8,128)(2,1)S(1)}, bf16[8,96,128]{2,1,0:T(8,128)(2,1)S(1)}, u32[]{:S(2)}, u32[]{:S(2)}) %collective-permute-start.2) | collective-permute-done | bytes 196640 | tf_op jit(solution)/shard_map/ppermute | solution.py:409
  44.1 0.1 shard_map.113.mine
  44.2 0.0 copy-start
  44.2 0.1 collective-permute-start.3
  44.3 3.6 %all-to-all-done.1.got = bf16[16,176,128]{2,1,0:T(8,128)(2,1)S(1)} async-done(((bf16[16,176,128]{2,1,0:T(8,128)(2,1)}), bf16[16,176,128]{2,1,0:T(8,128)(2,1)S(1)}, u32[]{:S(2)}, u32[]{:S(2)}) %all-to-all-start.1) | async-done | bytes 720928 | tf_op jit(solution)/shard_map/all_to_all | solution.py:31
  47.9 0.0 collective-permute-start
  47.9 0.0 collective-permute-done.3.theirs
  47.9 0.0 copy-done.3
  47.9 0.0 copy-done.4
  47.9 1.0 %shard_map.114.total = f32[256,128]{1,0:T(8,128)S(1)} custom-call(s32[1]{0:T(128)} %bitcast.band_at, s32[1]{0:T(128)} %bitcast.1.row_at, bf16[16,176,128]{2,1,0:T(8,128)(2,1)S(1)} %all-to-all-done.1.got, bf16[2,16,96,128]{3,2,1,0:T(8,128)(2,1)S(1)} %shard_map.113.mine, bf16[2,16,96,128]{3,2,1,0:T(8,128)(2,1)S(1)} %collective-permute-done.3.theirs, ...), custom_call_target="tpu_custom_call" | custom-call | tf_op jit(solution)/shard_map/pallas_call | solution.py:371
  48.9 1.2 %collective-permute-done.got_other = bf16[16,176,128]{2,1,0:T(8,128)(2,1)S(1)} collective-permute-done((bf16[16,176,128]{2,1,0:T(8,128)(2,1)S(1)}, bf16[16,176,128]{2,1,0:T(8,128)(2,1)S(1)}, u32[]{:S(2)}, u32[]{:S(2)}) %collective-permute-start) | collective-permute-done | bytes 720928 | tf_op jit(solution)/shard_map/ppermute | solution.py:412
  50.1 0.0 copy-done
  50.1 1.3 %shard_map.115 = (bf16[16,64,128]{2,1,0:T(8,128)(2,1)S(1)}, bf16[16,512]{1,0:T(8,128)(2,1)S(1)}, bf16[16,128]{1,0:T(8,128)(2,1)S(1)}, f32[16,16]{1,0:T(8,128)S(1)}) custom-call(s32[1]{0:T(128)} %bitcast.band_at, s32[1]{0:T(128)} %bitcast.1.row_at, bf16[16,176,128]{2,1,0:T(8,128)(2,1)S(1)} %all-to-all-done.1.got, ...), custom_call_target="tpu_custom_call" | custom-call | tf_op jit(solution)/shard_map/pallas_call | solution.py:371
  51.4 11.5 %all_to_all.16.got = bf16[16,64,128]{2,1,0:T(8,128)(2,1)S(1)} all-to-all(bf16[16,64,128]{2,1,0:T(8,128)(2,1)S(1)} %get-tuple-element.16), channel_id=1, replica_groups={{15,14,13,12,11,10,9,8,7,6,5,4,3,2,1,0},{31,30,29,28,27,26,25,24,23,22,..., dimensions={0} | all-to-all | bytes 524288 | tf_op jit(solution)/shard_map/all_to_all | solution.py:31
  62.9 0.8 %shard_map.116 = (bf16[16,2048]{1,0:T(8,128)(2,1)}, bf16[16,512]{1,0:T(8,128)(2,1)}, bf16[16,128]{1,0:T(8,128)(2,1)}, bf16[16,32]{1,0:T(8,128)(2,1)}) custom-call(s32[1]{0:T(128)} %bitcast.band_at, bf16[16,64,128]{2,1,0:T(8,128)(2,1)S(1)} %all_to_all.16.got, bf16[16,512]{1,0:T(8,128)(2,1)S(1)} %get-tuple-element.17.own_sixteen, ...), custom_call_target="tpu_custom_call" | custom-call | tf_op jit(solution)/shard_map/pallas_call | solution.py:371
Async XLA Ops:
  1.8 25.8 %copy-start.1 = (bf16[4,32,1024]{2,1,0:T(8,128)(2,1)S(1)}, bf16[4,32,1024]{2,1,0:T(8,128)(2,1)}, u32[]{:S(2)}) copy-start(bf16[4,32,1024]{2,1,0:T(8,128)(2,1)} %deconv.1) | copy-start | bytes 786436
  1.8 25.8 %copy-start.2 = (bf16[2,16,1024]{2,1,0:T(8,128)(2,1)S(1)}, bf16[2,16,1024]{2,1,0:T(8,128)(2,1)}, u32[]{:S(2)}) copy-start(bf16[2,16,1024]{2,1,0:T(8,128)(2,1)} %coarse_w.1) | copy-start | bytes 196612
  1.8 25.8 %copy-start.5 = (f32[32]{0:T(128)S(1)}, f32[32]{0:T(128)}, u32[]{:S(2)}) copy-start(f32[32]{0:T(128)} %param.10) | copy-start | bytes 388
  29.7 18.3 %copy-start.3 = (f32[6,256]{1,0:T(8,128)S(1)}, f32[6,256]{1,0:T(8,128)}, u32[]{:S(2)}) copy-start(f32[6,256]{1,0:T(8,128)} %gain.3) | copy-start | bytes 18436
  29.7 18.3 %copy-start.4 = (f32[6,256]{1,0:T(8,128)S(1)}, f32[6,256]{1,0:T(8,128)}, u32[]{:S(2)}) copy-start(f32[6,256]{1,0:T(8,128)} %shift.3) | copy-start | bytes 18436
  29.7 18.2 %all-to-all-start.1 = ((bf16[16,176,128]{2,1,0:T(8,128)(2,1)}), bf16[16,176,128]{2,1,0:T(8,128)(2,1)S(1)}, u32[]{:S(2)}, u32[]{:S(2)}) async-start(bf16[16,176,128]{2,1,0:T(8,128)(2,1)} %get-tuple-element.12), calls=%async_computation.1 | async-start | bytes 1441792 | tf_op jit(solution)/shard_map/all_to_all | solution.py:31
  35.4 5.7 %collective-permute-start.1 = (bf16[8,96,128]{2,1,0:T(8,128)(2,1)S(1)}, bf16[8,96,128]{2,1,0:T(8,128)(2,1)S(1)}, u32[]{:S(2)}, u32[]{:S(2)}) collective-permute-start(bf16[8,96,128]{2,1,0:T(8,128)(2,1)S(1)} %get-tuple-element.14), channel_id=1, source_target_pairs={{224,0},{0,32},{32,64},{64,96},{96,128},{128,160},{160,192},{192,2... | collective-permute-start | bytes 589832 | tf_op jit(solution)/shard_map/ppermute | solution.py:409
  37.4 6.8 %collective-permute-start.2 = (bf16[8,96,128]{2,1,0:T(8,128)(2,1)S(1)}, bf16[8,96,128]{2,1,0:T(8,128)(2,1)S(1)}, u32[]{:S(2)}, u32[]{:S(2)}) collective-permute-start(bf16[8,96,128]{2,1,0:T(8,128)(2,1)S(1)} %get-tuple-element.15), channel_id=1, source_target_pairs={{32,0},{64,32},{96,64},{128,96},{160,128},{192,160},{224,192},{0,2... | collective-permute-start | bytes 589832 | tf_op jit(solution)/shard_map/ppermute | solution.py:409
  44.2 5.9 %copy-start = (bf16[3,16,9,256]{3,1,2,0:T(8,128)(2,1)S(1)}, bf16[3,16,9,256]{3,1,2,0:T(8,128)(2,1)}, u32[]{:S(2)}) copy-start(bf16[3,16,9,256]{3,1,2,0:T(8,128)(2,1)} %param.13) | copy-start | bytes 663556
  44.2 3.7 %collective-permute-start.3 = (bf16[2,16,96,128]{3,2,1,0:T(8,128)(2,1)S(1)}, bf16[2,16,96,128]{3,2,1,0:T(8,128)(2,1)S(1)}, u32[]{:S(2)}, u32[]{:S(2)}) collective-permute-start(bf16[2,16,96,128]{3,2,1,0:T(8,128)(2,1)S(1)} %shard_map.113.mine), channel_id=1, source_target_pairs={{0,16},{16,0},{1,17},{17,1},{2,18},{18,2},{3,19},{19,3},{4,20},{20... | collective-permute-start | bytes 2359304 | tf_op jit(solution)/shard_map/ppermute | solution.py:412
  47.9 2.2 %collective-permute-start = (bf16[16,176,128]{2,1,0:T(8,128)(2,1)S(1)}, bf16[16,176,128]{2,1,0:T(8,128)(2,1)S(1)}, u32[]{:S(2)}, u32[]{:S(2)}) collective-permute-start(bf16[16,176,128]{2,1,0:T(8,128)(2,1)S(1)} %all-to-all-done.1.got), channel_id=1, source_target_pairs={{0,16},{16,0},{1,17},{17,1},{2,18},{18,2},{3,19},{19,3},{4,20},{20... | collective-permute-start | bytes 2162696 | tf_op jit(solution)/shard_map/ppermute | solution.py:412

commit v5 on v4

--- a/solution.py
+++ b/solution.py
@@ -18,23 +18,23 @@
 PER_SHARE = 6
 
 
-GATHER_ORDER, SPREAD_ORDER, RETURN_ORDER = -1, 1, -1
-
-
-def place(index, members, order):
-    return index if order > 0 else members - 1 - index
+MEMBERS = 16
+GATHER_ORDER = tuple((m + 10) % MEMBERS for m in range(MEMBERS))
+SPREAD_ORDER = tuple(range(MEMBERS))
+RETURN_ORDER = tuple((m + 10) % MEMBERS for m in range(MEMBERS))
+
+
+def place(index, order):
+    return order.index(index)
 
 
 def exchanged(blocks, order):
-    members = blocks.shape[0]
-    groups = [[place(m, members, order) for m in range(members)]]
-    return lax.all_to_all(blocks, MP, 0, 0, tiled=True, axis_index_groups=None if order > 0 else groups)
+    return lax.all_to_all(blocks, MP, 0, 0, tiled=True, axis_index_groups=[list(order)])
 
 
 def by_source(blocks, order):
-    if order < 0:
-        blocks = jnp.concatenate([blocks[m : m + 1] for m in reversed(range(blocks.shape[0]))], axis=0)
-    return blocks
+    places = [place(m, order) for m in range(MEMBERS)]
+    return jnp.concatenate([blocks[k : k + 1] for k in places], axis=0)
 
 
 def dot(a, b):
@@ -62,7 +62,7 @@
     share, at = index // PER_SHARE, index % PER_SHARE
     return jnp.concatenate(
         [
-            half[share, :, at * NECK_ROWS : (at + 1) * NECK_ROWS].reshape(-1, LANES)
+            half[share][:, at * NECK_ROWS : (at + 1) * NECK_ROWS].reshape(-1, LANES)
             for half in halves
         ],
         axis=1,
@@ -154,7 +154,7 @@
     first = band_at[0] == 0
     for m in range(members):
         row = jnp.where(first, m, members - 1 - m)
-        at = place(m, members, SPREAD_ORDER)
+        at = place(m, SPREAD_ORDER)
         for k in range(3):
             out[at, k * half_local : (k + 1) * half_local] = rows[
                 jnp.clip(row + k - 1, 0, members - 1)
@@ -202,7 +202,16 @@
     return low, high
 
 
-def level_eight(band_at, row_at, got, mine, theirs, gain, shift, total_out):
+def lateral_tile(source, k, start):
+    base = start + k * NECK_ROWS
+    rows = by_source(source[:, base : base + NECK_ROWS], SPREAD_ORDER)
+    return rows.reshape(-1, LANES).astype(F32)
+
+
+def own_band(
+    band_at, row_at, got, mine, theirs, conv, gain, shift,
+    total_out, sixteen_out, thirty_out,
+):
     members = got.shape[0]
     first = band_at[0] == 0
     row = jnp.where(first, row_at[0], members - 1 - row_at[0])
@@ -231,47 +240,61 @@
             part = dot(weight_piece(halves, 3 * r + q), window)
             total = part if total is None else total + part
     total_out[...] = total
-
-
-def small_conv(normed, halo, weight, width, first):
+    start = 3 * half_local
+    middle = jnp.concatenate([lateral_tile(got, k, start) for k in range(4)], axis=1)
+    normed = channel_norm(middle, *scaled(table, 2)).astype(BF)
+    sixteen_out[...] = small_conv(normed, conv[1], LANES // 2)
+    normed = channel_norm(lateral_tile(got, 4, start), *scaled(table, 4)).astype(BF)
+    thirty_out[...] = small_conv(normed, conv[2], LANES // 4)
+
+
+def across(products, r, out_local, width):
+    size = products.shape[1]
+    column = iota((out_local, size), 1) % width
+    pieces = [
+        products[(3 * r + q) * out_local : (3 * r + q + 1) * out_local] for q in range(3)
+    ]
+    left = jnp.where(column == 0, 0.0, pltpu.roll(pieces[0], 1, 1))
+    right = jnp.where(column == width - 1, 0.0, pltpu.roll(pieces[2], size - 1, 1))
+    return left + pieces[1] + right
+
+
+def small_conv(normed, weight, width):
     taps, out_local, depth = weight.shape
-    stacked = weight.reshape(taps * out_local, depth)
-    main = dot(stacked, normed)
-    rim = dot(stacked, halo)
+    products = dot(weight.reshape(taps * out_local, depth), normed)
     cells = normed.shape[1]
-
-    def across(values, r):
-        size = values.shape[1]
-        column = iota((out_local, size), 1) % width
-        pieces = [
-            values[(3 * r + q) * out_local : (3 * r + q + 1) * out_local] for q in range(3)
-        ]
-        left = jnp.where(column == 0, 0.0, pltpu.roll(pieces[0], 1, 1))
-        right = jnp.where(column == width - 1, 0.0, pltpu.roll(pieces[2], size - 1, 1))
-        return left + pieces[1] + right
-
     lane = iota((out_local, cells), 1)
-    rim_above = jnp.where(first, 0.0, across(rim, 0))
-    rim_below = jnp.where(first, pltpu.roll(across(rim, 2), LANES - width, 1), 0.0)
-    if cells > LANES:
-        blank = jnp.zeros((out_local, cells - LANES), F32)
-        rim_above = jnp.concatenate([rim_above, blank], axis=1)
-        rim_below = jnp.concatenate([blank, rim_below], axis=1)
-    above = jnp.where(lane < width, rim_above, pltpu.roll(across(main, 0), width, 1))
-    below = jnp.where(
-        lane >= cells - width, rim_below, pltpu.roll(across(main, 2), cells - width, 1)
-    )
-    return above + across(main, 1) + below
+    above = pltpu.roll(across(products, 0, out_local, width), width, 1)
+    below = pltpu.roll(across(products, 2, out_local, width), cells - width, 1)
+    above = jnp.where(lane < width, 0.0, above)
+    below = jnp.where(lane >= cells - width, 0.0, below)
+    return above + across(products, 1, out_local, width) + below
+
+
+def small_rim(total, halo, weight, width, first):
+    taps, out_local, depth = weight.shape
+    products = dot(weight.reshape(taps * out_local, depth), halo)
+    cells = total.shape[1]
+    lane = iota((out_local, LANES), 1)
+    above = jnp.where(lane < width, across(products, 0, out_local, width), 0.0)
+    below = jnp.where(lane < width, across(products, 2, out_local, width), 0.0)
+    above = jnp.where(first, 0.0, above)
+    below = jnp.where(first, pltpu.roll(below, LANES - width, 1), 0.0)
+    if cells == LANES:
+        return total + (above + below)
+    return jnp.concatenate(
+        [total[:, :LANES] + above, total[:, LANES : cells - LANES], total[:, cells - LANES :] + below],
+        axis=1,
+    )
 
 
 def levels(
-    band_at, row_at, got, got_other, total, mine, theirs, conv, gain, shift,
+    band_at, row_at, got_other, total, total_sixteen, total_thirty, mine, theirs, conv, gain, shift,
     out, own_sixteen, own_thirty, own_table, table_at,
 ):
-    members = got.shape[0]
+    members = got_other.shape[0]
     first = band_at[0] == 0
-    neck = members * NECK_ROWS
-    half_local = (got.shape[1] - 5 * NECK_ROWS) // 3
+    half_local = (got_other.shape[1] - 5 * NECK_ROWS) // 3
     columns = LANES // 2
     table = columns_of(gain, shift)
     table_at[...] = table
@@ -293,26 +316,17 @@
     mix = one_hot((LANES, LANES), lambda l: (l % 2) * columns + l // 2)
     level = dot(level, mix).astype(BF).reshape(members, NECK_ROWS, LANES)
     for m in range(members):
-        out[place(m, members, RETURN_ORDER), :NECK_ROWS] = level[m]
-
-    def tile(source, k):
-        base = 3 * half_local + k * NECK_ROWS
-        return by_source(source[:, base : base + NECK_ROWS], SPREAD_ORDER).reshape(neck, LANES).astype(F32)
-
-    middle = jnp.concatenate([tile(got, k) for k in range(4)], axis=1)
-    rim = jnp.where(first, tile(got_other, 0), pltpu.roll(tile(got_other, 3), columns, 1))
-    sixteen = small_conv(
-        channel_norm(middle, *scaled(table, 2)).astype(BF),
-        channel_norm(rim, *scaled(table, 2)).astype(BF),
-        conv[1], columns, first,
-    ).astype(BF)
-    rim = tile(got_other, 4)
+        out[place(m, RETURN_ORDER), :NECK_ROWS] = level[m]
+
+    start = 3 * half_local
+    rim = lateral_tile(got_other, 3, start)
+    rim = jnp.where(first, lateral_tile(got_other, 0, start), pltpu.roll(rim, columns, 1))
+    normed = channel_norm(rim, *scaled(table, 2)).astype(BF)
+    sixteen = small_rim(total_sixteen[...], normed, conv[1], columns, first).astype(BF)
+    rim = lateral_tile(got_other, 4, start)
     rim = jnp.where(first, rim, pltpu.roll(rim, columns // 2, 1))
-    thirty = small_conv(
-        channel_norm(tile(got, 4), *scaled(table, 4)).astype(BF),
-        channel_norm(rim, *scaled(table, 4)).astype(BF),
-        conv[2], columns // 2, first,
-    ).astype(BF)
+    normed = channel_norm(rim, *scaled(table, 4)).astype(BF)
+    thirty = small_rim(total_thirty[...], normed, conv[2], columns // 2, first).astype(BF)
     own_sixteen[...] = sixteen
     own_thirty[...] = thirty
     floats = jnp.concatenate([sixteen, thirty], axis=1).astype(F32)
@@ -321,14 +335,15 @@
     pieces = floats.shape[1] // LANES
     stats = jnp.concatenate(
         [part[:, k * LANES : (k + 1) * LANES] for part in (sums, squares) for k in range(pieces)]
-        + [jnp.zeros((NECK_ROWS - 2 * pieces, LANES), F32)],
+        ,
         axis=0,
     )
     parts = []
     for _ in range(3):
         parts.append(stats.astype(BF))
         stats = stats - parts[-1].astype(F32)
-    parts = jnp.concatenate(parts, axis=0)
+    parts.append(jnp.zeros((out.shape[1] - NECK_ROWS - 6 * pieces, LANES), BF))
+    parts = jnp.concatenate([part.astype(F32) for part in parts], axis=0).astype(BF)
     for m in range(members):
         out[m, NECK_ROWS:] = parts
 
@@ -338,12 +353,13 @@
     first = band_at[0] == 0
     neck = members * NECK_ROWS
     for r in range(members):
-        source = jnp.where(first == (RETURN_ORDER > 0), r, members - 1 - r)
+        source = jnp.where(
+            first, place(r, RETURN_ORDER), place(members - 1 - r, RETURN_ORDER)
+        )
         eight[:, r * LANES : (r + 1) * LANES] = got[source, :NECK_ROWS]
     stats = jnp.sum(got[:, NECK_ROWS:].astype(F32), axis=0)
-    stats = stats[:NECK_ROWS] + stats[NECK_ROWS : 2 * NECK_ROWS] + stats[2 * NECK_ROWS :]
-    stats = stats / neck
     pieces = own_sixteen.shape[1] // LANES + 1
+    stats = sum(stats[2 * pieces * k : 2 * pieces * (k + 1)] for k in range(3)) / neck
 
     def apply(values, k, index):
         gain, shift = scaled(table, index)
@@ -393,7 +409,7 @@
     pixels = row_count * col_count
     half_local = deconv_weight.shape[1]
     neck = norm_gain.shape[1]
-    assert members == 2 * row_count and 2 * col_count == LANES
+    assert members == MEMBERS == 2 * row_count and 2 * col_count == LANES
     assert lateral_eight.shape[0] == NECK_ROWS and members * NECK_ROWS == neck
     shape = jax.ShapeDtypeStruct
     band, row, plane = (
@@ -445,20 +461,26 @@
     )
     theirs = from_core(mine)
     got_other = from_core(got)
-    total = call(
-        level_eight,
-        shape((neck, LANES), F32),
-        (band, row), got, mine, theirs, norm_gain, norm_shift,
+    where = (band, row)
+    weights = (mine, theirs)
+    total, total_sixteen, total_thirty = call(
+        own_band,
+        (
+            shape((neck, LANES), F32),
+            shape((NECK_ROWS, pixels), F32),
+            shape((NECK_ROWS, pixels // 4), F32),
+        ),
+        where, got, *weights, conv, norm_gain, norm_shift,
     )
     blocks, own_sixteen, own_thirty, table = call(
         levels,
         (
-            shape((members, 4 * NECK_ROWS, LANES), BF),
+            shape((members, 3 * NECK_ROWS, LANES), BF),
             shape((NECK_ROWS, pixels), BF),
             shape((NECK_ROWS, pixels // 4), BF),
             shape((NECK_ROWS, 16), F32),
         ),
-        (band, row), got, got_other, total, mine, theirs, conv, norm_gain, norm_shift,
+        where, got_other, total, total_sixteen, total_thirty, *weights, conv, norm_gain, norm_shift,
         scratch=[pltpu.VMEM((neck, 16), F32)],
     )
     got = exchanged(blocks, RETURN_ORDER)

time: 65 us -> 62.7 us (0.965)
  blocking collectives: 37.3 us -> 35.5 us
    all_to_all x2, blocking collectives: 37.3 us -> 35.5 us  [exchanged(): lax.all_to_all(blocks, MP, 0, 0, tiled=True, axis_index_groups=[list(orde...]
  transfers between devices with their start and end apart: 5 -> 5, of which waited for: 4 -> 4; matrix products, arithmetic and copies ran while one was open for 0% -> 0% of each run, Pallas kernels for 2% -> 3%
where the time goes in v5:
time: 62.7 us; the launch traced here: 62 us
  blocking collectives  35.5 us (57%)
  waiting for transfers between devices  11.4 us (18%)
  starting transfers between devices  7.66 us (12%)
  Pallas kernels  6.66 us (11%)
  between operations  0.74 us (1%)
    all_to_all x2, blocking collectives, exchanged(): lax.all_to_all(blocks, MP, 0, 0, tiled=True, axis_index_groups=[list(orde...  35.5 us
    ppermute x2, waiting for transfers between devices, from_plane(): lax.ppermute(value, 'dp', [((i + step) % planes, i) for i in range(planes)])  6.74 us
    pallas_call x6, Pallas kernels, call(): pl.pallas_call(kernel, in_specs=specs, out_specs=jax.tree.map(lambda _: p...  6.66 us
    all_to_all x1, starting transfers between devices, exchanged(): lax.all_to_all(blocks, MP, 0, 0, tiled=True, axis_index_groups=[list(orde...  5.46 us
    all_to_all x1, waiting for transfers between devices, exchanged(): lax.all_to_all(blocks, MP, 0, 0, tiled=True, axis_index_groups=[list(orde...  4.02 us
    ppermute x2, starting transfers between devices, from_plane(): lax.ppermute(value, 'dp', [((i + step) % planes, i) for i in range(planes)])  2.1 us
  transfers between devices with their start and end apart: 5, of which 4 were waited for; matrix products, arithmetic and copies ran while one was open for 0% of the time, Pallas kernels for 3%

profile of v5, /device:TPU:64, one launch (start us, length us, event | category | flops | bytes accessed | tf_op | source)
XLA Modules:
  0.0 62.0 jit_solution(14436012434210079401)
XLA Ops:
  0.6 1.2 %shard_map.111 = bf16[16,352,128]{2,1,0:T(8,128)(2,1)S(1)} custom-call(s32[1]{0:T(128)} %bitcast.band_at, s32[1]{0:T(128)} %bitcast.2.parity_at, bf16[512,64]{1,0:T(8,128)(2,1)} %bitcast.10, bf16[3,9,16,256]{3,2,1,0:T(8,128)(2,1)} %bitcast.6, bf16[16,512]{1,0:T(8,128)(2,1)} %lat_from.1), custom_call_target="tpu_custom_call" | custom-call | tf_op jit(solution)/shard_map/pallas_call | solution.py:387
  1.8 0.0 copy-start.1
  1.8 0.0 copy-start.2
  1.8 0.0 copy-start.5
  1.8 25.1 %all_to_all.15.gathered = bf16[16,352,128]{2,1,0:T(8,128)(2,1)S(1)} all-to-all(bf16[16,352,128]{2,1,0:T(8,128)(2,1)S(1)} %shard_map.111), channel_id=1, replica_groups={{10,11,12,13,14,15,0,1,2,3,4,5,6,7,8,9},{26,27,28,29,30,31,16,17,18,19,..., dimensions={0} | all-to-all | bytes 2883584 | tf_op jit(solution)/shard_map/all_to_all | solution.py:32
  27.0 0.0 copy-done.1
  27.0 0.0 copy-done.2
  27.0 0.0 copy-done.5
  27.0 2.0 %shard_map.112 = (bf16[16,176,128]{2,1,0:T(8,128)(2,1)}, bf16[16,96,128]{2,1,0:T(8,128)(2,1)S(1)}, bf16[8,96,128]{2,1,0:T(8,128)(2,1)S(1)}, bf16[8,96,128]{2,1,0:T(8,128)(2,1)S(1)}) custom-call(s32[1]{0:T(128)} %bitcast.band_at, bf16[16,352,128]{2,1,0:T(8,128)(2,1)S(1)} %all_to_all.15.gathered, bf16[4,32,1024]{2,1,0:T(8,128)(2,1)S(1)} %copy-done.1, ...), custom_call_target="tpu_custom_call" | custom-call | tf_op jit(solution)/shard_map/pallas_call | solution.py:387
  29.0 0.0 copy-start
  29.0 0.0 copy-start.3
  29.0 0.0 copy-start.4
  29.0 5.5 %all-to-all-start.1 = ((bf16[16,176,128]{2,1,0:T(8,128)(2,1)}), bf16[16,176,128]{2,1,0:T(8,128)(2,1)S(1)}, u32[]{:S(2)}, u32[]{:S(2)}) async-start(bf16[16,176,128]{2,1,0:T(8,128)(2,1)} %get-tuple-element.15), calls=%async_computation.1 | async-start | bytes 1441792 | tf_op jit(solution)/shard_map/all_to_all | solution.py:32
  34.5 2.0 %collective-permute-start.1 = (bf16[8,96,128]{2,1,0:T(8,128)(2,1)S(1)}, bf16[8,96,128]{2,1,0:T(8,128)(2,1)S(1)}, u32[]{:S(2)}, u32[]{:S(2)}) collective-permute-start(bf16[8,96,128]{2,1,0:T(8,128)(2,1)S(1)} %get-tuple-element.17), channel_id=1, source_target_pairs={{224,0},{0,32},{32,64},{64,96},{96,128},{128,160},{160,192},{192,2... | collective-permute-start | bytes 589832 | tf_op jit(solution)/shard_map/ppermute | solution.py:425
  36.5 0.1 collective-permute-start.2
  36.6 3.7 %collective-permute-done.1.low = bf16[8,96,128]{2,1,0:T(8,128)(2,1)S(1)} collective-permute-done((bf16[8,96,128]{2,1,0:T(8,128)(2,1)S(1)}, bf16[8,96,128]{2,1,0:T(8,128)(2,1)S(1)}, u32[]{:S(2)}, u32[]{:S(2)}) %collective-permute-start.1) | collective-permute-done | bytes 196640 | tf_op jit(solution)/shard_map/ppermute | solution.py:425
  40.3 3.0 %collective-permute-done.2.high = bf16[8,96,128]{2,1,0:T(8,128)(2,1)S(1)} collective-permute-done((bf16[8,96,128]{2,1,0:T(8,128)(2,1)S(1)}, bf16[8,96,128]{2,1,0:T(8,128)(2,1)S(1)}, u32[]{:S(2)}, u32[]{:S(2)}) %collective-permute-start.2) | collective-permute-done | bytes 196640 | tf_op jit(solution)/shard_map/ppermute | solution.py:425
  43.3 0.1 shard_map.113.mine
  43.4 0.1 collective-permute-start.3
  43.5 4.0 %all-to-all-done.1.got = bf16[16,176,128]{2,1,0:T(8,128)(2,1)S(1)} async-done(((bf16[16,176,128]{2,1,0:T(8,128)(2,1)}), bf16[16,176,128]{2,1,0:T(8,128)(2,1)S(1)}, u32[]{:S(2)}, u32[]{:S(2)}) %all-to-all-start.1) | async-done | bytes 720928 | tf_op jit(solution)/shard_map/all_to_all | solution.py:32
  47.5 0.0 collective-permute-start
  47.5 0.0 collective-permute-done.3.theirs
  47.5 0.0 copy-done
  47.5 0.0 copy-done.3
  47.5 0.0 copy-done.4
  47.5 1.5 %shard_map.114 = (f32[256,128]{1,0:T(8,128)S(1)}, f32[16,512]{1,0:T(8,128)S(1)}, f32[16,128]{1,0:T(8,128)S(1)}) custom-call(s32[1]{0:T(128)} %bitcast.band_at, s32[1]{0:T(128)} %bitcast.1.row_at, bf16[16,176,128]{2,1,0:T(8,128)(2,1)S(1)} %all-to-all-done.1.got, bf16[2,16,96,128]{3,2,1,0:T(8,128)(2,1)S(1)} %shard_map.113.mine, ...), custom_call_target="tpu_custom_call" | custom-call | tf_op jit(solution)/shard_map/pallas_call | solution.py:387
  49.0 0.6 %collective-permute-done.got_other = bf16[16,176,128]{2,1,0:T(8,128)(2,1)S(1)} collective-permute-done((bf16[16,176,128]{2,1,0:T(8,128)(2,1)S(1)}, bf16[16,176,128]{2,1,0:T(8,128)(2,1)S(1)}, u32[]{:S(2)}, u32[]{:S(2)}) %collective-permute-start) | collective-permute-done | bytes 720928 | tf_op jit(solution)/shard_map/ppermute | solution.py:428
  49.7 1.1 %shard_map.115 = (bf16[16,48,128]{2,1,0:T(8,128)(2,1)S(1)}, bf16[16,512]{1,0:T(8,128)(2,1)S(1)}, bf16[16,128]{1,0:T(8,128)(2,1)S(1)}, f32[16,16]{1,0:T(8,128)S(1)}) custom-call(s32[1]{0:T(128)} %bitcast.band_at, s32[1]{0:T(128)} %bitcast.1.row_at, bf16[16,176,128]{2,1,0:T(8,128)(2,1)S(1)} %collective-permute-done.got_other, ...), custom_call_target="tpu_custom_call" | custom-call | tf_op jit(solution)/shard_map/pallas_call | solution.py:387
  50.8 10.4 %all_to_all.16.got = bf16[16,48,128]{2,1,0:T(8,128)(2,1)S(1)} all-to-all(bf16[16,48,128]{2,1,0:T(8,128)(2,1)S(1)} %get-tuple-element.22), channel_id=1, replica_groups={{10,11,12,13,14,15,0,1,2,3,4,5,6,7,8,9},{26,27,28,29,30,31,16,17,18,19,..., dimensions={0} | all-to-all | bytes 393216 | tf_op jit(solution)/shard_map/all_to_all | solution.py:32
  61.2 0.8 %shard_map.116 = (bf16[16,2048]{1,0:T(8,128)(2,1)}, bf16[16,512]{1,0:T(8,128)(2,1)}, bf16[16,128]{1,0:T(8,128)(2,1)}, bf16[16,32]{1,0:T(8,128)(2,1)}) custom-call(s32[1]{0:T(128)} %bitcast.band_at, bf16[16,48,128]{2,1,0:T(8,128)(2,1)S(1)} %all_to_all.16.got, bf16[16,512]{1,0:T(8,128)(2,1)S(1)} %get-tuple-element.23.own_sixteen, ...), custom_call_target="tpu_custom_call" | custom-call | tf_op jit(solution)/shard_map/pallas_call | solution.py:387
Async XLA Ops:
  1.8 25.2 %copy-start.1 = (bf16[4,32,1024]{2,1,0:T(8,128)(2,1)S(1)}, bf16[4,32,1024]{2,1,0:T(8,128)(2,1)}, u32[]{:S(2)}) copy-start(bf16[4,32,1024]{2,1,0:T(8,128)(2,1)} %deconv.1) | copy-start | bytes 786436
  1.8 25.2 %copy-start.2 = (bf16[2,16,1024]{2,1,0:T(8,128)(2,1)S(1)}, bf16[2,16,1024]{2,1,0:T(8,128)(2,1)}, u32[]{:S(2)}) copy-start(bf16[2,16,1024]{2,1,0:T(8,128)(2,1)} %coarse_w.1) | copy-start | bytes 196612
  1.8 25.1 %copy-start.5 = (f32[32]{0:T(128)S(1)}, f32[32]{0:T(128)}, u32[]{:S(2)}) copy-start(f32[32]{0:T(128)} %param.10) | copy-start | bytes 388
  29.0 18.5 %copy-start = (bf16[3,16,9,256]{3,1,2,0:T(8,128)(2,1)S(1)}, bf16[3,16,9,256]{3,1,2,0:T(8,128)(2,1)}, u32[]{:S(2)}) copy-start(bf16[3,16,9,256]{3,1,2,0:T(8,128)(2,1)} %param.13) | copy-start | bytes 663556
  29.0 18.5 %copy-start.3 = (f32[6,256]{1,0:T(8,128)S(1)}, f32[6,256]{1,0:T(8,128)}, u32[]{:S(2)}) copy-start(f32[6,256]{1,0:T(8,128)} %gain.3) | copy-start | bytes 18436
  29.0 18.5 %copy-start.4 = (f32[6,256]{1,0:T(8,128)S(1)}, f32[6,256]{1,0:T(8,128)}, u32[]{:S(2)}) copy-start(f32[6,256]{1,0:T(8,128)} %shift.3) | copy-start | bytes 18436
  29.0 18.5 %all-to-all-start.1 = ((bf16[16,176,128]{2,1,0:T(8,128)(2,1)}), bf16[16,176,128]{2,1,0:T(8,128)(2,1)S(1)}, u32[]{:S(2)}, u32[]{:S(2)}) async-start(bf16[16,176,128]{2,1,0:T(8,128)(2,1)} %get-tuple-element.15), calls=%async_computation.1 | async-start | bytes 1441792 | tf_op jit(solution)/shard_map/all_to_all | solution.py:32
  34.5 5.8 %collective-permute-start.1 = (bf16[8,96,128]{2,1,0:T(8,128)(2,1)S(1)}, bf16[8,96,128]{2,1,0:T(8,128)(2,1)S(1)}, u32[]{:S(2)}, u32[]{:S(2)}) collective-permute-start(bf16[8,96,128]{2,1,0:T(8,128)(2,1)S(1)} %get-tuple-element.17), channel_id=1, source_target_pairs={{224,0},{0,32},{32,64},{64,96},{96,128},{128,160},{160,192},{192,2... | collective-permute-start | bytes 589832 | tf_op jit(solution)/shard_map/ppermute | solution.py:425
  36.5 6.9 %collective-permute-start.2 = (bf16[8,96,128]{2,1,0:T(8,128)(2,1)S(1)}, bf16[8,96,128]{2,1,0:T(8,128)(2,1)S(1)}, u32[]{:S(2)}, u32[]{:S(2)}) collective-permute-start(bf16[8,96,128]{2,1,0:T(8,128)(2,1)S(1)} %get-tuple-element.18), channel_id=1, source_target_pairs={{32,0},{64,32},{96,64},{128,96},{160,128},{192,160},{224,192},{0,2... | collective-permute-start | bytes 589832 | tf_op jit(solution)/shard_map/ppermute | solution.py:425
  43.4 4.1 %collective-permute-start.3 = (bf16[2,16,96,128]{3,2,1,0:T(8,128)(2,1)S(1)}, bf16[2,16,96,128]{3,2,1,0:T(8,128)(2,1)S(1)}, u32[]{:S(2)}, u32[]{:S(2)}) collective-permute-start(bf16[2,16,96,128]{3,2,1,0:T(8,128)(2,1)S(1)} %shard_map.113.mine), channel_id=1, source_target_pairs={{0,16},{16,0},{1,17},{17,1},{2,18},{18,2},{3,19},{19,3},{4,20},{20... | collective-permute-start | bytes 2359304 | tf_op jit(solution)/shard_map/ppermute | solution.py:428
  47.5 2.2 %collective-permute-start = (bf16[16,176,128]{2,1,0:T(8,128)(2,1)S(1)}, bf16[16,176,128]{2,1,0:T(8,128)(2,1)S(1)}, u32[]{:S(2)}, u32[]{:S(2)}) collective-permute-start(bf16[16,176,128]{2,1,0:T(8,128)(2,1)S(1)} %all-to-all-done.1.got), channel_id=1, source_target_pairs={{0,16},{16,0},{1,17},{17,1},{2,18},{18,2},{3,19},{19,3},{4,20},{20... | collective-permute-start | bytes 2162696 | tf_op jit(solution)/shard_map/ppermute | solution.py:428

commit v6 on v5

--- a/solution.py
+++ b/solution.py
@@ -70,86 +70,151 @@
 
 
 def spread_features(
-    band_at, parity_at, x_from, conv_from, lat_from, out, x, conv, lat, arrived
+    band_at, parity_at, x_from, conv_from, lat_from, bias_from, deconv_from, coarse_from,
+    out, pair_out, half_out, x, conv, lat, bias, arrived,
 ):
+    end = deconv_from.shape[0]
+    ends = end + coarse_from.shape[0]
     copies = [
-        pltpu.make_async_copy(x_from, x, arrived.at[0]),
-        pltpu.make_async_copy(conv_from.at[0], conv, arrived.at[1]),
-        pltpu.make_async_copy(lat_from, lat, arrived.at[2]),
+        pltpu.make_async_copy(source, target, arrived.at[k])
+        for k, (source, target) in enumerate(
+            (
+                (x_from, x),
+                (conv_from.at[0], conv),
+                (lat_from, lat),
+                (bias_from, bias),
+                (deconv_from, pair_out.at[:end]),
+                (coarse_from, pair_out.at[end:ends]),
+            )
+        )
     ]
     for copy in copies:
         copy.start()
-    for copy in copies:
+    for copy in copies[:4]:
         copy.wait()
     members = out.shape[0]
     first = band_at[0] == 0
     even = parity_at[0] == 0
-    flat = x[...].astype(F32).T.astype(BF)
-    flat = jnp.concatenate(
-        [flat[:, k : k + LANES] for k in range(0, flat.shape[1], LANES)], axis=0
-    )
+    columns = x.shape[1] // 2
+    flats = []
+    for h in range(2):
+        part = x[:, h * columns : (h + 1) * columns].reshape(-1, x.shape[2])
+        flat = part.astype(F32).T.astype(BF)
+        flats.append(
+            jnp.concatenate(
+                [flat[:, k : k + LANES] for k in range(0, flat.shape[1], LANES)], axis=0
+            )
+        )
     half = lat.shape[1] // 2
     lateral = jnp.where(first, lat[:, :half], lat[:, half:])
     pieces = [jnp.where(first, conv[t, :, :LANES], conv[t, :, LANES:]) for t in range(9)]
     pieces += [lateral[:, :LANES], lateral[:, LANES:], lateral[:, LANES:]]
     weights = [jnp.where(even, pieces[k], pieces[PER_SHARE + k]) for k in range(PER_SHARE)]
     weights = jnp.concatenate(weights, axis=0)
-    start = flat.shape[0]
+    start = flats[0].shape[0]
     for m in range(members):
-        out[m, :start] = flat
-        out[m, start:] = weights
-
-
-def raise_map(band_at, gathered, deconv, bias, coarse_w, out, share, share_low, share_high, rows):
-    members = gathered.shape[0]
-    taps, half_local, depth = deconv.shape
-    local = depth // members
-    weight_rows = share.shape[1]
-    split = gathered.shape[1] - weight_rows
-    pixels = split // local * LANES
-    half = members // 2
+        at = place(m, GATHER_ORDER)
+        out[at, :start] = flats[m % 2]
+        out[at, start:] = weights
+    rest = jnp.concatenate(
+        [bias[...], jnp.zeros((1, LANES - bias.shape[1]), F32)], axis=1
+    )
+    parts = []
+    for _ in range(3):
+        parts.append(rest.astype(BF).astype(F32))
+        rest = rest - parts[-1]
+    parts = jnp.concatenate(parts + [jnp.zeros((NECK_ROWS - 3, LANES), F32)], axis=0)
+    pair_out[ends:, :LANES] = parts.astype(BF)
+    pair_out[ends:, LANES:] = jnp.zeros((NECK_ROWS, pair_out.shape[1] - LANES), BF)
+    for copy in copies[4:]:
+        copy.wait()
+    half = half_out.shape[1]
+    half_out[...] = jnp.where(first, pair_out[:, :half], pair_out[:, half:])
+
+
+def join_halves(band_at, mine, theirs, out):
+    first = band_at[0] == 0
+    half = mine.shape[1]
+    out[:, :half] = jnp.where(first, mine[...], theirs[...])
+    out[:, half:] = jnp.where(first, theirs[...], mine[...])
+
+
+def take_shares(gathered, share, share_low, share_high):
+    half = gathered.shape[0] // 2
+    split = gathered.shape[1] - share.shape[1]
     weights = by_source(gathered[:, split:], GATHER_ORDER)
     share[...] = weights
     share_low[...] = weights[:half]
     share_high[...] = weights[half:]
-    x = jnp.concatenate(
-        [
-            by_source(gathered[:, k : k + local], GATHER_ORDER).reshape(depth, LANES)
-            for k in range(0, split, local)
-        ],
-        axis=1,
-    )
-    columns = 2 * pixels // members
-    raised = dot(deconv[...].reshape(taps * half_local, depth), x)
+
+
+def raise_map(band_at, row_at, gathered, own, other, out, rows):
+    members = gathered.shape[0]
+    half_local = rows.shape[1]
+    depth = own.shape[1]
+    local = depth // members
+    split = gathered.shape[1] - PER_SHARE * NECK_ROWS
+    tiles = [
+        by_source(gathered[:, k : k + local], GATHER_ORDER).reshape(depth, LANES)
+        for k in range(0, split, local)
+    ]
+    x = jnp.concatenate(tiles, axis=1)
+    columns = LANES // 4
+    even = (row_at[0] & 1) == 0
+
+    def of_pair(start, stop):
+        mine, theirs = own[start:stop], other[start:stop]
+        return jnp.where(even, mine, theirs), jnp.where(even, theirs, mine)
+
+    end = 4 * half_local
+    raised = [dot(weight, x) for weight in of_pair(0, end)]
+    coarse_w = [of_pair(end + k * NECK_ROWS, end + (k + 1) * NECK_ROWS) for k in range(2)]
     diagonal = iota((half_local, half_local), 0) == iota((half_local, half_local), 1)
-    bias_column = jnp.sum(jnp.where(diagonal, bias[...], 0.0), axis=1, keepdims=True)
-    low = iota((half_local, LANES), 1) < columns
+    biases = []
+    for parts in of_pair(end + 2 * NECK_ROWS, own.shape[0]):
+        parts = parts[:, :LANES].astype(F32)
+        row = (parts[0:1] + parts[1:2] + parts[2:3])[:, :half_local]
+        biases.append(jnp.sum(jnp.where(diagonal, row, 0.0), axis=1, keepdims=True))
+    chunk = iota((half_local, LANES), 1) // columns
     for a in range(2):
-        for p in range(pixels // LANES):
-            tiles = [
-                raised[
-                    (2 * a + b) * half_local : (2 * a + b + 1) * half_local,
-                    p * LANES : (p + 1) * LANES,
+        for t in range(len(tiles)):
+            parts = [
+                raised[k // 2][
+                    (2 * a + k % 2) * half_local : (2 * a + k % 2 + 1) * half_local,
+                    t * LANES : (t + 1) * LANES,
                 ]
-                + bias_column
-                for b in range(2)
+                + biases[k // 2]
+                for k in range(4)
             ]
-            swapped = [pltpu.roll(tile, columns, 1) for tile in tiles]
-            rows[4 * p + a] = jnp.where(low, tiles[0], swapped[1]).astype(BF)
-            rows[4 * p + 2 + a] = jnp.where(low, swapped[0], tiles[1]).astype(BF)
-    middle = dot(coarse_w[0], x).astype(BF)
-    low = iota((depth, LANES), 1) < columns
+            for c in range(4):
+                row = parts[c]
+                for k in range(4):
+                    if k != c:
+                        moved = pltpu.roll(parts[k], (k - c) * columns % LANES, 1)
+                        row = jnp.where(chunk == k, moved, row)
+                rows[2 * (4 * t + c) + a] = row.astype(BF)
+    middle = [dot(weight, x).astype(BF) for weight in coarse_w[0]]
+    chunk = iota((depth, LANES), 1) // columns
     pairs = []
-    for p in range(pixels // LANES):
-        tile = x[:, p * LANES : (p + 1) * LANES].astype(F32)
-        pairs.append(jnp.maximum(tile, pltpu.roll(tile, columns, 1)))
-    packed = []
-    for p in range(0, len(pairs), 2):
-        both = jnp.where(low, pairs[p], pairs[p + 1])
-        packed.append(jnp.maximum(both, pltpu.roll(both, LANES - 1, 1)).astype(BF))
-    coarse = dot(coarse_w[1], jnp.concatenate(packed, axis=1)).astype(BF)
-    coarse = dot(coarse, one_hot((pixels // 2, LANES), lambda l: 2 * l)).astype(BF)
-    tail = [middle[:, p * LANES : (p + 1) * LANES] for p in range(pixels // LANES)] + [coarse]
+    for tile in tiles:
+        tile = tile.astype(F32)
+        pairs.append(jnp.maximum(tile, pltpu.roll(tile, LANES - columns, 1)))
+    both = jnp.where(chunk % 2 == 0, pairs[0], pltpu.roll(pairs[1], columns, 1))
+    pooled = jnp.maximum(both, pltpu.roll(both, LANES - 1, 1)).astype(BF)
+    small = columns // 2
+    coarse = 0.0
+    for q, weight in enumerate(coarse_w[1]):
+        values = dot(weight, pooled).astype(BF)
+
+        def source(lane, q=q):
+            row, at = (lane - q * 4 * small) // small, lane % small
+            inside = (lane >= q * 4 * small) & (lane < (q + 1) * 4 * small)
+            return jnp.where(inside, ((row % 2) * 2 + row // 2) * columns + 2 * at, -1)
+
+        coarse = coarse + dot(values, one_hot((LANES, LANES), source))
+    tail = [
+        part[:, t * LANES : (t + 1) * LANES] for t in range(len(tiles)) for part in middle
+    ] + [coarse.astype(BF)]
     tail = jnp.concatenate(tail, axis=0)
     first = band_at[0] == 0
     for m in range(members):
@@ -186,14 +251,29 @@
 
 def windows(center):
     lane = iota(center.shape, 1)
-    columns = LANES // 2
-    odd = lane >= columns
-    swapped = pltpu.roll(center, columns, 1)
-    left = jnp.where(odd, swapped, pltpu.roll(swapped, 1, 1))
+    columns = LANES // 4
+    odd = lane // columns % 2 == 1
+    at = lane % columns
+    left = jnp.where(at == 0, pltpu.roll(center, 1, 1), pltpu.roll(center, LANES - columns + 1, 1))
+    left = jnp.where(odd, pltpu.roll(center, columns, 1), left)
     left = jnp.where(lane == 0, 0.0, left)
-    right = jnp.where(odd, pltpu.roll(swapped, LANES - 1, 1), swapped)
+    right = jnp.where(
+        at == columns - 1, pltpu.roll(center, LANES - 1, 1), pltpu.roll(center, columns - 1, 1)
+    )
+    right = jnp.where(odd, right, pltpu.roll(center, LANES - columns, 1))
     right = jnp.where(lane == LANES - 1, 0.0, right)
     return [window.astype(BF) for window in (left, center, right)]
+
+
+def paired(blocks):
+    members, rows, _ = blocks.shape
+    blocks = blocks.reshape(members // 2, 2, rows, LANES).astype(F32)
+    sides = [blocks[:, h].reshape(-1, LANES) for h in range(2)]
+    low = iota(sides[0].shape, 1) < LANES // 2
+    near = jnp.where(low, sides[0], pltpu.roll(sides[1], LANES // 2, 1))
+    far = jnp.where(low, pltpu.roll(sides[0], LANES // 2, 1), sides[1])
+    both = [side.reshape(members // 2, 1, rows, LANES) for side in (near, far)]
+    return jnp.concatenate(both, axis=1).reshape(members * rows, LANES)
 
 
 def ordered_halves(first, mine, theirs):
@@ -203,9 +283,32 @@
 
 
 def lateral_tile(source, k, start):
-    base = start + k * NECK_ROWS
-    rows = by_source(source[:, base : base + NECK_ROWS], SPREAD_ORDER)
-    return rows.reshape(-1, LANES).astype(F32)
+    base = start + k // 2 * 2 * NECK_ROWS
+    blocks = by_source(source[:, base : base + 2 * NECK_ROWS], SPREAD_ORDER)
+    blocks = blocks.reshape(-1, 2, 2 * NECK_ROWS, LANES).astype(F32)
+    sides = [blocks[:, h].reshape(-1, LANES) for h in range(2)]
+    columns = LANES // 4
+    chunk = iota(sides[0].shape, 1) // columns
+    tile = None
+    for c in range(4):
+        shift = (c - (2 * k + c // 2) % 4) * columns % LANES
+        side = sides[c % 2]
+        moved = pltpu.roll(side, shift, 1) if shift else side
+        tile = moved if tile is None else jnp.where(chunk == c, moved, tile)
+    return tile
+
+
+def coarse_tile(source, start):
+    base = start + 4 * NECK_ROWS
+    rows = paired(by_source(source[:, base : base + NECK_ROWS], SPREAD_ORDER)).astype(BF)
+    small = LANES // 8
+    return dot(
+        rows,
+        one_hot(
+            (LANES, LANES),
+            lambda l: l % (2 * small) // small * (4 * small) + l // (2 * small) * small + l % small,
+        ),
+    )
 
 
 def own_band(
@@ -220,9 +323,7 @@
     halves = ordered_halves(first, mine, theirs)
     raised = jnp.concatenate(
         [
-            by_source(got[:, r * half_local : (r + 1) * half_local], SPREAD_ORDER).reshape(
-                members * half_local, LANES
-            )
+            paired(by_source(got[:, r * half_local : (r + 1) * half_local], SPREAD_ORDER)).astype(BF)
             for r in range(3)
         ],
         axis=1,
@@ -244,7 +345,7 @@
     middle = jnp.concatenate([lateral_tile(got, k, start) for k in range(4)], axis=1)
     normed = channel_norm(middle, *scaled(table, 2)).astype(BF)
     sixteen_out[...] = small_conv(normed, conv[1], LANES // 2)
-    normed = channel_norm(lateral_tile(got, 4, start), *scaled(table, 4)).astype(BF)
+    normed = channel_norm(coarse_tile(got, start), *scaled(table, 4)).astype(BF)
     thirty_out[...] = small_conv(normed, conv[2], LANES // 4)
 
 
@@ -303,7 +404,7 @@
 
     halves = ordered_halves(first, mine, theirs)
     raised = by_source(got_other[:, half_local : 2 * half_local], SPREAD_ORDER)
-    raised = raised.reshape(members * half_local, LANES)
+    raised = paired(raised).astype(BF)
     lat = dot(lateral_weight(halves), raised).astype(BF).astype(F32)
     center = channel_norm(lat, *scaled(table, 0))
     center = jnp.where(row_at[0] == members - 1, center, 0.0)
@@ -313,7 +414,9 @@
         convolved = convolved + dot(tap, window)
     convolved = convolved.astype(BF).astype(F32)
     level = channel_norm(convolved, *scaled(table, 1)).astype(BF)
-    mix = one_hot((LANES, LANES), lambda l: (l % 2) * columns + l // 2)
+    mix = one_hot(
+        (LANES, LANES), lambda l: l // columns * columns + (l % 2) * (columns // 2) + l % columns // 2
+    )
     level = dot(level, mix).astype(BF).reshape(members, NECK_ROWS, LANES)
     for m in range(members):
         out[place(m, RETURN_ORDER), :NECK_ROWS] = level[m]
@@ -323,7 +426,7 @@
     rim = jnp.where(first, lateral_tile(got_other, 0, start), pltpu.roll(rim, columns, 1))
     normed = channel_norm(rim, *scaled(table, 2)).astype(BF)
     sixteen = small_rim(total_sixteen[...], normed, conv[1], columns, first).astype(BF)
-    rim = lateral_tile(got_other, 4, start)
+    rim = coarse_tile(got_other, start)
     rim = jnp.where(first, rim, pltpu.roll(rim, columns // 2, 1))
     normed = channel_norm(rim, *scaled(table, 4)).astype(BF)
     thirty = small_rim(total_thirty[...], normed, conv[2], columns // 2, first).astype(BF)
@@ -381,8 +484,9 @@
 
 
 def call(kernel, outs, where, *operands, scratch=(), space=pltpu.VMEM):
+    spaces = space if isinstance(space, tuple) else (space,) * len(operands)
     specs = [pl.BlockSpec(memory_space=pltpu.SMEM) for _ in where] + [
-        pl.BlockSpec(memory_space=space) for _ in operands
+        pl.BlockSpec(memory_space=space) for space in spaces
     ]
     return pl.pallas_call(
         kernel,
@@ -391,7 +495,7 @@
         out_shape=outs,
         scratch_shapes=scratch,
         compiler_params=pltpu.CompilerParams(vmem_limit_bytes=GRANT),
-    )(*where, *(pltpu.with_memory_space_constraint(x, space) for x in operands))
+    )(*where, *map(pltpu.with_memory_space_constraint, operands, spaces))
 
 
 def per_device(
@@ -427,28 +531,39 @@
     def from_core(value):
         return lax.ppermute(value, "space", [(0, 1), (1, 0)])
 
-    blocks = call(
+    bias = deconv_bias.reshape(1, half_local)
+    depth = deconv_weight.shape[2]
+    kept = (features, conv, lateral_eight, bias)
+    sent = (deconv_weight.reshape(-1, depth), lateral_coarse.reshape(-1, depth))
+    pair_rows = 4 * half_local + 3 * NECK_ROWS
+    blocks, pair, pair_half = call(
         spread_features,
-        shape((members, local * pixels // LANES + share_rows, LANES), BF),
-        (band, parity), features.reshape(pixels, local), conv, lateral_eight,
+        (
+            shape((members, local * pixels // 2 // LANES + share_rows, LANES), BF),
+            shape((pair_rows, depth), BF),
+            shape((pair_rows, depth // 2), BF),
+        ),
+        (band, parity), *kept, *sent,
         space=pltpu.HBM,
         scratch=[
-            pltpu.VMEM((pixels, local), BF),
-            pltpu.VMEM(conv.shape[1:], BF),
-            pltpu.VMEM(lateral_eight.shape, BF),
-            pltpu.SemaphoreType.DMA((3,)),
+            *(pltpu.VMEM(x.shape[k == 1 :], x.dtype) for k, x in enumerate(kept)),
+            pltpu.SemaphoreType.DMA((len(kept) + len(sent),)),
         ],
     )
+    pair_half = lax.ppermute(pair_half, MP, [(m, m ^ 1) for m in range(members)])
     gathered = exchanged(blocks, GATHER_ORDER)
-    blocks, share, share_low, share_high = call(
+    pair_other = call(
+        join_halves, shape((pair_rows, depth), BF), (band,), pair_half, from_core(pair_half)
+    )
+    share, share_low, share_high = call(
+        take_shares,
+        tuple(shape((rows, share_rows, LANES), BF) for rows in (members, members // 2, members // 2)),
+        (), gathered,
+    )
+    blocks = call(
         raise_map,
-        (
-            shape((members, 3 * half_local + 5 * NECK_ROWS, LANES), BF),
-            shape((members, share_rows, LANES), BF),
-            shape((members // 2, share_rows, LANES), BF),
-            shape((members // 2, share_rows, LANES), BF),
-        ),
-        (band,), gathered, deconv_weight, deconv_bias.reshape(1, half_local), lateral_coarse,
+        shape((members, 3 * half_local + 5 * NECK_ROWS, LANES), BF),
+        (band, row), gathered, pair, pair_other,
         scratch=[pltpu.VMEM((members, half_local, LANES), BF)],
     )
     got = exchanged(blocks, SPREAD_ORDER)

time: 62.7 us -> 62.8 us (level)
  blocking collectives: 35.5 us -> 10.4 us
  waiting for transfers between devices: 11.4 us -> 27.8 us
  starting transfers between devices: 7.66 us -> 14.9 us
  Pallas kernels: 6.66 us -> 8.12 us
    all_to_all x2 -> x1, blocking collectives: 35.5 us -> 10.4 us  [exchanged(): lax.all_to_all(blocks, MP, 0, 0, tiled=True, axis_index_groups=[list(orde...]
    ppermute x0 -> x1, waiting for transfers between devices: none -> 14.3 us  [per_device(): lax.ppermute(pair_half, MP, [(m, m ^ 1) for m in range(members)])]
    all_to_all x1 -> x2, starting transfers between devices: 5.46 us -> 12.7 us  [exchanged(): lax.all_to_all(blocks, MP, 0, 0, tiled=True, axis_index_groups=[list(orde...]
    pallas_call x6 -> x8, Pallas kernels: 6.66 us -> 8.12 us  [call(): pl.pallas_call(kernel, in_specs=specs, out_specs=jax.tree.map(lambda _: p...]
    ppermute x2, waiting for transfers between devices: 6.74 us -> 7.94 us  [from_plane(): lax.ppermute(value, 'dp', [((i + step) % planes, i) for i in range(planes)])]
    ppermute x2 -> x3, waiting for transfers between devices: 0.65 us -> 1.73 us  [from_core(): return lax.ppermute(value, 'space', [(0, 1), (1, 0)])]
    all_to_all x1 -> x2, waiting for transfers between devices: 4.02 us -> 3.87 us  [exchanged(): lax.all_to_all(blocks, MP, 0, 0, tiled=True, axis_index_groups=[list(orde...]
  transfers between devices with their start and end apart: 5 -> 8, of which waited for: 4 -> 6; matrix products, arithmetic and copies ran while one was open for 0% -> 0% of each run, Pallas kernels for 3% -> 3%
where the time goes in v6:
time: 62.8 us; the launch traced here: 62 us
  waiting for transfers between devices  27.8 us (44%)
  starting transfers between devices  14.9 us (24%)
  blocking collectives  10.4 us (17%)
  Pallas kernels  8.12 us (13%)
  between operations  0.73 us (1%)
    ppermute x1, waiting for transfers between devices, per_device(): lax.ppermute(pair_half, MP, [(m, m ^ 1) for m in range(members)])  14.3 us
    all_to_all x2, starting transfers between devices, exchanged(): lax.all_to_all(blocks, MP, 0, 0, tiled=True, axis_index_groups=[list(orde...  12.7 us
    all_to_all x1, blocking collectives, exchanged(): lax.all_to_all(blocks, MP, 0, 0, tiled=True, axis_index_groups=[list(orde...  10.4 us
    pallas_call x8, Pallas kernels, call(): pl.pallas_call(kernel, in_specs=specs, out_specs=jax.tree.map(lambda _: p...  8.12 us
    ppermute x2, waiting for transfers between devices, from_plane(): lax.ppermute(value, 'dp', [((i + step) % planes, i) for i in range(planes)])  7.94 us
    all_to_all x2, waiting for transfers between devices, exchanged(): lax.all_to_all(blocks, MP, 0, 0, tiled=True, axis_index_groups=[list(orde...  3.87 us
    ppermute x2, starting transfers between devices, from_plane(): lax.ppermute(value, 'dp', [((i + step) % planes, i) for i in range(planes)])  2.1 us
    ppermute x3, waiting for transfers between devices, from_core(): return lax.ppermute(value, 'space', [(0, 1), (1, 0)])  1.73 us
  transfers between devices with their start and end apart: 8, of which 6 were waited for; matrix products, arithmetic and copies ran while one was open for 0% of the time, Pallas kernels for 3%

profile of v6, /device:TPU:64, one launch (start us, length us, event | category | flops | bytes accessed | tf_op | source)
XLA Modules:
  0.0 62.0 jit_solution(312510038144537673)
XLA Ops:
  0.6 2.1 %shard_map.111 = (bf16[16,224,128]{2,1,0:T(8,128)(2,1)}, bf16[176,1024]{1,0:T(8,128)(2,1)S(1)}, bf16[176,512]{1,0:T(8,128)(2,1)S(1)}) custom-call(s32[1]{0:T(128)} %bitcast.band_at, s32[1]{0:T(128)} %bitcast.2.parity_at, bf16[8,64,64]{2,1,0:T(8,128)(2,1)} %x_from.1, bf16[3,9,16,256]{3,2,1,0:T(8,128)(2,1)} %bitcast.7, bf16[16,512]{1,0:T(8,128)(2,1)} %lat_from.1, ...), custom_call_target="tpu_custom_call" | custom-call | tf_op jit(solution)/shard_map/pallas_call | solution.py:491
  2.7 9.1 %all-to-all-start = ((bf16[16,224,128]{2,1,0:T(8,128)(2,1)}), bf16[16,224,128]{2,1,0:T(8,128)(2,1)S(1)}, u32[]{:S(2)}, u32[]{:S(2)}) async-start(bf16[16,224,128]{2,1,0:T(8,128)(2,1)} %get-tuple-element.17), calls=%async_computation | async-start | bytes 1835008 | tf_op jit(solution)/shard_map/all_to_all | solution.py:32
  11.9 0.0 collective-permute-start
  11.9 14.3 %collective-permute-done.mine = bf16[176,512]{1,0:T(8,128)(2,1)S(1)} collective-permute-done((bf16[176,512]{1,0:T(8,128)(2,1)S(1)}, bf16[176,512]{1,0:T(8,128)(2,1)S(1)}, u32[]{:S(2)}, u32[]{:S(2)}) %collective-permute-start) | collective-permute-done | bytes 180256 | tf_op jit(solution)/shard_map/ppermute | solution.py:553
  26.2 0.0 collective-permute-start.1
  26.2 1.4 %collective-permute-done.1.theirs = bf16[176,512]{1,0:T(8,128)(2,1)S(1)} collective-permute-done((bf16[176,512]{1,0:T(8,128)(2,1)S(1)}, bf16[176,512]{1,0:T(8,128)(2,1)S(1)}, u32[]{:S(2)}, u32[]{:S(2)}) %collective-permute-start.1) | collective-permute-done | bytes 180256 | tf_op jit(solution)/shard_map/ppermute | solution.py:532
  27.6 0.0 all-to-all-done.gathered
  27.6 1.8 %shard_map.113 = bf16[16,176,128]{2,1,0:T(8,128)(2,1)} custom-call(s32[1]{0:T(128)} %bitcast.band_at, s32[1]{0:T(128)} %bitcast.1.row_at, bf16[16,224,128]{2,1,0:T(8,128)(2,1)S(1)} %all-to-all-done.gathered, bf16[176,1024]{1,0:T(8,128)(2,1)S(1)} %get-tuple-element.18.own, bf16[176,1024]{1,0:T(8,128)(2,1)S(1)} %shard_map.112.other), custom_call_target="tpu_custom_call" | custom-call | tf_op jit(solution)/shard_map/pallas_call | solution.py:491
  29.5 3.6 %all-to-all-start.1 = ((bf16[16,176,128]{2,1,0:T(8,128)(2,1)}), bf16[16,176,128]{2,1,0:T(8,128)(2,1)S(1)}, u32[]{:S(2)}, u32[]{:S(2)}) async-start(bf16[16,176,128]{2,1,0:T(8,128)(2,1)} %shard_map.113), calls=%async_computation.1 | async-start | bytes 1441792 | tf_op jit(solution)/shard_map/all_to_all | solution.py:32
  33.1 0.1 shard_map.114
  33.2 2.0 %collective-permute-start.3 = (bf16[8,96,128]{2,1,0:T(8,128)(2,1)S(1)}, bf16[8,96,128]{2,1,0:T(8,128)(2,1)S(1)}, u32[]{:S(2)}, u32[]{:S(2)}) collective-permute-start(bf16[8,96,128]{2,1,0:T(8,128)(2,1)S(1)} %get-tuple-element.21), channel_id=1, source_target_pairs={{224,0},{0,32},{32,64},{64,96},{96,128},{128,160},{160,192},{192,2... | collective-permute-start | bytes 589832 | tf_op jit(solution)/shard_map/ppermute | solution.py:529
  35.2 0.1 collective-permute-start.4
  35.3 4.9 %collective-permute-done.3.low = bf16[8,96,128]{2,1,0:T(8,128)(2,1)S(1)} collective-permute-done((bf16[8,96,128]{2,1,0:T(8,128)(2,1)S(1)}, bf16[8,96,128]{2,1,0:T(8,128)(2,1)S(1)}, u32[]{:S(2)}, u32[]{:S(2)}) %collective-permute-start.3) | collective-permute-done | bytes 196640 | tf_op jit(solution)/shard_map/ppermute | solution.py:529
  40.2 3.0 %collective-permute-done.4.high = bf16[8,96,128]{2,1,0:T(8,128)(2,1)S(1)} collective-permute-done((bf16[8,96,128]{2,1,0:T(8,128)(2,1)S(1)}, bf16[8,96,128]{2,1,0:T(8,128)(2,1)S(1)}, u32[]{:S(2)}, u32[]{:S(2)}) %collective-permute-start.4) | collective-permute-done | bytes 196640 | tf_op jit(solution)/shard_map/ppermute | solution.py:529
  43.2 0.0 copy-start
  43.2 0.0 copy-start.1
  43.2 0.0 copy-start.2
  43.2 0.1 shard_map.115.mine
  43.3 0.1 collective-permute-start.5
  43.4 3.9 %all-to-all-done.1.got = bf16[16,176,128]{2,1,0:T(8,128)(2,1)S(1)} async-done(((bf16[16,176,128]{2,1,0:T(8,128)(2,1)}), bf16[16,176,128]{2,1,0:T(8,128)(2,1)S(1)}, u32[]{:S(2)}, u32[]{:S(2)}) %all-to-all-start.1) | async-done | bytes 720928 | tf_op jit(solution)/shard_map/all_to_all | solution.py:32
  47.3 0.0 collective-permute-start.2
  47.3 0.0 collective-permute-done.5.theirs
  47.3 0.0 copy-done
  47.3 0.0 copy-done.1
  47.3 0.0 copy-done.2
  47.3 1.8 %shard_map.116 = (f32[256,128]{1,0:T(8,128)S(1)}, f32[16,512]{1,0:T(8,128)S(1)}, f32[16,128]{1,0:T(8,128)S(1)}) custom-call(s32[1]{0:T(128)} %bitcast.band_at, s32[1]{0:T(128)} %bitcast.1.row_at, bf16[16,176,128]{2,1,0:T(8,128)(2,1)S(1)} %all-to-all-done.1.got, bf16[2,16,96,128]{3,2,1,0:T(8,128)(2,1)S(1)} %shard_map.115.mine, ...), custom_call_target="tpu_custom_call" | custom-call | tf_op jit(solution)/shard_map/pallas_call | solution.py:491
  49.1 0.3 collective-permute-done.2.got_other
  49.4 1.4 %shard_map.117 = (bf16[16,48,128]{2,1,0:T(8,128)(2,1)S(1)}, bf16[16,512]{1,0:T(8,128)(2,1)S(1)}, bf16[16,128]{1,0:T(8,128)(2,1)S(1)}, f32[16,16]{1,0:T(8,128)S(1)}) custom-call(s32[1]{0:T(128)} %bitcast.band_at, s32[1]{0:T(128)} %bitcast.1.row_at, bf16[16,176,128]{2,1,0:T(8,128)(2,1)S(1)} %collective-permute-done.2.got_other, ...), custom_call_target="tpu_custom_call" | custom-call | tf_op jit(solution)/shard_map/pallas_call | solution.py:491
  50.8 10.4 %all_to_all.15.got = bf16[16,48,128]{2,1,0:T(8,128)(2,1)S(1)} all-to-all(bf16[16,48,128]{2,1,0:T(8,128)(2,1)S(1)} %get-tuple-element.26), channel_id=1, replica_groups={{10,11,12,13,14,15,0,1,2,3,4,5,6,7,8,9},{26,27,28,29,30,31,16,17,18,19,..., dimensions={0} | all-to-all | bytes 393216 | tf_op jit(solution)/shard_map/all_to_all | solution.py:32
  61.2 0.8 %shard_map.118 = (bf16[16,2048]{1,0:T(8,128)(2,1)}, bf16[16,512]{1,0:T(8,128)(2,1)}, bf16[16,128]{1,0:T(8,128)(2,1)}, bf16[16,32]{1,0:T(8,128)(2,1)}) custom-call(s32[1]{0:T(128)} %bitcast.band_at, bf16[16,48,128]{2,1,0:T(8,128)(2,1)S(1)} %all_to_all.15.got, bf16[16,512]{1,0:T(8,128)(2,1)S(1)} %get-tuple-element.27.own_sixteen, ...), custom_call_target="tpu_custom_call" | custom-call | tf_op jit(solution)/shard_map/pallas_call | solution.py:491
  (1 shorter events, 0.0 us)
Async XLA Ops:
  2.7 24.9 %all-to-all-start = ((bf16[16,224,128]{2,1,0:T(8,128)(2,1)}), bf16[16,224,128]{2,1,0:T(8,128)(2,1)S(1)}, u32[]{:S(2)}, u32[]{:S(2)}) async-start(bf16[16,224,128]{2,1,0:T(8,128)(2,1)} %get-tuple-element.17), calls=%async_computation | async-start | bytes 1835008 | tf_op jit(solution)/shard_map/all_to_all | solution.py:32
  11.9 14.3 %collective-permute-start = (bf16[176,512]{1,0:T(8,128)(2,1)S(1)}, bf16[176,512]{1,0:T(8,128)(2,1)S(1)}, u32[]{:S(2)}, u32[]{:S(2)}) collective-permute-start(bf16[176,512]{1,0:T(8,128)(2,1)S(1)} %get-tuple-element.19), channel_id=1, source_target_pairs={{0,1},{1,0},{2,3},{3,2},{4,5},{5,4},{6,7},{7,6},{8,9},{9,8},{10,11... | collective-permute-start | bytes 540680 | tf_op jit(solution)/shard_map/ppermute | solution.py:553
  26.2 1.4 %collective-permute-start.1 = (bf16[176,512]{1,0:T(8,128)(2,1)S(1)}, bf16[176,512]{1,0:T(8,128)(2,1)S(1)}, u32[]{:S(2)}, u32[]{:S(2)}) collective-permute-start(bf16[176,512]{1,0:T(8,128)(2,1)S(1)} %collective-permute-done.mine), channel_id=1, source_target_pairs={{0,16},{16,0},{1,17},{17,1},{2,18},{18,2},{3,19},{19,3},{4,20},{20... | collective-permute-start | bytes 540680 | tf_op jit(solution)/shard_map/ppermute | solution.py:532
  29.5 17.8 %all-to-all-start.1 = ((bf16[16,176,128]{2,1,0:T(8,128)(2,1)}), bf16[16,176,128]{2,1,0:T(8,128)(2,1)S(1)}, u32[]{:S(2)}, u32[]{:S(2)}) async-start(bf16[16,176,128]{2,1,0:T(8,128)(2,1)} %shard_map.113), calls=%async_computation.1 | async-start | bytes 1441792 | tf_op jit(solution)/shard_map/all_to_all | solution.py:32
  33.2 7.0 %collective-permute-start.3 = (bf16[8,96,128]{2,1,0:T(8,128)(2,1)S(1)}, bf16[8,96,128]{2,1,0:T(8,128)(2,1)S(1)}, u32[]{:S(2)}, u32[]{:S(2)}) collective-permute-start(bf16[8,96,128]{2,1,0:T(8,128)(2,1)S(1)} %get-tuple-element.21), channel_id=1, source_target_pairs={{224,0},{0,32},{32,64},{64,96},{96,128},{128,160},{160,192},{192,2... | collective-permute-start | bytes 589832 | tf_op jit(solution)/shard_map/ppermute | solution.py:529
  35.2 8.1 %collective-permute-start.4 = (bf16[8,96,128]{2,1,0:T(8,128)(2,1)S(1)}, bf16[8,96,128]{2,1,0:T(8,128)(2,1)S(1)}, u32[]{:S(2)}, u32[]{:S(2)}) collective-permute-start(bf16[8,96,128]{2,1,0:T(8,128)(2,1)S(1)} %get-tuple-element.22), channel_id=1, source_target_pairs={{32,0},{64,32},{96,64},{128,96},{160,128},{192,160},{224,192},{0,2... | collective-permute-start | bytes 589832 | tf_op jit(solution)/shard_map/ppermute | solution.py:529
  43.2 4.0 %copy-start = (bf16[3,16,9,256]{3,1,2,0:T(8,128)(2,1)S(1)}, bf16[3,16,9,256]{3,1,2,0:T(8,128)(2,1)}, u32[]{:S(2)}) copy-start(bf16[3,16,9,256]{3,1,2,0:T(8,128)(2,1)} %param.13) | copy-start | bytes 663556
  43.2 4.0 %copy-start.1 = (f32[6,256]{1,0:T(8,128)S(1)}, f32[6,256]{1,0:T(8,128)}, u32[]{:S(2)}) copy-start(f32[6,256]{1,0:T(8,128)} %gain.3) | copy-start | bytes 18436
  43.2 4.0 %copy-start.2 = (f32[6,256]{1,0:T(8,128)S(1)}, f32[6,256]{1,0:T(8,128)}, u32[]{:S(2)}) copy-start(f32[6,256]{1,0:T(8,128)} %shift.3) | copy-start | bytes 18436
  43.3 4.0 %collective-permute-start.5 = (bf16[2,16,96,128]{3,2,1,0:T(8,128)(2,1)S(1)}, bf16[2,16,96,128]{3,2,1,0:T(8,128)(2,1)S(1)}, u32[]{:S(2)}, u32[]{:S(2)}) collective-permute-start(bf16[2,16,96,128]{3,2,1,0:T(8,128)(2,1)S(1)} %shard_map.115.mine), channel_id=1, source_target_pairs={{0,16},{16,0},{1,17},{17,1},{2,18},{18,2},{3,19},{19,3},{4,20},{20... | collective-permute-start | bytes 2359304 | tf_op jit(solution)/shard_map/ppermute | solution.py:532
  47.3 2.2 %collective-permute-start.2 = (bf16[16,176,128]{2,1,0:T(8,128)(2,1)S(1)}, bf16[16,176,128]{2,1,0:T(8,128)(2,1)S(1)}, u32[]{:S(2)}, u32[]{:S(2)}) collective-permute-start(bf16[16,176,128]{2,1,0:T(8,128)(2,1)S(1)} %all-to-all-done.1.got), channel_id=1, source_target_pairs={{0,16},{16,0},{1,17},{17,1},{2,18},{18,2},{3,19},{19,3},{4,20},{20... | collective-permute-start | bytes 2162696 | tf_op jit(solution)/shard_map/ppermute | solution.py:532

commit v7 on v6

--- a/solution.py
+++ b/solution.py
@@ -71,7 +71,7 @@
 
 def spread_features(
     band_at, parity_at, x_from, conv_from, lat_from, bias_from, deconv_from, coarse_from,
-    out, pair_out, half_out, x, conv, lat, bias, arrived,
+    out, pair_out, half_out, x, conv, lat, bias, arrived, blocks, left,
 ):
     end = deconv_from.shape[0]
     ends = end + coarse_from.shape[0]
@@ -112,10 +112,14 @@
     weights = [jnp.where(even, pieces[k], pieces[PER_SHARE + k]) for k in range(PER_SHARE)]
     weights = jnp.concatenate(weights, axis=0)
     start = flats[0].shape[0]
+    for h in range(2):
+        blocks[h, :start] = flats[h]
+        blocks[h, start:] = weights
+    leaving = []
     for m in range(members):
-        at = place(m, GATHER_ORDER)
-        out[at, :start] = flats[m % 2]
-        out[at, start:] = weights
+        target = out.at[place(m, GATHER_ORDER)]
+        leaving.append(pltpu.make_async_copy(blocks.at[m % 2], target, left.at[m]))
+        leaving[-1].start()
     rest = jnp.concatenate(
         [bias[...], jnp.zeros((1, LANES - bias.shape[1]), F32)], axis=1
     )
@@ -130,6 +134,8 @@
         copy.wait()
     half = half_out.shape[1]
     half_out[...] = jnp.where(first, pair_out[:, :half], pair_out[:, half:])
+    for copy in leaving:
+        copy.wait()
 
 
 def join_halves(band_at, mine, theirs, out):
@@ -148,7 +154,7 @@
     share_high[...] = weights[half:]
 
 
-def raise_map(band_at, row_at, gathered, own, other, out, rows):
+def raise_map(band_at, row_at, gathered, own, other, out, rows, blocks, left):
     members = gathered.shape[0]
     half_local = rows.shape[1]
     depth = own.shape[1]
@@ -217,14 +223,19 @@
     ] + [coarse.astype(BF)]
     tail = jnp.concatenate(tail, axis=0)
     first = band_at[0] == 0
+    leaving = []
     for m in range(members):
         row = jnp.where(first, m, members - 1 - m)
         at = place(m, SPREAD_ORDER)
         for k in range(3):
-            out[at, k * half_local : (k + 1) * half_local] = rows[
+            blocks[at, k * half_local : (k + 1) * half_local] = rows[
                 jnp.clip(row + k - 1, 0, members - 1)
             ]
-        out[at, 3 * half_local :] = tail
+        blocks[at, 3 * half_local :] = tail
+        leaving.append(pltpu.make_async_copy(blocks.at[at], out.at[at], left.at[at]))
+        leaving[-1].start()
+    for copy in leaving:
+        copy.wait()
 
 
 def columns_of(gain, shift):
@@ -483,7 +494,7 @@
     sixty[...] = dot(last, pick).astype(BF)
 
 
-def call(kernel, outs, where, *operands, scratch=(), space=pltpu.VMEM):
+def call(kernel, outs, where, *operands, scratch=(), space=pltpu.VMEM, direct=False):
     spaces = space if isinstance(space, tuple) else (space,) * len(operands)
     specs = [pl.BlockSpec(memory_space=pltpu.SMEM) for _ in where] + [
         pl.BlockSpec(memory_space=space) for space in spaces
@@ -491,7 +502,13 @@
     return pl.pallas_call(
         kernel,
         in_specs=specs,
-        out_specs=jax.tree.map(lambda _: pl.BlockSpec(memory_space=pltpu.VMEM), outs),
+        out_specs=jax.tree.unflatten(
+            jax.tree.structure(outs),
+            [
+                pl.BlockSpec(memory_space=pltpu.HBM if direct and k == 0 else pltpu.VMEM)
+                for k in range(len(jax.tree.leaves(outs)))
+            ],
+        ),
         out_shape=outs,
         scratch_shapes=scratch,
         compiler_params=pltpu.CompilerParams(vmem_limit_bytes=GRANT),
@@ -545,9 +562,12 @@
         ),
         (band, parity), *kept, *sent,
         space=pltpu.HBM,
+        direct=True,
         scratch=[
             *(pltpu.VMEM(x.shape[k == 1 :], x.dtype) for k, x in enumerate(kept)),
             pltpu.SemaphoreType.DMA((len(kept) + len(sent),)),
+            pltpu.VMEM((2, local * pixels // 2 // LANES + share_rows, LANES), BF),
+            pltpu.SemaphoreType.DMA((members,)),
         ],
     )
     pair_half = lax.ppermute(pair_half, MP, [(m, m ^ 1) for m in range(members)])
@@ -564,7 +584,12 @@
         raise_map,
         shape((members, 3 * half_local + 5 * NECK_ROWS, LANES), BF),
         (band, row), gathered, pair, pair_other,
-        scratch=[pltpu.VMEM((members, half_local, LANES), BF)],
+        scratch=[
+            pltpu.VMEM((members, half_local, LANES), BF),
+            pltpu.VMEM((members, 3 * half_local + 5 * NECK_ROWS, LANES), BF),
+            pltpu.SemaphoreType.DMA((members,)),
+        ],
+        direct=True,
     )
     got = exchanged(blocks, SPREAD_ORDER)
     share_low = from_plane(share_low, -1)

time: 62.8 us -> 63 us (level)
  no operation moved by 1% of the time
where the time goes in v7:
time: 63 us; the launch traced here: 62.2 us
  waiting for transfers between devices  27.8 us (44%)
  starting transfers between devices  14.9 us (24%)
  blocking collectives  10.4 us (17%)
  Pallas kernels  8.28 us (13%)
  between operations  0.74 us (1%)
    ppermute x1, waiting for transfers between devices, per_device(): lax.ppermute(pair_half, MP, [(m, m ^ 1) for m in range(members)])  14.3 us
    all_to_all x2, starting transfers between devices, exchanged(): lax.all_to_all(blocks, MP, 0, 0, tiled=True, axis_index_groups=[list(orde...  12.7 us
    all_to_all x1, blocking collectives, exchanged(): lax.all_to_all(blocks, MP, 0, 0, tiled=True, axis_index_groups=[list(orde...  10.4 us
    pallas_call x8, Pallas kernels, call(): pl.pallas_call(kernel, in_specs=specs, out_specs=jax.tree.unflatten(jax.t...  8.28 us
    ppermute x2, waiting for transfers between devices, from_plane(): lax.ppermute(value, 'dp', [((i + step) % planes, i) for i in range(planes)])  7.95 us
    all_to_all x2, waiting for transfers between devices, exchanged(): lax.all_to_all(blocks, MP, 0, 0, tiled=True, axis_index_groups=[list(orde...  3.86 us
    ppermute x2, starting transfers between devices, from_plane(): lax.ppermute(value, 'dp', [((i + step) % planes, i) for i in range(planes)])  2.1 us
    ppermute x3, waiting for transfers between devices, from_core(): return lax.ppermute(value, 'space', [(0, 1), (1, 0)])  1.73 us
  transfers between devices with their start and end apart: 8, of which 6 were waited for; matrix products, arithmetic and copies ran while one was open for 0% of the time, Pallas kernels for 3%

profile of v7, /device:TPU:64, one launch (start us, length us, event | category | flops | bytes accessed | tf_op | source)
XLA Modules:
  0.0 62.2 jit_solution(12172534198719810740)
XLA Ops:
  0.6 2.2 %shard_map.111 = (bf16[16,224,128]{2,1,0:T(8,128)(2,1)}, bf16[176,1024]{1,0:T(8,128)(2,1)S(1)}, bf16[176,512]{1,0:T(8,128)(2,1)S(1)}) custom-call(s32[1]{0:T(128)} %bitcast.band_at, s32[1]{0:T(128)} %bitcast.2.parity_at, bf16[8,64,64]{2,1,0:T(8,128)(2,1)} %x_from.1, bf16[3,9,16,256]{3,2,1,0:T(8,128)(2,1)} %bitcast.7, bf16[16,512]{1,0:T(8,128)(2,1)} %lat_from.1, ...), custom_call_target="tpu_custom_call" | custom-call | tf_op jit(solution)/shard_map/pallas_call | solution.py:502
  2.8 9.1 %all-to-all-start = ((bf16[16,224,128]{2,1,0:T(8,128)(2,1)}), bf16[16,224,128]{2,1,0:T(8,128)(2,1)S(1)}, u32[]{:S(2)}, u32[]{:S(2)}) async-start(bf16[16,224,128]{2,1,0:T(8,128)(2,1)} %get-tuple-element.17), calls=%async_computation | async-start | bytes 1835008 | tf_op jit(solution)/shard_map/all_to_all | solution.py:32
  11.9 0.0 collective-permute-start
  11.9 14.3 %collective-permute-done.mine = bf16[176,512]{1,0:T(8,128)(2,1)S(1)} collective-permute-done((bf16[176,512]{1,0:T(8,128)(2,1)S(1)}, bf16[176,512]{1,0:T(8,128)(2,1)S(1)}, u32[]{:S(2)}, u32[]{:S(2)}) %collective-permute-start) | collective-permute-done | bytes 180256 | tf_op jit(solution)/shard_map/ppermute | solution.py:573
  26.2 0.0 collective-permute-start.1
  26.2 1.4 %collective-permute-done.1.theirs = bf16[176,512]{1,0:T(8,128)(2,1)S(1)} collective-permute-done((bf16[176,512]{1,0:T(8,128)(2,1)S(1)}, bf16[176,512]{1,0:T(8,128)(2,1)S(1)}, u32[]{:S(2)}, u32[]{:S(2)}) %collective-permute-start.1) | collective-permute-done | bytes 180256 | tf_op jit(solution)/shard_map/ppermute | solution.py:549
  27.7 0.0 all-to-all-done.gathered
  27.7 1.9 %shard_map.113 = bf16[16,176,128]{2,1,0:T(8,128)(2,1)} custom-call(s32[1]{0:T(128)} %bitcast.band_at, s32[1]{0:T(128)} %bitcast.1.row_at, bf16[16,224,128]{2,1,0:T(8,128)(2,1)S(1)} %all-to-all-done.gathered, bf16[176,1024]{1,0:T(8,128)(2,1)S(1)} %get-tuple-element.18.own, bf16[176,1024]{1,0:T(8,128)(2,1)S(1)} %shard_map.112.other), custom_call_target="tpu_custom_call" | custom-call | tf_op jit(solution)/shard_map/pallas_call | solution.py:502
  29.6 3.6 %all-to-all-start.1 = ((bf16[16,176,128]{2,1,0:T(8,128)(2,1)}), bf16[16,176,128]{2,1,0:T(8,128)(2,1)S(1)}, u32[]{:S(2)}, u32[]{:S(2)}) async-start(bf16[16,176,128]{2,1,0:T(8,128)(2,1)} %shard_map.113), calls=%async_computation.1 | async-start | bytes 1441792 | tf_op jit(solution)/shard_map/all_to_all | solution.py:32
  33.2 0.1 shard_map.114
  33.4 2.0 %collective-permute-start.3 = (bf16[8,96,128]{2,1,0:T(8,128)(2,1)S(1)}, bf16[8,96,128]{2,1,0:T(8,128)(2,1)S(1)}, u32[]{:S(2)}, u32[]{:S(2)}) collective-permute-start(bf16[8,96,128]{2,1,0:T(8,128)(2,1)S(1)} %get-tuple-element.21), channel_id=1, source_target_pairs={{224,0},{0,32},{32,64},{64,96},{96,128},{128,160},{160,192},{192,2... | collective-permute-start | bytes 589832 | tf_op jit(solution)/shard_map/ppermute | solution.py:546
  35.4 0.1 collective-permute-start.4
  35.5 4.9 %collective-permute-done.3.low = bf16[8,96,128]{2,1,0:T(8,128)(2,1)S(1)} collective-permute-done((bf16[8,96,128]{2,1,0:T(8,128)(2,1)S(1)}, bf16[8,96,128]{2,1,0:T(8,128)(2,1)S(1)}, u32[]{:S(2)}, u32[]{:S(2)}) %collective-permute-start.3) | collective-permute-done | bytes 196640 | tf_op jit(solution)/shard_map/ppermute | solution.py:546
  40.4 3.0 %collective-permute-done.4.high = bf16[8,96,128]{2,1,0:T(8,128)(2,1)S(1)} collective-permute-done((bf16[8,96,128]{2,1,0:T(8,128)(2,1)S(1)}, bf16[8,96,128]{2,1,0:T(8,128)(2,1)S(1)}, u32[]{:S(2)}, u32[]{:S(2)}) %collective-permute-start.4) | collective-permute-done | bytes 196640 | tf_op jit(solution)/shard_map/ppermute | solution.py:546
  43.4 0.0 copy-start
  43.4 0.0 copy-start.1
  43.4 0.0 copy-start.2
  43.4 0.1 shard_map.115.mine
  43.5 0.1 collective-permute-start.5
  43.6 3.9 %all-to-all-done.1.got = bf16[16,176,128]{2,1,0:T(8,128)(2,1)S(1)} async-done(((bf16[16,176,128]{2,1,0:T(8,128)(2,1)}), bf16[16,176,128]{2,1,0:T(8,128)(2,1)S(1)}, u32[]{:S(2)}, u32[]{:S(2)}) %all-to-all-start.1) | async-done | bytes 720928 | tf_op jit(solution)/shard_map/all_to_all | solution.py:32
  47.4 0.0 collective-permute-start.2
  47.4 0.0 collective-permute-done.5.theirs
  47.4 0.0 copy-done
  47.4 0.0 copy-done.1
  47.5 0.0 copy-done.2
  47.5 1.8 %shard_map.116 = (f32[256,128]{1,0:T(8,128)S(1)}, f32[16,512]{1,0:T(8,128)S(1)}, f32[16,128]{1,0:T(8,128)S(1)}) custom-call(s32[1]{0:T(128)} %bitcast.band_at, s32[1]{0:T(128)} %bitcast.1.row_at, bf16[16,176,128]{2,1,0:T(8,128)(2,1)S(1)} %all-to-all-done.1.got, bf16[2,16,96,128]{3,2,1,0:T(8,128)(2,1)S(1)} %shard_map.115.mine, ...), custom_call_target="tpu_custom_call" | custom-call | tf_op jit(solution)/shard_map/pallas_call | solution.py:502
  49.3 0.3 collective-permute-done.2.got_other
  49.6 1.4 %shard_map.117 = (bf16[16,48,128]{2,1,0:T(8,128)(2,1)S(1)}, bf16[16,512]{1,0:T(8,128)(2,1)S(1)}, bf16[16,128]{1,0:T(8,128)(2,1)S(1)}, f32[16,16]{1,0:T(8,128)S(1)}) custom-call(s32[1]{0:T(128)} %bitcast.band_at, s32[1]{0:T(128)} %bitcast.1.row_at, bf16[16,176,128]{2,1,0:T(8,128)(2,1)S(1)} %collective-permute-done.2.got_other, ...), custom_call_target="tpu_custom_call" | custom-call | tf_op jit(solution)/shard_map/pallas_call | solution.py:502
  51.0 10.4 %all_to_all.15.got = bf16[16,48,128]{2,1,0:T(8,128)(2,1)S(1)} all-to-all(bf16[16,48,128]{2,1,0:T(8,128)(2,1)S(1)} %get-tuple-element.26), channel_id=1, replica_groups={{10,11,12,13,14,15,0,1,2,3,4,5,6,7,8,9},{26,27,28,29,30,31,16,17,18,19,..., dimensions={0} | all-to-all | bytes 393216 | tf_op jit(solution)/shard_map/all_to_all | solution.py:32
  61.4 0.8 %shard_map.118 = (bf16[16,2048]{1,0:T(8,128)(2,1)}, bf16[16,512]{1,0:T(8,128)(2,1)}, bf16[16,128]{1,0:T(8,128)(2,1)}, bf16[16,32]{1,0:T(8,128)(2,1)}) custom-call(s32[1]{0:T(128)} %bitcast.band_at, bf16[16,48,128]{2,1,0:T(8,128)(2,1)S(1)} %all_to_all.15.got, bf16[16,512]{1,0:T(8,128)(2,1)S(1)} %get-tuple-element.27.own_sixteen, ...), custom_call_target="tpu_custom_call" | custom-call | tf_op jit(solution)/shard_map/pallas_call | solution.py:502
  (1 shorter events, 0.0 us)
Async XLA Ops:
  2.8 24.9 %all-to-all-start = ((bf16[16,224,128]{2,1,0:T(8,128)(2,1)}), bf16[16,224,128]{2,1,0:T(8,128)(2,1)S(1)}, u32[]{:S(2)}, u32[]{:S(2)}) async-start(bf16[16,224,128]{2,1,0:T(8,128)(2,1)} %get-tuple-element.17), calls=%async_computation | async-start | bytes 1835008 | tf_op jit(solution)/shard_map/all_to_all | solution.py:32
  11.9 14.3 %collective-permute-start = (bf16[176,512]{1,0:T(8,128)(2,1)S(1)}, bf16[176,512]{1,0:T(8,128)(2,1)S(1)}, u32[]{:S(2)}, u32[]{:S(2)}) collective-permute-start(bf16[176,512]{1,0:T(8,128)(2,1)S(1)} %get-tuple-element.19), channel_id=1, source_target_pairs={{0,1},{1,0},{2,3},{3,2},{4,5},{5,4},{6,7},{7,6},{8,9},{9,8},{10,11... | collective-permute-start | bytes 540680 | tf_op jit(solution)/shard_map/ppermute | solution.py:573
  26.2 1.4 %collective-permute-start.1 = (bf16[176,512]{1,0:T(8,128)(2,1)S(1)}, bf16[176,512]{1,0:T(8,128)(2,1)S(1)}, u32[]{:S(2)}, u32[]{:S(2)}) collective-permute-start(bf16[176,512]{1,0:T(8,128)(2,1)S(1)} %collective-permute-done.mine), channel_id=1, source_target_pairs={{0,16},{16,0},{1,17},{17,1},{2,18},{18,2},{3,19},{19,3},{4,20},{20... | collective-permute-start | bytes 540680 | tf_op jit(solution)/shard_map/ppermute | solution.py:549
  29.6 17.8 %all-to-all-start.1 = ((bf16[16,176,128]{2,1,0:T(8,128)(2,1)}), bf16[16,176,128]{2,1,0:T(8,128)(2,1)S(1)}, u32[]{:S(2)}, u32[]{:S(2)}) async-start(bf16[16,176,128]{2,1,0:T(8,128)(2,1)} %shard_map.113), calls=%async_computation.1 | async-start | bytes 1441792 | tf_op jit(solution)/shard_map/all_to_all | solution.py:32
  33.4 7.0 %collective-permute-start.3 = (bf16[8,96,128]{2,1,0:T(8,128)(2,1)S(1)}, bf16[8,96,128]{2,1,0:T(8,128)(2,1)S(1)}, u32[]{:S(2)}, u32[]{:S(2)}) collective-permute-start(bf16[8,96,128]{2,1,0:T(8,128)(2,1)S(1)} %get-tuple-element.21), channel_id=1, source_target_pairs={{224,0},{0,32},{32,64},{64,96},{96,128},{128,160},{160,192},{192,2... | collective-permute-start | bytes 589832 | tf_op jit(solution)/shard_map/ppermute | solution.py:546
  35.4 8.1 %collective-permute-start.4 = (bf16[8,96,128]{2,1,0:T(8,128)(2,1)S(1)}, bf16[8,96,128]{2,1,0:T(8,128)(2,1)S(1)}, u32[]{:S(2)}, u32[]{:S(2)}) collective-permute-start(bf16[8,96,128]{2,1,0:T(8,128)(2,1)S(1)} %get-tuple-element.22), channel_id=1, source_target_pairs={{32,0},{64,32},{96,64},{128,96},{160,128},{192,160},{224,192},{0,2... | collective-permute-start | bytes 589832 | tf_op jit(solution)/shard_map/ppermute | solution.py:546
  43.4 4.0 %copy-start = (bf16[3,16,9,256]{3,1,2,0:T(8,128)(2,1)S(1)}, bf16[3,16,9,256]{3,1,2,0:T(8,128)(2,1)}, u32[]{:S(2)}) copy-start(bf16[3,16,9,256]{3,1,2,0:T(8,128)(2,1)} %param.13) | copy-start | bytes 663556
  43.4 4.0 %copy-start.1 = (f32[6,256]{1,0:T(8,128)S(1)}, f32[6,256]{1,0:T(8,128)}, u32[]{:S(2)}) copy-start(f32[6,256]{1,0:T(8,128)} %gain.3) | copy-start | bytes 18436
  43.4 4.0 %copy-start.2 = (f32[6,256]{1,0:T(8,128)S(1)}, f32[6,256]{1,0:T(8,128)}, u32[]{:S(2)}) copy-start(f32[6,256]{1,0:T(8,128)} %shift.3) | copy-start | bytes 18436
  43.5 4.0 %collective-permute-start.5 = (bf16[2,16,96,128]{3,2,1,0:T(8,128)(2,1)S(1)}, bf16[2,16,96,128]{3,2,1,0:T(8,128)(2,1)S(1)}, u32[]{:S(2)}, u32[]{:S(2)}) collective-permute-start(bf16[2,16,96,128]{3,2,1,0:T(8,128)(2,1)S(1)} %shard_map.115.mine), channel_id=1, source_target_pairs={{0,16},{16,0},{1,17},{17,1},{2,18},{18,2},{3,19},{19,3},{4,20},{20... | collective-permute-start | bytes 2359304 | tf_op jit(solution)/shard_map/ppermute | solution.py:549
  47.4 2.2 %collective-permute-start.2 = (bf16[16,176,128]{2,1,0:T(8,128)(2,1)S(1)}, bf16[16,176,128]{2,1,0:T(8,128)(2,1)S(1)}, u32[]{:S(2)}, u32[]{:S(2)}) collective-permute-start(bf16[16,176,128]{2,1,0:T(8,128)(2,1)S(1)} %all-to-all-done.1.got), channel_id=1, source_target_pairs={{0,16},{16,0},{1,17},{17,1},{2,18},{18,2},{3,19},{19,3},{4,20},{20... | collective-permute-start | bytes 2162696 | tf_op jit(solution)/shard_map/ppermute | solution.py:549

commit v8 on v6

--- a/solution.py
+++ b/solution.py
@@ -267,11 +267,11 @@
 
 def paired(blocks):
     members, rows, _ = blocks.shape
-    blocks = blocks.reshape(members // 2, 2, rows, LANES).astype(F32)
+    blocks = blocks.reshape(members // 2, 2, rows, LANES)
     sides = [blocks[:, h].reshape(-1, LANES) for h in range(2)]
-    low = iota(sides[0].shape, 1) < LANES // 2
-    near = jnp.where(low, sides[0], pltpu.roll(sides[1], LANES // 2, 1))
-    far = jnp.where(low, pltpu.roll(sides[0], LANES // 2, 1), sides[1])
+    middle = LANES // 2
+    near = jnp.concatenate([side[:, :middle] for side in sides], axis=1)
+    far = jnp.concatenate([side[:, middle:] for side in sides], axis=1)
     both = [side.reshape(members // 2, 1, rows, LANES) for side in (near, far)]
     return jnp.concatenate(both, axis=1).reshape(members * rows, LANES)
 

time: 62.8 us -> 62.8 us (level)
  no operation moved by 1% of the time
where the time goes in v8:
time: 62.8 us; the launch traced here: 62 us
  waiting for transfers between devices  27.8 us (44%)
  starting transfers between devices  14.9 us (24%)
  blocking collectives  10.4 us (17%)
  Pallas kernels  8.09 us (13%)
  between operations  0.73 us (1%)
    ppermute x1, waiting for transfers between devices, per_device(): lax.ppermute(pair_half, MP, [(m, m ^ 1) for m in range(members)])  14.3 us
    all_to_all x2, starting transfers between devices, exchanged(): lax.all_to_all(blocks, MP, 0, 0, tiled=True, axis_index_groups=[list(orde...  12.7 us
    all_to_all x1, blocking collectives, exchanged(): lax.all_to_all(blocks, MP, 0, 0, tiled=True, axis_index_groups=[list(orde...  10.4 us
    pallas_call x8, Pallas kernels, call(): pl.pallas_call(kernel, in_specs=specs, out_specs=jax.tree.map(lambda _: p...  8.09 us
    ppermute x2, waiting for transfers between devices, from_plane(): lax.ppermute(value, 'dp', [((i + step) % planes, i) for i in range(planes)])  7.94 us
    all_to_all x2, waiting for transfers between devices, exchanged(): lax.all_to_all(blocks, MP, 0, 0, tiled=True, axis_index_groups=[list(orde...  3.87 us
    ppermute x2, starting transfers between devices, from_plane(): lax.ppermute(value, 'dp', [((i + step) % planes, i) for i in range(planes)])  2.1 us
    ppermute x3, waiting for transfers between devices, from_core(): return lax.ppermute(value, 'space', [(0, 1), (1, 0)])  1.74 us
  transfers between devices with their start and end apart: 8, of which 6 were waited for; matrix products, arithmetic and copies ran while one was open for 0% of the time, Pallas kernels for 3%

profile of v8, /device:TPU:64, one launch (start us, length us, event | category | flops | bytes accessed | tf_op | source)
XLA Modules:
  0.0 62.0 jit_solution(8224522466403032134)
XLA Ops:
  0.6 2.1 %shard_map.111 = (bf16[16,224,128]{2,1,0:T(8,128)(2,1)}, bf16[176,1024]{1,0:T(8,128)(2,1)S(1)}, bf16[176,512]{1,0:T(8,128)(2,1)S(1)}) custom-call(s32[1]{0:T(128)} %bitcast.band_at, s32[1]{0:T(128)} %bitcast.2.parity_at, bf16[8,64,64]{2,1,0:T(8,128)(2,1)} %x_from.1, bf16[3,9,16,256]{3,2,1,0:T(8,128)(2,1)} %bitcast.7, bf16[16,512]{1,0:T(8,128)(2,1)} %lat_from.1, ...), custom_call_target="tpu_custom_call" | custom-call | tf_op jit(solution)/shard_map/pallas_call | solution.py:491
  2.7 9.1 %all-to-all-start = ((bf16[16,224,128]{2,1,0:T(8,128)(2,1)}), bf16[16,224,128]{2,1,0:T(8,128)(2,1)S(1)}, u32[]{:S(2)}, u32[]{:S(2)}) async-start(bf16[16,224,128]{2,1,0:T(8,128)(2,1)} %get-tuple-element.17), calls=%async_computation | async-start | bytes 1835008 | tf_op jit(solution)/shard_map/all_to_all | solution.py:32
  11.9 0.0 collective-permute-start
  11.9 14.3 %collective-permute-done.mine = bf16[176,512]{1,0:T(8,128)(2,1)S(1)} collective-permute-done((bf16[176,512]{1,0:T(8,128)(2,1)S(1)}, bf16[176,512]{1,0:T(8,128)(2,1)S(1)}, u32[]{:S(2)}, u32[]{:S(2)}) %collective-permute-start) | collective-permute-done | bytes 180256 | tf_op jit(solution)/shard_map/ppermute | solution.py:553
  26.2 0.0 collective-permute-start.1
  26.2 1.4 %collective-permute-done.1.theirs = bf16[176,512]{1,0:T(8,128)(2,1)S(1)} collective-permute-done((bf16[176,512]{1,0:T(8,128)(2,1)S(1)}, bf16[176,512]{1,0:T(8,128)(2,1)S(1)}, u32[]{:S(2)}, u32[]{:S(2)}) %collective-permute-start.1) | collective-permute-done | bytes 180256 | tf_op jit(solution)/shard_map/ppermute | solution.py:532
  27.6 0.0 all-to-all-done.gathered
  27.6 1.8 %shard_map.113 = bf16[16,176,128]{2,1,0:T(8,128)(2,1)} custom-call(s32[1]{0:T(128)} %bitcast.band_at, s32[1]{0:T(128)} %bitcast.1.row_at, bf16[16,224,128]{2,1,0:T(8,128)(2,1)S(1)} %all-to-all-done.gathered, bf16[176,1024]{1,0:T(8,128)(2,1)S(1)} %get-tuple-element.18.own, bf16[176,1024]{1,0:T(8,128)(2,1)S(1)} %shard_map.112.other), custom_call_target="tpu_custom_call" | custom-call | tf_op jit(solution)/shard_map/pallas_call | solution.py:491
  29.5 3.6 %all-to-all-start.1 = ((bf16[16,176,128]{2,1,0:T(8,128)(2,1)}), bf16[16,176,128]{2,1,0:T(8,128)(2,1)S(1)}, u32[]{:S(2)}, u32[]{:S(2)}) async-start(bf16[16,176,128]{2,1,0:T(8,128)(2,1)} %shard_map.113), calls=%async_computation.1 | async-start | bytes 1441792 | tf_op jit(solution)/shard_map/all_to_all | solution.py:32
  33.1 0.1 shard_map.114
  33.2 2.0 %collective-permute-start.3 = (bf16[8,96,128]{2,1,0:T(8,128)(2,1)S(1)}, bf16[8,96,128]{2,1,0:T(8,128)(2,1)S(1)}, u32[]{:S(2)}, u32[]{:S(2)}) collective-permute-start(bf16[8,96,128]{2,1,0:T(8,128)(2,1)S(1)} %get-tuple-element.21), channel_id=1, source_target_pairs={{224,0},{0,32},{32,64},{64,96},{96,128},{128,160},{160,192},{192,2... | collective-permute-start | bytes 589832 | tf_op jit(solution)/shard_map/ppermute | solution.py:529
  35.2 0.1 collective-permute-start.4
  35.3 4.9 %collective-permute-done.3.low = bf16[8,96,128]{2,1,0:T(8,128)(2,1)S(1)} collective-permute-done((bf16[8,96,128]{2,1,0:T(8,128)(2,1)S(1)}, bf16[8,96,128]{2,1,0:T(8,128)(2,1)S(1)}, u32[]{:S(2)}, u32[]{:S(2)}) %collective-permute-start.3) | collective-permute-done | bytes 196640 | tf_op jit(solution)/shard_map/ppermute | solution.py:529
  40.2 3.0 %collective-permute-done.4.high = bf16[8,96,128]{2,1,0:T(8,128)(2,1)S(1)} collective-permute-done((bf16[8,96,128]{2,1,0:T(8,128)(2,1)S(1)}, bf16[8,96,128]{2,1,0:T(8,128)(2,1)S(1)}, u32[]{:S(2)}, u32[]{:S(2)}) %collective-permute-start.4) | collective-permute-done | bytes 196640 | tf_op jit(solution)/shard_map/ppermute | solution.py:529
  43.2 0.0 copy-start
  43.2 0.0 copy-start.1
  43.2 0.0 copy-start.2
  43.2 0.1 shard_map.115.mine
  43.3 0.1 collective-permute-start.5
  43.4 3.9 %all-to-all-done.1.got = bf16[16,176,128]{2,1,0:T(8,128)(2,1)S(1)} async-done(((bf16[16,176,128]{2,1,0:T(8,128)(2,1)}), bf16[16,176,128]{2,1,0:T(8,128)(2,1)S(1)}, u32[]{:S(2)}, u32[]{:S(2)}) %all-to-all-start.1) | async-done | bytes 720928 | tf_op jit(solution)/shard_map/all_to_all | solution.py:32
  47.3 0.0 collective-permute-start.2
  47.3 0.0 collective-permute-done.5.theirs
  47.3 0.0 copy-done
  47.3 0.0 copy-done.1
  47.3 0.0 copy-done.2
  47.3 1.8 %shard_map.116 = (f32[256,128]{1,0:T(8,128)S(1)}, f32[16,512]{1,0:T(8,128)S(1)}, f32[16,128]{1,0:T(8,128)S(1)}) custom-call(s32[1]{0:T(128)} %bitcast.band_at, s32[1]{0:T(128)} %bitcast.1.row_at, bf16[16,176,128]{2,1,0:T(8,128)(2,1)S(1)} %all-to-all-done.1.got, bf16[2,16,96,128]{3,2,1,0:T(8,128)(2,1)S(1)} %shard_map.115.mine, ...), custom_call_target="tpu_custom_call" | custom-call | tf_op jit(solution)/shard_map/pallas_call | solution.py:491
  49.1 0.3 collective-permute-done.2.got_other
  49.4 1.4 %shard_map.117 = (bf16[16,48,128]{2,1,0:T(8,128)(2,1)S(1)}, bf16[16,512]{1,0:T(8,128)(2,1)S(1)}, bf16[16,128]{1,0:T(8,128)(2,1)S(1)}, f32[16,16]{1,0:T(8,128)S(1)}) custom-call(s32[1]{0:T(128)} %bitcast.band_at, s32[1]{0:T(128)} %bitcast.1.row_at, bf16[16,176,128]{2,1,0:T(8,128)(2,1)S(1)} %collective-permute-done.2.got_other, ...), custom_call_target="tpu_custom_call" | custom-call | tf_op jit(solution)/shard_map/pallas_call | solution.py:491
  50.8 10.4 %all_to_all.15.got = bf16[16,48,128]{2,1,0:T(8,128)(2,1)S(1)} all-to-all(bf16[16,48,128]{2,1,0:T(8,128)(2,1)S(1)} %get-tuple-element.26), channel_id=1, replica_groups={{10,11,12,13,14,15,0,1,2,3,4,5,6,7,8,9},{26,27,28,29,30,31,16,17,18,19,..., dimensions={0} | all-to-all | bytes 393216 | tf_op jit(solution)/shard_map/all_to_all | solution.py:32
  61.2 0.8 %shard_map.118 = (bf16[16,2048]{1,0:T(8,128)(2,1)}, bf16[16,512]{1,0:T(8,128)(2,1)}, bf16[16,128]{1,0:T(8,128)(2,1)}, bf16[16,32]{1,0:T(8,128)(2,1)}) custom-call(s32[1]{0:T(128)} %bitcast.band_at, bf16[16,48,128]{2,1,0:T(8,128)(2,1)S(1)} %all_to_all.15.got, bf16[16,512]{1,0:T(8,128)(2,1)S(1)} %get-tuple-element.27.own_sixteen, ...), custom_call_target="tpu_custom_call" | custom-call | tf_op jit(solution)/shard_map/pallas_call | solution.py:491
  (1 shorter events, 0.0 us)
Async XLA Ops:
  2.7 24.9 %all-to-all-start = ((bf16[16,224,128]{2,1,0:T(8,128)(2,1)}), bf16[16,224,128]{2,1,0:T(8,128)(2,1)S(1)}, u32[]{:S(2)}, u32[]{:S(2)}) async-start(bf16[16,224,128]{2,1,0:T(8,128)(2,1)} %get-tuple-element.17), calls=%async_computation | async-start | bytes 1835008 | tf_op jit(solution)/shard_map/all_to_all | solution.py:32
  11.9 14.3 %collective-permute-start = (bf16[176,512]{1,0:T(8,128)(2,1)S(1)}, bf16[176,512]{1,0:T(8,128)(2,1)S(1)}, u32[]{:S(2)}, u32[]{:S(2)}) collective-permute-start(bf16[176,512]{1,0:T(8,128)(2,1)S(1)} %get-tuple-element.19), channel_id=1, source_target_pairs={{0,1},{1,0},{2,3},{3,2},{4,5},{5,4},{6,7},{7,6},{8,9},{9,8},{10,11... | collective-permute-start | bytes 540680 | tf_op jit(solution)/shard_map/ppermute | solution.py:553
  26.2 1.4 %collective-permute-start.1 = (bf16[176,512]{1,0:T(8,128)(2,1)S(1)}, bf16[176,512]{1,0:T(8,128)(2,1)S(1)}, u32[]{:S(2)}, u32[]{:S(2)}) collective-permute-start(bf16[176,512]{1,0:T(8,128)(2,1)S(1)} %collective-permute-done.mine), channel_id=1, source_target_pairs={{0,16},{16,0},{1,17},{17,1},{2,18},{18,2},{3,19},{19,3},{4,20},{20... | collective-permute-start | bytes 540680 | tf_op jit(solution)/shard_map/ppermute | solution.py:532
  29.5 17.8 %all-to-all-start.1 = ((bf16[16,176,128]{2,1,0:T(8,128)(2,1)}), bf16[16,176,128]{2,1,0:T(8,128)(2,1)S(1)}, u32[]{:S(2)}, u32[]{:S(2)}) async-start(bf16[16,176,128]{2,1,0:T(8,128)(2,1)} %shard_map.113), calls=%async_computation.1 | async-start | bytes 1441792 | tf_op jit(solution)/shard_map/all_to_all | solution.py:32
  33.2 7.0 %collective-permute-start.3 = (bf16[8,96,128]{2,1,0:T(8,128)(2,1)S(1)}, bf16[8,96,128]{2,1,0:T(8,128)(2,1)S(1)}, u32[]{:S(2)}, u32[]{:S(2)}) collective-permute-start(bf16[8,96,128]{2,1,0:T(8,128)(2,1)S(1)} %get-tuple-element.21), channel_id=1, source_target_pairs={{224,0},{0,32},{32,64},{64,96},{96,128},{128,160},{160,192},{192,2... | collective-permute-start | bytes 589832 | tf_op jit(solution)/shard_map/ppermute | solution.py:529
  35.2 8.1 %collective-permute-start.4 = (bf16[8,96,128]{2,1,0:T(8,128)(2,1)S(1)}, bf16[8,96,128]{2,1,0:T(8,128)(2,1)S(1)}, u32[]{:S(2)}, u32[]{:S(2)}) collective-permute-start(bf16[8,96,128]{2,1,0:T(8,128)(2,1)S(1)} %get-tuple-element.22), channel_id=1, source_target_pairs={{32,0},{64,32},{96,64},{128,96},{160,128},{192,160},{224,192},{0,2... | collective-permute-start | bytes 589832 | tf_op jit(solution)/shard_map/ppermute | solution.py:529
  43.2 4.0 %copy-start = (bf16[3,16,9,256]{3,1,2,0:T(8,128)(2,1)S(1)}, bf16[3,16,9,256]{3,1,2,0:T(8,128)(2,1)}, u32[]{:S(2)}) copy-start(bf16[3,16,9,256]{3,1,2,0:T(8,128)(2,1)} %param.13) | copy-start | bytes 663556
  43.2 4.0 %copy-start.1 = (f32[6,256]{1,0:T(8,128)S(1)}, f32[6,256]{1,0:T(8,128)}, u32[]{:S(2)}) copy-start(f32[6,256]{1,0:T(8,128)} %gain.3) | copy-start | bytes 18436
  43.2 4.0 %copy-start.2 = (f32[6,256]{1,0:T(8,128)S(1)}, f32[6,256]{1,0:T(8,128)}, u32[]{:S(2)}) copy-start(f32[6,256]{1,0:T(8,128)} %shift.3) | copy-start | bytes 18436
  43.3 4.0 %collective-permute-start.5 = (bf16[2,16,96,128]{3,2,1,0:T(8,128)(2,1)S(1)}, bf16[2,16,96,128]{3,2,1,0:T(8,128)(2,1)S(1)}, u32[]{:S(2)}, u32[]{:S(2)}) collective-permute-start(bf16[2,16,96,128]{3,2,1,0:T(8,128)(2,1)S(1)} %shard_map.115.mine), channel_id=1, source_target_pairs={{0,16},{16,0},{1,17},{17,1},{2,18},{18,2},{3,19},{19,3},{4,20},{20... | collective-permute-start | bytes 2359304 | tf_op jit(solution)/shard_map/ppermute | solution.py:532
  47.3 2.2 %collective-permute-start.2 = (bf16[16,176,128]{2,1,0:T(8,128)(2,1)S(1)}, bf16[16,176,128]{2,1,0:T(8,128)(2,1)S(1)}, u32[]{:S(2)}, u32[]{:S(2)}) collective-permute-start(bf16[16,176,128]{2,1,0:T(8,128)(2,1)S(1)} %all-to-all-done.1.got), channel_id=1, source_target_pairs={{0,16},{16,0},{1,17},{17,1},{2,18},{18,2},{3,19},{19,3},{4,20},{20... | collective-permute-start | bytes 2162696 | tf_op jit(solution)/shard_map/ppermute | solution.py:532
